TPU v7x, 256 devices: a 8x8x2 block of a 8x8x16 slice. The times are simulated.
256 devices in a mesh: rep: 2 (over z), blk: 128 (over x, y, core).
Axes of the slice: x: 8, y: 8, z: 2, core: 2. Of those that a mesh axis runs over, the one named last changes fastest.
The devices are a block of a 8x8x16 slice.
Arguments:
- hidden: bfloat16 [32, 4096], P('rep', 'blk'), parts along dimension 0, may hold values from -4 to 4
- queries: bfloat16 [32, 4096], P('rep'), parts along dimension 0, may hold values from -180 to 180
- cache_kv: bfloat16 [2, 32, 4096, 1024], P(None, 'rep', 'blk'), parts along dimension 1, may hold values from -6 to 6
- cache_len: int32 [32], P('rep'), parts along dimension 0, may hold values from 1 to 4096
- inserted_key_value: bfloat16 [2, 16, 4096, 1024], P(None, 'rep', 'blk'), parts along dimension 1, may hold values from -6 to 6
- insert_slot: int32 [16], P('rep'), parts along dimension 0, may hold values from 0 to 15, as said below
- prefix_len: int32 [16], P('rep'), parts along dimension 0, may hold values from 1 to 4096, as said below
- out_weight: bfloat16 [4096, 4096], P(None, 'blk'), may hold values from -0.09375 to 0.09375
- norm_gain: bfloat16 [4096], replicated, may hold values from 0.25 to 1.75
- router_weight: bfloat16 [4096, 4], replicated, may hold values from -0.09375 to 0.09375
- expert_ids: int32 [32, 2], P('rep'), parts along dimension 0, may hold values from 0 to 3, all different within a row
- gate_up: bfloat16 [2, 4096, 28672], P(None, None, 'blk'), may hold values from -0.09375 to 0.09375
- down_proj: bfloat16 [28672, 4096], P('blk'), may hold values from -0.0625 to 0.0625
Outputs:
- layer_out: bfloat16 [32, 4096], P('rep', 'blk'), parts along dimension 0
There are 2 independent parts, one for each index of `rep`. A program takes and returns all parts, laid end to end along the dimension named above; an argument that names none is the same for every part. Nothing has to cross between parts.
Inputs may be any that keep to these rules, and one draw needn't show every extreme that they name: `insert_slot`: 8 different slot numbers. `prefix_len`: some inserted request has all 4096 positions.
All inputs are finite; a program needn't handle non-finite values.
Results may differ from a plain program's by a relative error of at most 0.012.
Values may be sent and summed in bfloat16 or wider, within the bound.
No kernel may reach another device: no remote copies, remote signals or barrier semaphores. Data moves between devices by JAX's collectives and lax.ppermute only.
A program may use at most 128 MiB of HBM per device.

v0:
```python
import math

import jax
import jax.numpy as jnp
from jax import lax
from jax.sharding import Mesh
from jax.sharding import PartitionSpec as P

QUERY_HEADS = 32
KEY_VALUE_HEADS = 8
HEAD_SIZE = 128
EXPERTS = 4
FF = 7168
BLK = ("blk_0", "blk_1", "blk_2")


def shifted(shard, axis, by):
    count = lax.axis_size(axis)
    return lax.ppermute(shard, axis, [(i, (i + by) % count) for i in range(count)])


def all_in_one(shard, axis):
    leaves = jax.tree.leaves(shard)
    order = sorted(range(len(leaves)), key=lambda k: -leaves[k].size)
    width = (1, *leaves[order[0]].shape)[-1]
    lines = [
        jnp.pad(leaves[k].reshape(-1), (0, -leaves[k].size % width)).reshape(-1, width)
        for k in order
    ]
    both, at, found = (lax.all_gather(jnp.concatenate(lines), axis), 0, {})
    for k, line in zip(order, lines):
        piece = both[:, at : at + len(line)].reshape(len(both), -1)
        found[k] = piece[:, : leaves[k].size].reshape(-1, *leaves[k].shape)
        at += len(line)
    numbers = iter(range(len(leaves)))
    return jax.tree.map(lambda _: found[next(numbers)], shard)


def combined_by_axis(shard, axes, combine):
    for axis in axes:
        pieces = all_in_one(shard, axis)
        shard = jax.tree.map(lambda part: part[0], pieces)
        for k in range(1, lax.axis_size(axis)):
            shard = combine(shard, jax.tree.map(lambda part: part[k], pieces))
    return shard


def sum_in_order(tiles, axes, order):
    inside = tiles.shape[1:]
    tiles = tiles.reshape(*(lax.axis_size(a) for a in axes), *inside)
    tiles = jnp.moveaxis(tiles, order, range(len(axes))).reshape(-1, *inside)
    for k in order:
        tiles = lax.psum_scatter(tiles, axes[k], scatter_dimension=0, tiled=True)
    return tiles[0]


def split_up(shard, dim, count):
    before, after = (shard.shape[:dim], shard.shape[dim + 1 :])
    return jnp.moveaxis(shard.reshape(*before, count, -1, *after), dim, 0)


def summed_rows(shard, axes, order, dim):
    count = lax.axis_size(axes)
    return sum_in_order(split_up(shard, dim, count), axes, order)


def block_attention(queries, key_rows, value_rows, valid):
    slot_list = queries.shape[0]
    query_groups = QUERY_HEADS // KEY_VALUE_HEADS
    heads_of_queries = queries.astype(jnp.float32).reshape(
        slot_list, KEY_VALUE_HEADS, query_groups, HEAD_SIZE
    )
    heads_of_keys = key_rows.astype(jnp.float32).reshape(slot_list, -1, KEY_VALUE_HEADS, HEAD_SIZE)
    heads_of_values = value_rows.astype(jnp.float32).reshape(
        slot_list, -1, KEY_VALUE_HEADS, HEAD_SIZE
    )
    scores = jnp.einsum("skgd,sckd->skgc", heads_of_queries, heads_of_keys) / math.sqrt(HEAD_SIZE)
    masked = valid[:, None, None, :]
    peak = jnp.max(jnp.where(masked, scores, -1e30), axis=-1)
    weights = jnp.where(masked, jnp.exp(scores - peak[..., None]), 0.0)
    totals = jnp.sum(weights, axis=-1)
    partial_value = jnp.einsum("skgc,sckd->skgd", weights, heads_of_values)
    return (
        partial_value.reshape(slot_list, QUERY_HEADS, HEAD_SIZE),
        peak.reshape(slot_list, QUERY_HEADS),
        totals.reshape(slot_list, QUERY_HEADS),
    )


def merge_pair(earlier, later):
    early_out, early_peak, early_total = earlier
    late_out, late_peak, late_total = later
    highest = jnp.maximum(early_peak, late_peak)
    early_scale = jnp.exp(early_peak - highest)
    late_scale = jnp.exp(late_peak - highest)
    merged_out = early_out * early_scale[..., None] + late_out * late_scale[..., None]
    return (merged_out, highest, early_total * early_scale + late_total * late_scale)


def route_shares(normed, router_weight, expert_ids):
    logits = jnp.dot(normed, router_weight, preferred_element_type=jnp.float32)
    chosen = (expert_ids[:, :, None] == jnp.arange(EXPERTS, dtype=jnp.int32)[None, None, :]).astype(
        jnp.float32
    )
    picked = jnp.sum(chosen * logits[:, None, :], axis=-1)
    gates = jax.nn.sigmoid(picked - picked[:, ::-1])
    return jnp.sum(gates[:, :, None] * chosen, axis=1)


def on_device(
    hidden,
    queries,
    cache_kv,
    cache_len,
    inserted_key_value,
    insert_slot,
    prefix_len,
    out_weight,
    norm_gain,
    router_weight,
    expert_ids,
    gate_up,
    down_proj,
):
    cycle_size = lax.axis_size(BLK)
    dev_index = lax.axis_index(BLK)
    half_cycle = cycle_size // 2
    ctx_rows = cache_kv.shape[2]
    arrived = shifted(inserted_key_value, BLK, half_cycle)
    cache = cache_kv.at[:, insert_slot].set(arrived)
    slot_lengths = cache_len.at[insert_slot].set(prefix_len)
    positions = dev_index * ctx_rows + jnp.arange(ctx_rows, dtype=jnp.int32)
    valid = positions[None, :] < slot_lengths[:, None]
    partial_value, peak, totals = block_attention(queries, cache[0], cache[1], valid)
    slot_list = queries.shape[0]
    summed, highest, all_totals = combined_by_axis((partial_value, peak, totals), BLK, merge_pair)
    attn = (
        (summed / all_totals[..., None])
        .reshape(slot_list, QUERY_HEADS * HEAD_SIZE)
        .astype(jnp.bfloat16)
    )
    local_mixed = (
        hidden.astype(jnp.float32) + jnp.dot(attn, out_weight, preferred_element_type=jnp.float32)
    ).astype(jnp.bfloat16)
    mixed = lax.all_gather(local_mixed, BLK, axis=1, tiled=True)
    mixed_f = mixed.astype(jnp.float32)
    scale = lax.rsqrt(jnp.mean(mixed_f * mixed_f, axis=-1, keepdims=True) + 1e-05)
    normed = (mixed_f * scale * norm_gain.astype(jnp.float32)).astype(jnp.bfloat16)
    shares = route_shares(normed, router_weight, expert_ids)
    unit_count = gate_up.shape[2]
    expert_now = dev_index * unit_count // FF
    picker = (jnp.arange(EXPERTS, dtype=jnp.int32) == expert_now).astype(jnp.float32)
    expert_share = jnp.sum(shares * picker[None, :], axis=1)
    act = (
        jax.nn.silu(jnp.dot(normed, gate_up[0], preferred_element_type=jnp.float32))
        * jnp.dot(normed, gate_up[1], preferred_element_type=jnp.float32)
    ).astype(jnp.bfloat16)
    term = expert_share[:, None] * jnp.dot(act, down_proj, preferred_element_type=jnp.float32)
    moe = summed_rows(term, BLK, (2, 0, 1), 1)
    return (local_mixed.astype(jnp.float32) + moe).astype(jnp.bfloat16)


def solution(mesh):
    split = Mesh(
        mesh.devices.reshape(mesh.shape["rep"], 8, 8, 2), ("rep", "blk_0", "blk_1", "blk_2")
    )
    return jax.shard_map(
        on_device,
        mesh=split,
        in_specs=(
            P("rep", BLK),
            P("rep", None),
            P(None, "rep", BLK, None),
            P("rep"),
            P(None, "rep", BLK, None),
            P("rep"),
            P("rep"),
            P(None, BLK),
            P(),
            P(),
            P("rep", None),
            P(None, None, BLK),
            P(BLK, None),
        ),
        out_specs=P("rep", BLK),
        check_vma=False,
    )
```

profile of v0, /device:TPU:513, one launch (start us, length us, event | category | flops | bytes accessed | tf_op | source)
XLA Modules:
  0.0 348.5 jit_solution(5497632940912069190)
XLA Ops:
  6.6 3.3 copy.67
  9.9 6.6 %collective-permute-start = (bf16[2,8,32,1024]{3,2,1,0:T(8,128)(2,1)}, bf16[2,8,32,1024]{3,2,1,0:T(8,128)(2,1)S(1)}, u32[]{:S(2)}, u32[]{:S(2)}) collective-permute-start(bf16[2,8,32,1024]{3,2,1,0:T(8,128)(2,1)} %param.17), channel_id=1, source_target_pairs={{0,64},{1,65},{2,66},{3,67},{4,68},{5,69},{6,70},{7,71},{8,72},{9,... | collective-permute-start | bytes 3145736 | tf_op jit(solution)/shard_map/ppermute | solution.py:19
  17.3 26.3 %collective-permute-done = bf16[2,8,32,1024]{3,2,1,0:T(8,128)(2,1)S(1)} collective-permute-done((bf16[2,8,32,1024]{3,2,1,0:T(8,128)(2,1)}, bf16[2,8,32,1024]{3,2,1,0:T(8,128)(2,1)S(1)}, u32[]{:S(2)}, u32[]{:S(2)}) %collective-permute-start) | collective-permute-done | bytes 1048608 | tf_op jit(solution)/shard_map/ppermute | solution.py:19
  43.6 1.0 copy-done.2
  44.6 1.3 copy.39
  45.9 2.9 scatter_fusion.1
  48.8 1.7 fusion.176
  51.0 0.7 select_reduce_fusion
  52.9 0.7 pad_maximum_fusion
  53.7 74.6 %all-gather.7.cloned.1.call-done = f32[4160,128]{1,0:T(8,128)} async-done(((f32[520,128]{1,0:T(8,128)}), f32[4160,128]{1,0:T(8,128)}) %all-gather.7.cloned.1.call-update) | async-done | bytes 2129936 | tf_op jit(solution)/shard_map/all_gather | solution.py:30
  128.3 0.7 fusion.151
  129.0 0.8 fusion.102
  129.8 0.7 fusion.150
  130.5 0.7 fusion.148
  131.2 0.7 fusion.146
  131.9 2.5 fusion.42
  134.4 0.7 pad_maximum_fusion.1
  135.3 41.0 %all-gather.9.cloned.1.call-done = f32[4160,128]{1,0:T(8,128)} async-done(((f32[520,128]{1,0:T(8,128)}), f32[4160,128]{1,0:T(8,128)}) %all-gather.9.cloned.1.call-update) | async-done | bytes 2129936 | tf_op jit(solution)/shard_map/all_gather | solution.py:30
  177.0 0.8 fusion.81
  177.9 0.7 fusion.135
  178.6 0.7 fusion.133
  179.3 0.7 fusion.131
  180.0 2.5 fusion.21
  182.5 6.9 %all-gather.2 = f32[1040,128]{1,0:T(8,128)S(1)} all-gather(f32[520,128]{1,0:T(8,128)S(1)} %pad_maximum_fusion.2), channel_id=4, replica_groups=mesh['rep'=2,'blk_0'=8,'blk_1'=8,'blk_2'=2] {'blk_2'}, dimensions={0}, use_global_device_ids=true | all-gather | bytes 798720 | tf_op jit(solution)/shard_map/all_gather | solution.py:30
  191.0 51.0 %all-gather.3 = bf16[128,32,16]{1,2,0:T(8,128)(2,1)S(1)} all-gather(bf16[1,32,16]{1,2,0:T(8,128)(2,1)S(1)} %bitcast.762), channel_id=1, replica_groups=mesh['rep'=2,'blk_0'=8,'blk_1'=8,'blk_2'=2] {'blk_0','blk_1','blk_2'}, dimensions={0}, use_global_device_ids=true | all-gather | bytes 132096 | tf_op jit(solution)/shard_map/all_gather | solution.py:145
  243.5 2.1 fusion.2
  245.9 2.9 convolution_multiply_fusion
  249.8 1.1 copy.45
  251.0 14.2 %reduce-scatter.4.cloned.1.call-done = f32[64,16,32]{2,1,0:T(8,128)} async-done(((f32[128,16,32]{2,1,0:T(8,128)}), f32[64,16,32]{2,1,0:T(8,128)}) %reduce-scatter.4.cloned.1.call-update) | async-done | bytes 131088 | tf_op jit(solution)/shard_map/reduce_scatter | solution.py:53
  265.4 36.0 %reduce-scatter.6.cloned.1.call-done = f32[8,16,32]{2,1,0:T(8,128)} async-done(((f32[64,16,32]{2,1,0:T(8,128)}), f32[8,16,32]{2,1,0:T(8,128)}) %reduce-scatter.6.cloned.1.call-update) | async-done | bytes 16400 | tf_op jit(solution)/shard_map/reduce_scatter | solution.py:53
  301.4 39.3 %reduce-scatter.8.cloned.1.call-done = f32[1,16,32]{2,1,0:T(8,128)} async-done(((f32[8,16,32]{2,1,0:T(8,128)}), f32[1,16,32]{2,1,0:T(8,128)}) %reduce-scatter.8.cloned.1.call-update) | async-done | bytes 2064 | tf_op jit(solution)/shard_map/reduce_scatter | solution.py:53
  340.7 1.3 fusion.74
  (73 shorter events, 7.9 us)
Async XLA Ops:
  6.5 239.3 %copy-start = (bf16[224,4096]{1,0:T(8,128)(2,1)S(1)}, bf16[224,4096]{1,0:T(8,128)(2,1)}, u32[]{:S(2)}) copy-start(bf16[224,4096]{1,0:T(8,128)(2,1)} %param.25) | copy-start | bytes 5505028
  6.6 9.9 %copy-start.4 = (bf16[16,4096]{1,0:T(8,128)(2,1)S(1)}, bf16[16,4096]{1,0:T(8,128)(2,1)}, u32[]{:S(2)}) copy-start(bf16[16,4096]{1,0:T(8,128)(2,1)} %param.14) | copy-start | bytes 393220
  6.6 121.7 %all-gather.7.cloned.1.call-start = ((), (), s32[]{:S(2)}) async-start(), calls=%async_computation.6 | async-start | bytes 2396160 | tf_op jit(solution)/shard_map/all_gather | solution.py:30
  6.6 10.0 %copy-start.10 = (s32[8]{0:T(128)S(1)}, s32[8]{0:T(128)}, u32[]{:S(2)}) copy-start(s32[8]{0:T(128)} %param.18) | copy-start | bytes 100
  6.6 10.0 %copy-start.1 = (s32[16]{0:T(128)S(1)}, s32[16]{0:T(128)}, u32[]{:S(2)}) copy-start(s32[16]{0:T(128)} %param.16) | copy-start | bytes 196
  6.6 10.0 %copy-start.8 = (s32[8]{0:T(128)S(1)}, s32[8]{0:T(128)}, u32[]{:S(2)}) copy-start(s32[8]{0:T(128)} %param.19) | copy-start | bytes 100
  9.9 33.7 %collective-permute-start = (bf16[2,8,32,1024]{3,2,1,0:T(8,128)(2,1)}, bf16[2,8,32,1024]{3,2,1,0:T(8,128)(2,1)S(1)}, u32[]{:S(2)}, u32[]{:S(2)}) collective-permute-start(bf16[2,8,32,1024]{3,2,1,0:T(8,128)(2,1)} %param.17), channel_id=1, source_target_pairs={{0,64},{1,65},{2,66},{3,67},{4,68},{5,69},{6,70},{7,71},{8,72},{9,... | collective-permute-start | bytes 3145736 | tf_op jit(solution)/shard_map/ppermute | solution.py:19
  43.6 1.0 copy-start.2
  52.8 82.5 %copy-start.5 = (bf16[4096]{0:T(1024)(128)(2,1)S(1)}, bf16[4096]{0:T(1024)(128)(2,1)}, u32[]{:S(2)}) copy-start(bf16[4096]{0:T(1024)(128)(2,1)} %param.21) | copy-start | bytes 24580
  53.7 122.7 %all-gather.9.cloned.1.call-start = ((), (), s32[]{:S(2)}) async-start(), calls=%async_computation.7 | async-start | bytes 2396160 | tf_op jit(solution)/shard_map/all_gather | solution.py:30
  135.2 130.1 %reduce-scatter.4.cloned.1.call-start = ((), (), s32[]{:S(2)}) async-start(), calls=%async_computation.3 | async-start | bytes 1572864 | tf_op jit(solution)/shard_map/reduce_scatter | solution.py:53
  182.4 7.9 %copy-start.3 = (bf16[4096,32]{0,1:T(8,128)(2,1)S(1)}, bf16[4096,32]{0,1:T(8,128)(2,1)}, u32[]{:S(2)}) copy-start(bf16[4096,32]{0,1:T(8,128)(2,1)} %param.20) | copy-start | bytes 786436
  182.4 7.9 %copy-start.6 = (bf16[16,32]{1,0:T(8,128)(2,1)S(1)}, bf16[16,32]{1,0:T(8,128)(2,1)}, u32[]{:S(2)}) copy-start(bf16[16,32]{1,0:T(8,128)(2,1)} %param.13) | copy-start | bytes 3076
  242.7 2.9 copy-start.9
  242.7 3.0 copy-start.7
  250.9 50.4 %reduce-scatter.6.cloned.1.call-start = ((), (), s32[]{:S(2)}) async-start(), calls=%async_computation.4 | async-start | bytes 589824 | tf_op jit(solution)/shard_map/reduce_scatter | solution.py:53
  265.3 75.4 %reduce-scatter.8.cloned.1.call-start = ((), (), s32[]{:S(2)}) async-start(), calls=%async_computation.5 | async-start | bytes 73728 | tf_op jit(solution)/shard_map/reduce_scatter | solution.py:53
Sparse Core Ops, SparseCore 0:
  53.8 74.4 all-gather.6
  135.3 41.0 all-gather.8
  251.0 14.1 reduce-scatter.3
  267.6 33.6 reduce-scatter.5
  303.7 36.9 reduce-scatter.7
where the time goes:
time: 354 us; the launch traced here: 349 us
  waiting for transfers between devices  232 us (66%)
  blocking collectives  57.9 us (16%)
  local copies, waits for them, and re-layouts  15.9 us (4%)
  other arithmetic  15.8 us (4%)
  between operations  13.6 us (4%)
  matrix products  6.94 us (2%)
  starting transfers between devices  6.82 us (2%)
    all_gather x2, waiting for transfers between devices, all_in_one(): both, at, found = (lax.all_gather(jnp.concatenate(lines), axis), 0, {})  116 us
    reduce_scatter x3, waiting for transfers between devices, sum_in_order(): tiles = lax.psum_scatter(tiles, axes[k], scatter_dimension=0, tiled=True)  89.5 us
    all_gather x1, blocking collectives, on_device(): mixed = lax.all_gather(local_mixed, BLK, axis=1, tiled=True)  51 us
    ppermute x1, waiting for transfers between devices, shifted(): lax.ppermute(shard, axis, [(i, (i + by) % count) for i in range(count)])  26.3 us
  transfers between devices with their start and end apart: 6, of which 6 were waited for; matrix products, arithmetic and copies ran while one was open for 0% of the time, Pallas kernels for 0%

commit v1 on v0

v1 whole, which is shorter than its diff:
```python
import math

import jax
import jax.numpy as jnp
from jax import lax
from jax.sharding import Mesh
from jax.sharding import PartitionSpec as P

QUERY_HEADS = 32
KEY_VALUE_HEADS = 8
HEAD_SIZE = 128
EXPERTS = 4
FF = 7168
BLK = ("blk_0", "blk_1", "blk_2")


def exchanged(pieces):
    return lax.all_to_all(pieces, BLK, 0, 0, tiled=True)


def gathered(shard):
    return exchanged(jnp.broadcast_to(shard[None], (lax.axis_size(BLK), *shard.shape)))


def block_attention(queries, key_rows, value_rows, valid):
    slot_list = queries.shape[0]
    query_groups = QUERY_HEADS // KEY_VALUE_HEADS
    heads_of_queries = queries.reshape(slot_list, KEY_VALUE_HEADS, query_groups, HEAD_SIZE)
    heads_of_keys = key_rows.reshape(slot_list, -1, KEY_VALUE_HEADS, HEAD_SIZE)
    heads_of_values = value_rows.reshape(slot_list, -1, KEY_VALUE_HEADS, HEAD_SIZE)
    scores = jnp.einsum(
        "skgd,sckd->skgc", heads_of_queries, heads_of_keys, preferred_element_type=jnp.float32
    ) / math.sqrt(HEAD_SIZE)
    masked = valid[:, None, None, :]
    peak = jnp.max(jnp.where(masked, scores, -1e30), axis=-1, keepdims=True)
    peak = lax.reduce_precision(peak, 8, 7)
    weights = jnp.where(masked, jnp.exp(jnp.where(masked, scores, peak) - peak), 0.0)
    totals = jnp.sum(weights, axis=-1, keepdims=True)
    partial_value = jnp.einsum(
        "skgc,sckd->skgd",
        weights.astype(jnp.bfloat16),
        heads_of_values,
        preferred_element_type=jnp.float32,
    )
    partial_value = partial_value / jnp.where(totals > 0, totals, 1.0)
    lanes = lax.broadcasted_iota(jnp.int32, partial_value.shape, 3)
    stats = jnp.where(lanes < HEAD_SIZE // 2, peak, totals)
    both = jnp.concatenate([partial_value, stats], axis=2).astype(jnp.bfloat16)
    return both.reshape(slot_list * KEY_VALUE_HEADS, 2 * query_groups, HEAD_SIZE)


def merged(pieces):
    rows = pieces.shape[1] // 2
    pieces = pieces.astype(jnp.float32)
    values, stats = pieces[:, :rows], pieces[:, rows:]
    peaks, totals = stats[:, :, :1], stats[:, :, HEAD_SIZE // 2 : HEAD_SIZE // 2 + 1]
    scales = jnp.exp(peaks - jnp.max(peaks, axis=0, keepdims=True)) * totals
    return (jnp.sum(values * scales, axis=0) / jnp.sum(scales, axis=0)).astype(jnp.bfloat16)


def route_shares(normed, router_weight, expert_ids):
    logits = jnp.dot(normed, router_weight, preferred_element_type=jnp.float32)
    chosen = (expert_ids[:, :, None] == jnp.arange(EXPERTS, dtype=jnp.int32)[None, None, :]).astype(
        jnp.float32
    )
    picked = jnp.sum(chosen * logits[:, None, :], axis=-1)
    gates = jax.nn.sigmoid(picked - picked[:, ::-1])
    return jnp.sum(gates[:, :, None] * chosen, axis=1)


def on_device(
    hidden,
    queries,
    cache_kv,
    cache_len,
    inserted_key_value,
    insert_slot,
    prefix_len,
    out_weight,
    norm_gain,
    router_weight,
    expert_ids,
    gate_up,
    down_proj,
):
    cycle_size = lax.axis_size(BLK)
    dev_index = lax.axis_index(BLK)
    ctx_rows = cache_kv.shape[2]
    slots, features = hidden.shape
    positions_in_all = cycle_size * ctx_rows
    cache = cache_kv.at[:, insert_slot].set(inserted_key_value)
    slot_lengths = cache_len.at[insert_slot].set(prefix_len)
    first = jnp.full_like(cache_len, dev_index * ctx_rows)
    first = first.at[insert_slot].set(
        (dev_index * ctx_rows + positions_in_all // 2) % positions_in_all
    )
    positions = first[:, None] + jnp.arange(ctx_rows, dtype=jnp.int32)[None, :]
    valid = positions < slot_lengths[:, None]
    partials = block_attention(queries, cache[0], cache[1], valid)
    attn = gathered(merged(exchanged(partials))).reshape(slots, QUERY_HEADS * HEAD_SIZE)
    local_mixed = (
        hidden.astype(jnp.float32) + jnp.dot(attn, out_weight, preferred_element_type=jnp.float32)
    ).astype(jnp.bfloat16)
    mixed = gathered(local_mixed.reshape(-1, 128)).reshape(cycle_size, slots, features)
    mixed = jnp.transpose(mixed, (1, 0, 2)).reshape(slots, cycle_size * features)
    mixed_f = mixed.astype(jnp.float32)
    scale = lax.rsqrt(jnp.mean(mixed_f * mixed_f, axis=-1, keepdims=True) + 1e-05)
    normed = (mixed_f * scale * norm_gain.astype(jnp.float32)).astype(jnp.bfloat16)
    shares = route_shares(normed, router_weight, expert_ids)
    unit_count = gate_up.shape[2]
    expert_now = dev_index * unit_count // FF
    picker = (jnp.arange(EXPERTS, dtype=jnp.int32) == expert_now).astype(jnp.float32)
    expert_share = jnp.sum(shares * picker[None, :], axis=1)
    act = (
        jax.nn.silu(jnp.dot(normed, gate_up[0], preferred_element_type=jnp.float32))
        * jnp.dot(normed, gate_up[1], preferred_element_type=jnp.float32)
    ).astype(jnp.bfloat16)
    term = expert_share[:, None] * jnp.dot(act, down_proj, preferred_element_type=jnp.float32)
    term = term.astype(jnp.bfloat16).reshape(slots, cycle_size, features)
    term = jnp.transpose(term, (1, 0, 2)).reshape(cycle_size, -1, 128)
    moe = jnp.sum(exchanged(term).astype(jnp.float32), axis=0).reshape(slots, features)
    return (local_mixed.astype(jnp.float32) + moe).astype(jnp.bfloat16)


def solution(mesh):
    split = Mesh(
        mesh.devices.reshape(mesh.shape["rep"], 8, 8, 2), ("rep", "blk_0", "blk_1", "blk_2")
    )
    return jax.shard_map(
        on_device,
        mesh=split,
        in_specs=(
            P("rep", BLK),
            P("rep", None),
            P(None, "rep", BLK, None),
            P("rep"),
            P(None, "rep", BLK, None),
            P("rep"),
            P("rep"),
            P(None, BLK),
            P(),
            P(),
            P("rep", None),
            P(None, None, BLK),
            P(BLK, None),
        ),
        out_specs=P("rep", BLK),
        check_vma=False,
    )
```

time: 354 us -> 128 us (0.36); the launches traced: 349 us -> 127 us
  waiting for transfers between devices: 232 us -> 12.2 us
  blocking collectives: 57.9 us -> 80 us
  between operations: 13.6 us -> 0.38 us
  other arithmetic: 15.8 us -> 2.84 us
    all_gather x2 -> x0, waiting for transfers between devices: 116 us -> none  [all_in_one(): both, at, found = (lax.all_gather(jnp.concatenate(lines), axis), 0, {})]
    reduce_scatter x3 -> x0, waiting for transfers between devices: 89.5 us -> none  [sum_in_order(): tiles = lax.psum_scatter(tiles, axes[k], scatter_dimension=0, tiled=True)]
    all_to_all x0 -> x3, blocking collectives: none -> 80 us  [exchanged(): return lax.all_to_all(pieces, BLK, 0, 0, tiled=True)]
    all_gather x2 -> x0, blocking collectives: 57.9 us -> none  [the longest x1 51 us: on_device(): mixed = lax.all_gather(local_mixed, BLK, axis=1, tiled=True)]
    ppermute x1 -> x0, waiting for transfers between devices: 26.3 us -> none  [shifted(): lax.ppermute(shard, axis, [(i, (i + by) % count) for i in range(count)])]
    all_to_all x0 -> x1, waiting for transfers between devices: none -> 12.2 us  [exchanged(): return lax.all_to_all(pieces, BLK, 0, 0, tiled=True)]
    all_to_all x0 -> x1, starting transfers between devices: none -> 7.77 us  [exchanged(): return lax.all_to_all(pieces, BLK, 0, 0, tiled=True)]
    add x6 -> x0, other arithmetic: 6.62 us -> none  [the longest x2 4.93 us: merge_pair(): early_out * early_scale[..., None] + late_out * late_scale[..., None]]
  transfers between devices with their start and end apart: 6 -> 1, of which waited for: 6 -> 1; matrix products, arithmetic and copies ran while one was open for 0% -> 0% of each run, Pallas kernels for 0% -> 0%
where the time goes in v1:
time: 128 us; the launch traced here: 127 us
  blocking collectives  80 us (62%)
  local copies, waits for them, and re-layouts  16.1 us (13%)
  waiting for transfers between devices  12.2 us (10%)
  matrix products  7.8 us (6%)
  starting transfers between devices  7.77 us (6%)
  other arithmetic  2.84 us (2%)
    all_to_all x3, blocking collectives, exchanged(): return lax.all_to_all(pieces, BLK, 0, 0, tiled=True)  80 us
    all_to_all x1, waiting for transfers between devices, exchanged(): return lax.all_to_all(pieces, BLK, 0, 0, tiled=True)  12.2 us
    all_to_all x1, starting transfers between devices, exchanged(): return lax.all_to_all(pieces, BLK, 0, 0, tiled=True)  7.77 us
    unnamed x24, local copies, waits for them, and re-layouts  6.27 us
    dot_general x1, matrix products, on_device(): jnp.dot(act, down_proj, preferred_element_type=jnp.float32)  2.9 us
    scatter x1, local copies, waits for them, and re-layouts, on_device(): cache = cache_kv.at[:, insert_slot].set(inserted_key_value)  2.89 us
  transfers between devices with their start and end apart: 1, of which 1 were waited for; matrix products, arithmetic and copies ran while one was open for 0% of the time, Pallas kernels for 0%

profile of v1, /device:TPU:513, one launch (start us, length us, event | category | flops | bytes accessed | tf_op | source)
XLA Modules:
  0.0 127.1 jit_solution(8908721699124739272)
XLA Ops:
  0.0 3.4 %copy.97 = bf16[2,16,32,1024]{3,2,1,0:T(8,128)(2,1)} copy(bf16[2,16,32,1024]{3,2,1,0:T(8,128)(2,1)} %param.15) | data formatting | bytes 4194304
  3.4 1.3 %copy.74 = bf16[8,2,32,1024]{3,2,1,0:T(8,128)(2,1)S(1)} copy(bf16[8,2,32,1024]{3,2,0,1:T(8,128)(2,1)} %bitcast.53) | data formatting | bytes 2097152 | tf_op args[4]
  4.7 0.6 scatter_custom_fusion
  5.3 2.9 %scatter_fusion.1 = bf16[2,16,32,1024]{3,2,1,0:T(8,128)(2,1)} fusion(bf16[2,16,32,1024]{3,2,1,0:T(8,128)(2,1)} %copy.97, s32[8]{0:T(128)S(1)} %compare_select_fusion.1, bf16[8,2,32,1024]{3,2,1,0:T(8,128)(2,1)S(1)} %copy.74), kind=kCustom, calls=%fused_computation.2 | custom fusion | bytes 3145760 | tf_op jit(solution)/shard_map/scatter | solution.py:91
  8.2 1.7 %fusion.41 = (bf16[1,16,32,1024]{3,2,1,0:T(8,128)(2,1)S(1)}, bf16[1,16,32,1024]{3,2,1,0:T(8,128)(2,1)S(1)}) fusion(bf16[2,16,32,1024]{3,2,1,0:T(8,128)(2,1)} %scatter_fusion.1), kind=kLoop, calls=%fused_computation.70 | loop fusion | bytes 4194304 | tf_op jit(solution)/shard_map/slice | solution.py:99
  10.0 1.3 copy.85
  11.3 0.6 scatter_fusion
  12.0 2.0 %select_reduce_fusion = (f32[16,8,4]{2,1,0:T(8,128)S(1)}, f32[16,8,32,4]{2,3,1,0:T(4,128)S(1)}) fusion(pred[16,32]{1,0:T(8,128)(4,1)S(1)} %add_compare_fusion, bf16[16,8,4,128]{3,2,1,0:T(4,128)(2,1)S(1)} %reshape.131, bf16[16,32,8,128]{3,2,1,0:T(8,128)(2,1)} %bitcast.54), kind=kOutput, calls=%fused_computation.35 | convolution fusion | flops 4242944 | bytes 1247744 | tf_op jit(solution)/shard_map/skgd,sckd->skgc/dot_general | solution.py:31
  14.0 0.4 bitcast_reduce_fusion
  14.4 0.3 copy.86
  14.7 0.5 fusion.7
  15.2 0.3 select_convert_fusion
  15.7 41.2 %all_to_all.20 = bf16[128,8,128]{2,1,0:T(8,128)(2,1)S(1)} all-to-all(bf16[128,8,128]{2,1,0:T(8,128)(2,1)S(1)} %pad_maximum_fusion), channel_id=1, replica_groups=mesh['rep'=2,'blk_0'=8,'blk_1'=8,'blk_2'=2] {'blk_0','blk_1','blk_2'}, dimensions={0} | all-to-all | bytes 524288 | tf_op jit(solution)/shard_map/all_to_all | solution.py:18
  56.9 0.2 copy.77
  57.3 0.2 fusion.40
  57.5 0.2 fusion.22
  57.9 19.5 %all_to_all.21 = bf16[128,4,128]{2,1,0:T(4,128)(2,1)S(1)} all-to-all(bf16[128,4,128]{2,1,0:T(4,128)(2,1)S(1)} %broadcast_in_dim.107), channel_id=1, replica_groups=mesh['rep'=2,'blk_0'=8,'blk_1'=8,'blk_2'=2] {'blk_0','blk_1','blk_2'}, dimensions={0} | all-to-all | bytes 262144 | tf_op jit(solution)/shard_map/all_to_all | solution.py:18
  77.8 0.7 broadcast_in_dim.109
  78.5 7.8 %all-to-all-start.2 = ((bf16[128,4,128]{2,1,0:T(4,128)(2,1)}), bf16[128,4,128]{2,1,0:T(4,128)(2,1)S(1)}, u32[]{:S(2)}, u32[]{:S(2)}) async-start(bf16[128,4,128]{2,1,0:T(4,128)(2,1)} %broadcast_in_dim.109), calls=%async_computation.2 | async-start | bytes 262144 | tf_op jit(solution)/shard_map/all_to_all | solution.py:18
  86.4 12.2 %all-to-all-done.2 = bf16[128,4,128]{2,1,0:T(4,128)(2,1)S(1)} async-done(((bf16[128,4,128]{2,1,0:T(4,128)(2,1)}), bf16[128,4,128]{2,1,0:T(4,128)(2,1)S(1)}, u32[]{:S(2)}, u32[]{:S(2)}) %all-to-all-start.2) | async-done | bytes 131104 | tf_op jit(solution)/shard_map/all_to_all | solution.py:18
  98.8 0.2 fusion.19
  99.0 0.3 copy.80
  99.4 0.5 reshape.136
  99.9 0.2 fusion.23
  100.3 0.3 copy.82
  100.6 0.5 convert_element_type.87
  101.2 2.1 %fusion.3 = f32[16,224]{1,0:T(8,128)S(1)} fusion(bf16[16,4096]{1,0:T(8,128)(2,1)S(1)} %convert_element_type.87, bf16[2,4096,224]{1,2,0:T(8,128)(2,1)} %param.24), kind=kOutput, calls=%fused_computation.7 | convolution fusion | flops 29360128 | bytes 1980416 | tf_op jit(solution)/shard_map/dot_general | solution.py:115
  103.3 2.9 %fusion = bf16[16,4096]{1,0:T(8,128)(2,1)S(1)} fusion(bf16[224,4096]{1,0:T(8,128)(2,1)S(1)} %copy-done, bf16[16,4096]{1,0:T(8,128)(2,1)S(1)} %convert_element_type.87, bf16[2,4096,224]{1,2,0:T(8,128)(2,1)} %param.24, f32[16]{0:T(128)S(1)} %multiply_reduce_fusion, f32[16,224]{1,0:T(8,128)S(1)} %fusion.3), kind=kOutput, calls=%fused_computation.4 | convolution fusion | flops 58872832 | bytes 3946560 | tf_op jit(solution)/shard_map/dot_general | solution.py:118
  106.2 0.4 reshape.133
  106.6 0.2 copy.83
  107.0 19.3 %all_to_all.22 = bf16[128,4,128]{2,1,0:T(4,128)(2,1)S(1)} all-to-all(bf16[128,4,128]{2,1,0:T(4,128)(2,1)S(1)} %copy.84), channel_id=1, replica_groups=mesh['rep'=2,'blk_0'=8,'blk_1'=8,'blk_2'=2] {'blk_0','blk_1','blk_2'}, dimensions={0} | all-to-all | bytes 262144 | tf_op jit(solution)/shard_map/all_to_all | solution.py:18
  126.5 0.6 add_convert_fusion
  (53 shorter events, 2.0 us)
Async XLA Ops:
  0.0 103.3 %copy-start = (bf16[224,4096]{1,0:T(8,128)(2,1)S(1)}, bf16[224,4096]{1,0:T(8,128)(2,1)}, u32[]{:S(2)}) copy-start(bf16[224,4096]{1,0:T(8,128)(2,1)} %param.25) | copy-start | bytes 5505028
  0.0 3.4 %copy-start.9 = (s32[8]{0:T(128)S(1)}, s32[8]{0:T(128)}, u32[]{:S(2)}) copy-start(s32[8]{0:T(128)} %param.18) | copy-start | bytes 100
  9.9 1.3 %copy-start.3 = (bf16[16,4096]{1,0:T(8,128)(2,1)S(1)}, bf16[16,4096]{1,0:T(8,128)(2,1)}, u32[]{:S(2)}) copy-start(bf16[16,4096]{1,0:T(8,128)(2,1)} %param.14) | copy-start | bytes 393220
  10.0 1.4 %copy-start.1 = (s32[16]{0:T(128)S(1)}, s32[16]{0:T(128)}, u32[]{:S(2)}) copy-start(s32[16]{0:T(128)} %param.16) | copy-start | bytes 196
  10.0 1.4 %copy-start.8 = (s32[8]{0:T(128)S(1)}, s32[8]{0:T(128)}, u32[]{:S(2)}) copy-start(s32[8]{0:T(128)} %param.19) | copy-start | bytes 100
  15.2 62.3 %copy-start.2 = (bf16[4096,32]{0,1:T(8,128)(2,1)S(1)}, bf16[4096,32]{0,1:T(8,128)(2,1)}, u32[]{:S(2)}) copy-start(bf16[4096,32]{0,1:T(8,128)(2,1)} %param.20) | copy-start | bytes 786436
  15.2 62.3 %copy-start.6 = (bf16[16,32]{1,0:T(8,128)(2,1)S(1)}, bf16[16,32]{1,0:T(8,128)(2,1)}, u32[]{:S(2)}) copy-start(bf16[16,32]{1,0:T(8,128)(2,1)} %param.13) | copy-start | bytes 3076
  15.6 70.7 %copy-start.5 = (bf16[4096]{0:T(1024)(128)(2,1)S(1)}, bf16[4096]{0:T(1024)(128)(2,1)}, u32[]{:S(2)}) copy-start(bf16[4096]{0:T(1024)(128)(2,1)} %param.21) | copy-start | bytes 24580
  77.7 22.2 %copy-start.4 = (bf16[4096,4]{0,1:T(4,128)(2,1)S(1)}, bf16[4096,4]{0,1:T(4,128)(2,1)}, u32[]{:S(2)}) copy-start(bf16[4096,4]{0,1:T(4,128)(2,1)} %param.22) | copy-start | bytes 98308
  78.5 21.6 %copy-start.7 = (s32[16,2]{0,1:T(2,128)S(1)}, s32[16,2]{0,1:T(2,128)}, u32[]{:S(2)}) copy-start(s32[16,2]{0,1:T(2,128)} %param.23) | copy-start | bytes 388
  78.5 20.2 %all-to-all-start.2 = ((bf16[128,4,128]{2,1,0:T(4,128)(2,1)}), bf16[128,4,128]{2,1,0:T(4,128)(2,1)S(1)}, u32[]{:S(2)}, u32[]{:S(2)}) async-start(bf16[128,4,128]{2,1,0:T(4,128)(2,1)} %broadcast_in_dim.109), calls=%async_computation.2 | async-start | bytes 262144 | tf_op jit(solution)/shard_map/all_to_all | solution.py:18

commit v2 on v1

v2 whole, which is shorter than its diff:
```python
import functools
import math

import jax
import jax.numpy as jnp
from jax import lax
from jax.experimental import pallas as pl
from jax.experimental.pallas import tpu as pltpu
from jax.sharding import Mesh
from jax.sharding import PartitionSpec as P

QUERY_HEADS = 32
KEY_VALUE_HEADS = 8
HEAD_SIZE = 128
EXPERTS = 4
FF = 7168
BLK = ("blk_0", "blk_1", "blk_2")
GROUP = QUERY_HEADS // KEY_VALUE_HEADS
LANES = 128
IN_VMEM = pl.BlockSpec(memory_space=pltpu.VMEM)
IN_SMEM = pl.BlockSpec(memory_space=pltpu.SMEM)
ANYWHERE = pl.BlockSpec(memory_space=pl.ANY)
MIB = 1 << 20


def exchanged(pieces):
    return lax.all_to_all(pieces, BLK, 0, 0, tiled=True)


def params(mib):
    return pltpu.CompilerParams(vmem_limit_bytes=mib * MIB)


def attention_kernel(
    first, lengths, insert_slot, prefix_len, queries, cache, inserted, out, spread, rows, sems
):
    slots, prefixes, count = lengths.shape[0], insert_slot.shape[0], rows.shape[2]
    wide = 2 * QUERY_HEADS
    valid = []
    for s in range(slots):
        length, found, at = lengths[s], jnp.int32(0), jnp.int32(0)
        for j in range(prefixes):
            here = insert_slot[j] == s
            length = jnp.where(here, prefix_len[j], length)
            at = jnp.where(here, j, at)
            found = jnp.where(here, 1, found)
        valid.append(length - jnp.where(found == 1, first[1], first[0]))

        @pl.when(found == 1)
        def _():
            pltpu.make_async_copy(inserted.at[:, at], rows.at[s], sems.at[s]).start()

        @pl.when(found == 0)
        def _():
            pltpu.make_async_copy(cache.at[:, s], rows.at[s], sems.at[s]).start()

    for g in range(KEY_VALUE_HEADS):
        for h in range(GROUP):
            at = (g * GROUP + h) * HEAD_SIZE
            one = queries[:, at : at + HEAD_SIZE].astype(jnp.float32)
            for twin in range(2):
                spread[pl.ds(g * 2 * GROUP + twin * GROUP + h, slots, stride=wide), :] = one
    shape = (wide, KEY_VALUE_HEADS * HEAD_SIZE)
    own = (
        lax.broadcasted_iota(jnp.int32, shape, 0) // (2 * GROUP)
        == lax.broadcasted_iota(jnp.int32, shape, 1) // HEAD_SIZE
    )
    is_value = lax.broadcasted_iota(jnp.int32, (wide, HEAD_SIZE), 0) % (2 * GROUP) < GROUP
    is_peak = lax.broadcasted_iota(jnp.int32, (wide, HEAD_SIZE), 1) < HEAD_SIZE // 2
    place = lax.broadcasted_iota(jnp.int32, (wide, count), 1)
    for s in range(slots):
        one = spread[s * wide : (s + 1) * wide, :]
        tiled = jnp.concatenate([one] * KEY_VALUE_HEADS, axis=1)
        blocks = jnp.where(own, tiled, 0.0).astype(jnp.bfloat16)
        pltpu.make_async_copy(cache.at[:, s], rows.at[s], sems.at[s]).wait()
        scores = lax.dot_general(
            blocks, rows[s, 0], (((1,), (1,)), ((), ())), preferred_element_type=jnp.float32
        ) * (1.0 / math.sqrt(HEAD_SIZE))
        inside = place < valid[s]
        scores = jnp.where(inside, scores, -1e30)
        peak = jnp.max(scores, axis=1, keepdims=True).astype(jnp.bfloat16).astype(jnp.float32)
        weights = jnp.where(inside, jnp.exp(scores - peak), 0.0)
        total = jnp.sum(weights, axis=1, keepdims=True)
        every = jnp.dot(
            weights.astype(jnp.bfloat16), rows[s, 1], preferred_element_type=jnp.float32
        )
        value = jnp.concatenate(
            [
                every[g * 2 * GROUP : (g + 1) * 2 * GROUP, g * HEAD_SIZE : (g + 1) * HEAD_SIZE]
                for g in range(KEY_VALUE_HEADS)
            ],
            axis=0,
        )
        value = value / jnp.where(total > 0.0, total, 1.0)
        result = jnp.where(is_value, value, jnp.where(is_peak, peak, total))
        out[s] = result.astype(jnp.bfloat16)


def combine_kernel(pieces, out):
    shape = pieces.shape[1:]
    left = lax.broadcasted_iota(jnp.int32, shape, 1) < HEAD_SIZE // 2
    half = HEAD_SIZE // 2
    found = pieces[...].astype(jnp.float32)
    highest = jnp.max(found, axis=0, keepdims=True)
    scale = jnp.exp(found - highest) * pltpu.roll(found, half, axis=2)
    scale = jnp.where(left[None], scale, pltpu.roll(scale, half, axis=2))
    scale = pltpu.roll(scale, GROUP, axis=1)
    value = jnp.sum(found * scale, axis=0) / jnp.sum(scale, axis=0)
    out[...] = jnp.broadcast_to(value[None, :GROUP].astype(jnp.bfloat16), out.shape)


def project_kernel(attn, weight, hidden, mixed, packed, spread):
    slots, columns = hidden.shape
    spread[...] = attn[...].astype(jnp.float32)
    blocks = [spread[pl.ds(k, slots, stride=QUERY_HEADS), :] for k in range(QUERY_HEADS)]
    whole = jnp.concatenate(blocks, axis=1).astype(jnp.bfloat16)
    total = hidden[...].astype(jnp.float32) + jnp.dot(
        whole, weight[...], preferred_element_type=jnp.float32
    )
    mixed[...] = total.astype(jnp.bfloat16)
    share = LANES // columns
    deep = slots // share
    line = jnp.concatenate([total[b * deep : (b + 1) * deep] for b in range(share)], axis=1)
    packed[...] = jnp.broadcast_to(line[None].astype(jnp.bfloat16), packed.shape)


def swapped(tiles, share):
    slots = tiles.shape[1]
    deep, width = slots // share, LANES // share
    row = lax.broadcasted_iota(jnp.int32, tiles.shape, 1) // deep
    lane = lax.broadcasted_iota(jnp.int32, tiles.shape, 2) // width
    turn = (lane - row + share) % share
    result = tiles
    for j in range(1, share):
        moved = pltpu.roll(pltpu.roll(tiles, j * width, axis=2), slots - j * deep, axis=1)
        result = jnp.where(turn == j, moved, result)
    return result


def experts_kernel(share, expert, gathered, gain, router, chosen, gate_up, down, out):
    blocks, slots = gathered.shape[0], gathered.shape[1]
    mixed = swapped(gathered[...].astype(jnp.float32), share)
    squares = jnp.sum(jnp.sum(mixed * mixed, axis=0), axis=1, keepdims=True)
    scale = lax.rsqrt(squares / (blocks * LANES) + 1e-05)
    normed = (mixed * scale[None] * gain[...].astype(jnp.float32)).astype(jnp.bfloat16)
    plain = normed.astype(jnp.float32)
    logits = [
        jnp.sum(
            jnp.sum(plain * router[e].astype(jnp.float32), axis=0), axis=1, keepdims=True
        )
        for e in range(EXPERTS)
    ]
    ids = [chosen[:, i : i + 1] for i in range(2)]
    picked = [sum(jnp.where(k == e, logits[e], 0.0) for e in range(EXPERTS)) for k in ids]
    gates = [jax.nn.sigmoid(picked[i] - picked[1 - i]) for i in range(2)]
    part = sum(jnp.where(ids[i] == expert[0], gates[i], 0.0) for i in range(2))
    line = jnp.concatenate([normed[k] for k in range(blocks)], axis=1)
    gate = jnp.dot(line, gate_up[0], preferred_element_type=jnp.float32)
    up = jnp.dot(line, gate_up[1], preferred_element_type=jnp.float32)
    act = (gate * jax.nn.sigmoid(gate) * up).astype(jnp.bfloat16)
    term = part * jnp.dot(act, down[...], preferred_element_type=jnp.float32)
    tiles = [term[None, :, k * LANES : (k + 1) * LANES] for k in range(blocks)]
    out[...] = swapped(jnp.concatenate(tiles, axis=0), share).astype(jnp.bfloat16)


def final_kernel(pieces, mixed, out):
    slots, columns = mixed.shape
    share = LANES // columns
    total = jnp.sum(pieces[...].astype(jnp.float32), axis=0)
    moe = jnp.concatenate(
        [total[:, b * columns : (b + 1) * columns] for b in range(share)], axis=0
    )
    out[...] = (mixed[...].astype(jnp.float32) + moe).astype(jnp.bfloat16)


def on_device(
    hidden,
    queries,
    cache_kv,
    cache_len,
    inserted_key_value,
    insert_slot,
    prefix_len,
    out_weight,
    norm_gain,
    router_weight,
    expert_ids,
    gate_up,
    down_proj,
):
    devices = lax.axis_size(BLK)
    dev_index = lax.axis_index(BLK)
    slots, columns = hidden.shape
    ctx_rows, kv_width = cache_kv.shape[2:]
    share = LANES // columns
    width = devices * columns
    blocks = width // LANES
    bf16 = jnp.bfloat16

    positions = devices * ctx_rows
    here = dev_index * ctx_rows
    first = jnp.stack([here, (here + positions // 2) % positions]).astype(jnp.int32)
    partials = pl.pallas_call(
        attention_kernel,
        out_shape=jax.ShapeDtypeStruct((slots, 2 * QUERY_HEADS, HEAD_SIZE), bf16),
        in_specs=[IN_SMEM] * 4 + [IN_VMEM, ANYWHERE, ANYWHERE],
        out_specs=IN_VMEM,
        scratch_shapes=[
            pltpu.VMEM((slots * 2 * QUERY_HEADS, HEAD_SIZE), jnp.float32),
            pltpu.VMEM((slots, 2, ctx_rows, kv_width), bf16),
            pltpu.SemaphoreType.DMA((slots,)),
        ],
        compiler_params=params(12),
        name="attention",
    )(first, cache_len, insert_slot, prefix_len, queries, cache_kv, inserted_key_value)
    pieces = exchanged(partials.reshape(slots * KEY_VALUE_HEADS, 2 * GROUP, HEAD_SIZE))

    own = pl.pallas_call(
        combine_kernel,
        out_shape=jax.ShapeDtypeStruct((devices, GROUP, HEAD_SIZE), bf16),
        in_specs=[IN_VMEM],
        out_specs=IN_VMEM,
        compiler_params=params(8),
        name="combine",
    )(pieces)
    attn = exchanged(own).reshape(slots * QUERY_HEADS, HEAD_SIZE)

    local_mixed, packed = pl.pallas_call(
        project_kernel,
        out_shape=(
            jax.ShapeDtypeStruct((slots, columns), bf16),
            jax.ShapeDtypeStruct((devices, slots // share, LANES), bf16),
        ),
        in_specs=[IN_VMEM] * 3,
        out_specs=(IN_VMEM, IN_VMEM),
        scratch_shapes=[pltpu.VMEM((slots * QUERY_HEADS, HEAD_SIZE), jnp.float32)],
        compiler_params=params(8),
        name="project",
    )(attn, out_weight, hidden)
    gathered = exchanged(packed).reshape(blocks, slots, LANES)

    expert = (dev_index * gate_up.shape[2] // FF).astype(jnp.int32).reshape(1)
    terms = pl.pallas_call(
        functools.partial(experts_kernel, share),
        out_shape=jax.ShapeDtypeStruct((blocks, slots, LANES), bf16),
        in_specs=[IN_SMEM] + [IN_VMEM] * 6,
        out_specs=IN_VMEM,
        compiler_params=params(16),
        name="experts",
    )(
        expert,
        gathered,
        norm_gain.reshape(blocks, 1, LANES),
        router_weight.T.reshape(EXPERTS, blocks, 1, LANES),
        expert_ids,
        gate_up,
        down_proj,
    )
    moe = exchanged(terms.reshape(devices, slots // share, LANES))
    return pl.pallas_call(
        final_kernel,
        out_shape=jax.ShapeDtypeStruct((slots, columns), bf16),
        in_specs=[IN_VMEM] * 2,
        out_specs=IN_VMEM,
        compiler_params=params(4),
        name="final",
    )(moe, local_mixed)


def solution(mesh):
    split = Mesh(
        mesh.devices.reshape(mesh.shape["rep"], 8, 8, 2), ("rep", "blk_0", "blk_1", "blk_2")
    )
    return jax.shard_map(
        on_device,
        mesh=split,
        in_specs=(
            P("rep", BLK),
            P("rep", None),
            P(None, "rep", BLK, None),
            P("rep"),
            P(None, "rep", BLK, None),
            P("rep"),
            P("rep"),
            P(None, BLK),
            P(),
            P(),
            P("rep", None),
            P(None, None, BLK),
            P(BLK, None),
        ),
        out_specs=P("rep", BLK),
        check_vma=False,
    )
```

time: 128 us -> 127 us (level)
  blocking collectives: 80 us -> 63.8 us
  Pallas kernels: 0 us -> 14.5 us
  matrix products: 7.8 us -> 0 us
  starting transfers between devices: 7.77 us -> 15.3 us
  waiting for transfers between devices: 12.2 us -> 17.7 us
  other arithmetic: 2.84 us -> 0.07 us
    all_to_all x3 -> x2, blocking collectives: 80 us -> 63.8 us  [exchanged(): return lax.all_to_all(pieces, BLK, 0, 0, tiled=True)]
    pallas_call x0 -> x5, Pallas kernels: none -> 14.5 us  [the longest x1 10.2 us: on_device(): pl.pallas_call(attention_kernel, out_shape=jax.ShapeDtypeStruct((slots, 2...]
    unnamed x24 -> x29, local copies, waits for them, and re-layouts: 6.27 us -> 14.8 us
    dot_general x6 -> x0, matrix products: 7.8 us -> none  [the longest x1 2.9 us: on_device(): jnp.dot(act, down_proj, preferred_element_type=jnp.float32)]
    all_to_all x1 -> x2, starting transfers between devices: 7.77 us -> 15.3 us  [exchanged(): return lax.all_to_all(pieces, BLK, 0, 0, tiled=True)]
    all_to_all x1 -> x2, waiting for transfers between devices: 12.2 us -> 17.7 us  [exchanged(): return lax.all_to_all(pieces, BLK, 0, 0, tiled=True)]
    scatter x3 -> x0, local copies, waits for them, and re-layouts: 4.09 us -> none  [the longest x1 2.89 us: on_device(): cache = cache_kv.at[:, insert_slot].set(inserted_key_value)]
    slice x1 -> x0, local copies, waits for them, and re-layouts: 1.72 us -> none  [on_device(): partials = block_attention(queries, cache[0], cache[1], valid)]
  transfers between devices with their start and end apart: 1 -> 2, of which waited for: 1 -> 2; matrix products, arithmetic and copies ran while one was open for 0% -> 6% of each run, Pallas kernels for 0% -> 0%
where the time goes in v2:
time: 127 us; the launch traced here: 126 us
  blocking collectives  63.8 us (50%)
  waiting for transfers between devices  17.7 us (14%)
  starting transfers between devices  15.3 us (12%)
  local copies, waits for them, and re-layouts  14.9 us (12%)
  Pallas kernels  14.5 us (11%)
    all_to_all x2, blocking collectives, exchanged(): return lax.all_to_all(pieces, BLK, 0, 0, tiled=True)  63.8 us
    all_to_all x2, waiting for transfers between devices, exchanged(): return lax.all_to_all(pieces, BLK, 0, 0, tiled=True)  17.7 us
    all_to_all x2, starting transfers between devices, exchanged(): return lax.all_to_all(pieces, BLK, 0, 0, tiled=True)  15.3 us
    unnamed x29, local copies, waits for them, and re-layouts  14.8 us
    pallas_call x1, Pallas kernels, on_device(): pl.pallas_call(attention_kernel, out_shape=jax.ShapeDtypeStruct((slots, 2...  10.2 us
  transfers between devices with their start and end apart: 2, of which 2 were waited for; matrix products, arithmetic and copies ran while one was open for 6% of the time, Pallas kernels for 0%

profile of v2, /device:TPU:513, one launch (start us, length us, event | category | flops | bytes accessed | tf_op | source)
XLA Modules:
  0.0 126.4 jit_solution(5769813511832512388)
XLA Ops:
  0.0 0.0 copy-start.5
  0.0 0.1 pad_add_fusion.first
  0.1 0.0 copy-start.1
  0.1 1.6 %copy-done.1 = bf16[2,16,32,1024]{3,2,1,0:T(8,128)(2,1)S(1)} copy-done((bf16[2,16,32,1024]{3,2,1,0:T(8,128)(2,1)S(1)}, bf16[2,16,32,1024]{3,2,1,0:T(8,128)(2,1)}, u32[]{:S(2)}) %copy-start.1) | copy-done | bytes 2097176
  1.7 1.2 copy-done.3
  2.9 0.9 copy-done.4
  3.8 0.7 copy-done.6
  4.5 0.7 copy-done.7
  5.1 0.7 copy-done.8
  5.8 10.2 %attention.1 = bf16[16,64,128]{2,1,0:T(8,128)(2,1)S(1)} custom-call(s32[2]{0:T(128)S(1)} %pad_add_fusion.first, s32[16]{0:T(128)S(1)} %copy-done.6, s32[8]{0:T(128)S(1)} %copy-done.7, s32[8]{0:T(128)S(1)} %copy-done.8, bf16[16,4096]{1,0:T(8,128)(2,1)S(1)} %copy-done.4, bf16[2,16,32,1024]{3,2,1,0:T(8,128)(2,1)S(1)} %copy-done.1, ...), custom_call_target="tpu_custom_call" | custom-call | tf_op jit(solution)/shard_map/attention/pallas_call | solution.py:203
  15.9 41.2 %all_to_all.20.pieces = bf16[128,8,128]{2,1,0:T(8,128)(2,1)S(1)} all-to-all(bf16[128,8,128]{2,1,0:T(8,128)(2,1)S(1)} %bitcast.9), channel_id=1, replica_groups=mesh['rep'=2,'blk_0'=8,'blk_1'=8,'blk_2'=2] {'blk_0','blk_1','blk_2'}, dimensions={0} | all-to-all | bytes 524288 | tf_op jit(solution)/shard_map/all_to_all | solution.py:27
  57.1 1.0 combine.1
  58.1 7.7 %all-to-all-start.1 = ((bf16[128,4,128]{2,1,0:T(4,128)(2,1)}), bf16[128,4,128]{2,1,0:T(4,128)(2,1)S(1)}, u32[]{:S(2)}, u32[]{:S(2)}) async-start(bf16[128,4,128]{2,1,0:T(4,128)(2,1)} %combine.1), calls=%async_computation.1 | async-start | bytes 262144 | tf_op jit(solution)/shard_map/all_to_all | solution.py:27
  65.8 0.0 copy-done.9
  65.9 0.5 copy.17.weight
  66.3 11.9 %all-to-all-done.1 = bf16[128,4,128]{2,1,0:T(4,128)(2,1)S(1)} async-done(((bf16[128,4,128]{2,1,0:T(4,128)(2,1)}), bf16[128,4,128]{2,1,0:T(4,128)(2,1)S(1)}, u32[]{:S(2)}, u32[]{:S(2)}) %all-to-all-start.1) | async-done | bytes 131104 | tf_op jit(solution)/shard_map/all_to_all | solution.py:27
  78.3 0.0 copy-done.5
  78.3 1.1 project.1
  79.4 7.6 %all-to-all-start.2 = ((bf16[128,4,128]{2,1,0:T(4,128)(2,1)}), bf16[128,4,128]{2,1,0:T(4,128)(2,1)S(1)}, u32[]{:S(2)}, u32[]{:S(2)}) async-start(bf16[128,4,128]{2,1,0:T(4,128)(2,1)} %get-tuple-element.7), calls=%async_computation.2 | async-start | bytes 262144 | tf_op jit(solution)/shard_map/all_to_all | solution.py:27
  87.0 0.0 copy-done.12
  87.0 0.1 copy.20.chosen
  87.1 0.0 copy-done.11
  87.2 0.0 copy-done.10
  87.2 0.1 reshape.28.router
  87.2 0.0 copy-start.2
  87.2 6.3 %copy.21.gate_up = bf16[2,4096,224]{2,1,0:T(8,128)(2,1)} copy(bf16[2,4096,224]{1,2,0:T(8,128)(2,1)} %param.24) | data formatting | bytes 7340032 | tf_op args[11]
  93.6 5.8 %all-to-all-done.2 = bf16[128,4,128]{2,1,0:T(4,128)(2,1)S(1)} async-done(((bf16[128,4,128]{2,1,0:T(4,128)(2,1)}), bf16[128,4,128]{2,1,0:T(4,128)(2,1)S(1)}, u32[]{:S(2)}, u32[]{:S(2)}) %all-to-all-start.2) | async-done | bytes 131104 | tf_op jit(solution)/shard_map/all_to_all | solution.py:27
  99.4 0.0 copy-done.2
  99.4 2.2 %copy-done = bf16[2,4096,224]{2,1,0:T(8,128)(2,1)S(1)} copy-done((bf16[2,4096,224]{2,1,0:T(8,128)(2,1)S(1)}, bf16[2,4096,224]{2,1,0:T(8,128)(2,1)}, u32[]{:S(2)}) %copy-start) | copy-done | bytes 3670040
  101.6 1.4 %experts.1 = bf16[32,16,128]{2,1,0:T(8,128)(2,1)S(1)} custom-call(s32[1]{0:T(128)} %bitcast.expert, bf16[32,16,128]{2,1,0:T(8,128)(2,1)S(1)} %bitcast.10, bf16[32,1,128]{2,1,0:T(2,128)(2,1)S(1)} %copy.18.gain, bf16[4,32,1,128]{3,2,1,0:T(2,128)(2,1)S(1)} %reshape.28.router, s32[16,2]{1,0:T(8,128)S(1)} %copy.20.chosen, bf16[2,4096,224]{2,1,0:T(8,128)(2,1)S(1)} %copy-done, ...), custom_call_target="tpu_custom_call" | custom-call | tf_op jit(solution)/shard_map/experts/pallas_call | solution.py:243
  102.9 22.7 %all_to_all.21.pieces = bf16[128,4,128]{2,1,0:T(4,128)(2,1)S(1)} all-to-all(bf16[128,4,128]{2,1,0:T(4,128)(2,1)S(1)} %bitcast.12), channel_id=1, replica_groups=mesh['rep'=2,'blk_0'=8,'blk_1'=8,'blk_2'=2] {'blk_0','blk_1','blk_2'}, dimensions={0} | all-to-all | bytes 262144 | tf_op jit(solution)/shard_map/all_to_all | solution.py:27
  125.6 0.8 final.1
  (11 shorter events, 0.0 us)
Async XLA Ops:
  0.0 78.3 %copy-start.5 = (bf16[16,32]{1,0:T(8,128)(2,1)S(1)}, bf16[16,32]{1,0:T(8,128)(2,1)}, u32[]{:S(2)}) copy-start(bf16[16,32]{1,0:T(8,128)(2,1)} %hidden.1) | copy-start | bytes 3076
  0.1 1.6 %copy-start.1 = (bf16[2,16,32,1024]{3,2,1,0:T(8,128)(2,1)S(1)}, bf16[2,16,32,1024]{3,2,1,0:T(8,128)(2,1)}, u32[]{:S(2)}) copy-start(bf16[2,16,32,1024]{3,2,1,0:T(8,128)(2,1)} %cache.1) | copy-start | bytes 6291460
  1.7 1.2 copy-start.3
  2.9 0.9 copy-start.4
  3.8 0.7 copy-start.6
  4.5 0.7 copy-start.7
  5.1 0.7 copy-start.8
  5.8 60.1 %copy-start.9 = (bf16[4096,32]{0,1:T(8,128)(2,1)S(1)}, bf16[4096,32]{0,1:T(8,128)(2,1)}, u32[]{:S(2)}) copy-start(bf16[4096,32]{0,1:T(8,128)(2,1)} %param.20) | copy-start | bytes 786436
  5.8 81.3 %copy-start.12 = (s32[16,2]{0,1:T(2,128)S(1)}, s32[16,2]{0,1:T(2,128)}, u32[]{:S(2)}) copy-start(s32[16,2]{0,1:T(2,128)} %param.23) | copy-start | bytes 388
  5.8 81.4 %copy-start.11 = (bf16[4096]{0:T(1024)(128)(2,1)S(1)}, bf16[4096]{0:T(1024)(128)(2,1)}, u32[]{:S(2)}) copy-start(bf16[4096]{0:T(1024)(128)(2,1)} %param.21) | copy-start | bytes 24580
  5.8 81.4 %copy-start.10 = (bf16[4096,4]{0,1:T(4,128)(2,1)S(1)}, bf16[4096,4]{0,1:T(4,128)(2,1)}, u32[]{:S(2)}) copy-start(bf16[4096,4]{0,1:T(4,128)(2,1)} %param.22) | copy-start | bytes 98308
  58.1 20.1 %all-to-all-start.1 = ((bf16[128,4,128]{2,1,0:T(4,128)(2,1)}), bf16[128,4,128]{2,1,0:T(4,128)(2,1)S(1)}, u32[]{:S(2)}, u32[]{:S(2)}) async-start(bf16[128,4,128]{2,1,0:T(4,128)(2,1)} %combine.1), calls=%async_computation.1 | async-start | bytes 262144 | tf_op jit(solution)/shard_map/all_to_all | solution.py:27
  79.4 20.0 %all-to-all-start.2 = ((bf16[128,4,128]{2,1,0:T(4,128)(2,1)}), bf16[128,4,128]{2,1,0:T(4,128)(2,1)S(1)}, u32[]{:S(2)}, u32[]{:S(2)}) async-start(bf16[128,4,128]{2,1,0:T(4,128)(2,1)} %get-tuple-element.7), calls=%async_computation.2 | async-start | bytes 262144 | tf_op jit(solution)/shard_map/all_to_all | solution.py:27
  87.2 12.2 %copy-start.2 = (bf16[224,4096]{1,0:T(8,128)(2,1)S(1)}, bf16[224,4096]{1,0:T(8,128)(2,1)}, u32[]{:S(2)}) copy-start(bf16[224,4096]{1,0:T(8,128)(2,1)} %down.1) | copy-start | bytes 5505028
  99.4 2.2 %copy-start = (bf16[2,4096,224]{2,1,0:T(8,128)(2,1)S(1)}, bf16[2,4096,224]{2,1,0:T(8,128)(2,1)}, u32[]{:S(2)}) copy-start(bf16[2,4096,224]{2,1,0:T(8,128)(2,1)} %copy.21.gate_up) | copy-start | bytes 11010052

commit v3 on v2

--- a/solution.py
+++ b/solution.py
@@ -19,8 +19,11 @@
 LANES = 128
 IN_VMEM = pl.BlockSpec(memory_space=pltpu.VMEM)
 IN_SMEM = pl.BlockSpec(memory_space=pltpu.SMEM)
-ANYWHERE = pl.BlockSpec(memory_space=pl.ANY)
+IN_HBM = pl.BlockSpec(memory_space=pltpu.HBM)
+BATCH = 4
 MIB = 1 << 20
+COVER = pl.CostEstimate(flops=8*10**8, bytes_accessed=8 << 20, transcendentals=0)
+ALL_VMEM = 67043328
 
 
 def exchanged(pieces):
@@ -32,34 +35,69 @@
 
 
 def attention_kernel(
-    first, lengths, insert_slot, prefix_len, queries, cache, inserted, out, spread, rows, sems
+    positions,
+    first,
+    lengths_in,
+    insert_slot_in,
+    prefix_len_in,
+    queries_in,
+    cache,
+    inserted,
+    out,
+    lengths,
+    insert_slot,
+    prefix_len,
+    queries,
+    spread,
+    rows,
+    score_of,
+    sems,
 ):
     slots, prefixes, count = lengths.shape[0], insert_slot.shape[0], rows.shape[2]
     wide = 2 * QUERY_HEADS
-    valid = []
-    for s in range(slots):
-        length, found, at = lengths[s], jnp.int32(0), jnp.int32(0)
-        for j in range(prefixes):
-            here = insert_slot[j] == s
-            length = jnp.where(here, prefix_len[j], length)
-            at = jnp.where(here, j, at)
-            found = jnp.where(here, 1, found)
-        valid.append(length - jnp.where(found == 1, first[1], first[0]))
-
-        @pl.when(found == 1)
-        def _():
-            pltpu.make_async_copy(inserted.at[:, at], rows.at[s], sems.at[s]).start()
-
-        @pl.when(found == 0)
-        def _():
-            pltpu.make_async_copy(cache.at[:, s], rows.at[s], sems.at[s]).start()
-
+    copies = [
+        pltpu.make_async_copy(lengths_in, lengths, sems.at[0]),
+        pltpu.make_async_copy(insert_slot_in, insert_slot, sems.at[1]),
+        pltpu.make_async_copy(prefix_len_in, prefix_len, sems.at[2]),
+        pltpu.make_async_copy(queries_in, queries, sems.at[3]),
+    ]
+    copies += [
+        pltpu.make_async_copy(cache.at[k, s], rows.at[s, k], sems.at[4 + 2 * s + k])
+        for s in range(slots)
+        for k in range(2)
+    ]
+    copies += [
+        pltpu.make_async_copy(
+            inserted.at[k, j], rows.at[slots + j, k], sems.at[4 + 2 * (slots + j) + k]
+        )
+        for j in range(prefixes)
+        for k in range(2)
+    ]
+    for copy in copies:
+        copy.start()
+    for copy in copies[:4]:
+        copy.wait()
     for g in range(KEY_VALUE_HEADS):
         for h in range(GROUP):
             at = (g * GROUP + h) * HEAD_SIZE
             one = queries[:, at : at + HEAD_SIZE].astype(jnp.float32)
             for twin in range(2):
                 spread[pl.ds(g * 2 * GROUP + twin * GROUP + h, slots, stride=wide), :] = one
+    here = first[0]
+    half = positions // 2
+    there = jnp.where(here < half, here + half, here - half)
+    valid, source = [], []
+    for s in range(slots):
+        length, at, start = lengths[s], jnp.int32(s), here
+        for j in range(prefixes):
+            mine = insert_slot[j] == s
+            length = jnp.where(mine, prefix_len[j], length)
+            at = jnp.where(mine, slots + j, at)
+            start = jnp.where(mine, there, start)
+        valid.append(length - start)
+        source.append(at)
+    for copy in copies[4:]:
+        copy.wait()
     shape = (wide, KEY_VALUE_HEADS * HEAD_SIZE)
     own = (
         lax.broadcasted_iota(jnp.int32, shape, 0) // (2 * GROUP)
@@ -72,28 +110,39 @@
         one = spread[s * wide : (s + 1) * wide, :]
         tiled = jnp.concatenate([one] * KEY_VALUE_HEADS, axis=1)
         blocks = jnp.where(own, tiled, 0.0).astype(jnp.bfloat16)
-        pltpu.make_async_copy(cache.at[:, s], rows.at[s], sems.at[s]).wait()
-        scores = lax.dot_general(
-            blocks, rows[s, 0], (((1,), (1,)), ((), ())), preferred_element_type=jnp.float32
+        score_of[s] = lax.dot_general(
+            blocks,
+            rows[source[s], 0],
+            (((1,), (1,)), ((), ())),
+            preferred_element_type=jnp.float32,
         ) * (1.0 / math.sqrt(HEAD_SIZE))
-        inside = place < valid[s]
-        scores = jnp.where(inside, scores, -1e30)
-        peak = jnp.max(scores, axis=1, keepdims=True).astype(jnp.bfloat16).astype(jnp.float32)
-        weights = jnp.where(inside, jnp.exp(scores - peak), 0.0)
-        total = jnp.sum(weights, axis=1, keepdims=True)
-        every = jnp.dot(
-            weights.astype(jnp.bfloat16), rows[s, 1], preferred_element_type=jnp.float32
-        )
-        value = jnp.concatenate(
-            [
-                every[g * 2 * GROUP : (g + 1) * 2 * GROUP, g * HEAD_SIZE : (g + 1) * HEAD_SIZE]
-                for g in range(KEY_VALUE_HEADS)
-            ],
-            axis=0,
-        )
-        value = value / jnp.where(total > 0.0, total, 1.0)
-        result = jnp.where(is_value, value, jnp.where(is_peak, peak, total))
-        out[s] = result.astype(jnp.bfloat16)
+    for batch in range(0, slots, BATCH):
+        several = range(batch, batch + BATCH)
+        inside = [place < valid[s] for s in several]
+        scores = [jnp.where(i, score_of[s], -1e30) for i, s in zip(inside, several)]
+        peaks = [jnp.max(x, axis=1, keepdims=True) for x in scores]
+        peaks = [x.astype(jnp.bfloat16).astype(jnp.float32) for x in peaks]
+        weights = [
+            jnp.where(i, jnp.exp(x - p), 0.0) for i, x, p in zip(inside, scores, peaks)
+        ]
+        totals = [jnp.sum(x, axis=1, keepdims=True) for x in weights]
+        every = [
+            jnp.dot(
+                x.astype(jnp.bfloat16), rows[source[s], 1], preferred_element_type=jnp.float32
+            )
+            for x, s in zip(weights, several)
+        ]
+        for s, full, peak, total in zip(several, every, peaks, totals):
+            value = jnp.concatenate(
+                [
+                    full[g * 2 * GROUP : (g + 1) * 2 * GROUP, g * HEAD_SIZE : (g + 1) * HEAD_SIZE]
+                    for g in range(KEY_VALUE_HEADS)
+                ],
+                axis=0,
+            )
+            value = value / jnp.where(total > 0.0, total, 1.0)
+            result = jnp.where(is_value, value, jnp.where(is_peak, peak, total))
+            out[s] = result.astype(jnp.bfloat16)
 
 
 def combine_kernel(pieces, out):
@@ -114,8 +163,8 @@
     spread[...] = attn[...].astype(jnp.float32)
     blocks = [spread[pl.ds(k, slots, stride=QUERY_HEADS), :] for k in range(QUERY_HEADS)]
     whole = jnp.concatenate(blocks, axis=1).astype(jnp.bfloat16)
-    total = hidden[...].astype(jnp.float32) + jnp.dot(
-        whole, weight[...], preferred_element_type=jnp.float32
+    total = hidden[...].astype(jnp.float32) + lax.dot_general(
+        whole, weight[...], (((1,), (1,)), ((), ())), preferred_element_type=jnp.float32
     )
     mixed[...] = total.astype(jnp.bfloat16)
     share = LANES // columns
@@ -139,24 +188,36 @@
 
 def experts_kernel(share, expert, gathered, gain, router, chosen, gate_up, down, out):
     blocks, slots = gathered.shape[0], gathered.shape[1]
-    mixed = swapped(gathered[...].astype(jnp.float32), share)
-    squares = jnp.sum(jnp.sum(mixed * mixed, axis=0), axis=1, keepdims=True)
-    scale = lax.rsqrt(squares / (blocks * LANES) + 1e-05)
-    normed = (mixed * scale[None] * gain[...].astype(jnp.float32)).astype(jnp.bfloat16)
+    tiles = swapped(gathered[...].astype(jnp.float32), share)
+    mixed = jnp.concatenate([tiles[k] for k in range(blocks)], axis=1)
+    scale = lax.rsqrt(jnp.sum(mixed * mixed, axis=1, keepdims=True) / (blocks * LANES) + 1e-05)
+    normed = (mixed * scale * gain[...].astype(jnp.float32).reshape(1, blocks * LANES)).astype(jnp.bfloat16)
     plain = normed.astype(jnp.float32)
+    weights = router[...].astype(jnp.float32)
     logits = [
+        jnp.sum(plain * weights[e : e + 1], axis=1, keepdims=True) for e in range(EXPERTS)
+    ]
+    upright = lax.broadcasted_iota(jnp.int32, (slots, slots), 0) == lax.broadcasted_iota(
+        jnp.int32, (slots, slots), 1
+    )
+    ids = [
         jnp.sum(
-            jnp.sum(plain * router[e].astype(jnp.float32), axis=0), axis=1, keepdims=True
+            jnp.where(upright, chosen[i : i + 1, :].astype(jnp.float32), 0.0),
+            axis=1,
+            keepdims=True,
         )
-        for e in range(EXPERTS)
-    ]
-    ids = [chosen[:, i : i + 1] for i in range(2)]
+        for i in range(2)
+    ]
     picked = [sum(jnp.where(k == e, logits[e], 0.0) for e in range(EXPERTS)) for k in ids]
     gates = [jax.nn.sigmoid(picked[i] - picked[1 - i]) for i in range(2)]
-    part = sum(jnp.where(ids[i] == expert[0], gates[i], 0.0) for i in range(2))
-    line = jnp.concatenate([normed[k] for k in range(blocks)], axis=1)
-    gate = jnp.dot(line, gate_up[0], preferred_element_type=jnp.float32)
-    up = jnp.dot(line, gate_up[1], preferred_element_type=jnp.float32)
+    mine = expert[0].astype(jnp.float32)
+    part = sum(jnp.where(ids[i] == mine, gates[i], 0.0) for i in range(2))
+    gate, up = [
+        lax.dot_general(
+            normed, gate_up[i], (((1,), (1,)), ((), ())), preferred_element_type=jnp.float32
+        )
+        for i in range(2)
+    ]
     act = (gate * jax.nn.sigmoid(gate) * up).astype(jnp.bfloat16)
     term = part * jnp.dot(act, down[...], preferred_element_type=jnp.float32)
     tiles = [term[None, :, k * LANES : (k + 1) * LANES] for k in range(blocks)]
@@ -192,25 +253,29 @@
     dev_index = lax.axis_index(BLK)
     slots, columns = hidden.shape
     ctx_rows, kv_width = cache_kv.shape[2:]
+    prefixes = insert_slot.shape[0]
     share = LANES // columns
     width = devices * columns
     blocks = width // LANES
     bf16 = jnp.bfloat16
 
-    positions = devices * ctx_rows
-    here = dev_index * ctx_rows
-    first = jnp.stack([here, (here + positions // 2) % positions]).astype(jnp.int32)
+    first = (dev_index * ctx_rows).astype(jnp.int32).reshape(1)
     partials = pl.pallas_call(
-        attention_kernel,
+        functools.partial(attention_kernel, devices * ctx_rows),
         out_shape=jax.ShapeDtypeStruct((slots, 2 * QUERY_HEADS, HEAD_SIZE), bf16),
-        in_specs=[IN_SMEM] * 4 + [IN_VMEM, ANYWHERE, ANYWHERE],
+        in_specs=[IN_SMEM] + [IN_HBM] * 6,
         out_specs=IN_VMEM,
         scratch_shapes=[
+            pltpu.SMEM((slots,), jnp.int32),
+            pltpu.SMEM((prefixes,), jnp.int32),
+            pltpu.SMEM((prefixes,), jnp.int32),
+            pltpu.VMEM(queries.shape, bf16),
             pltpu.VMEM((slots * 2 * QUERY_HEADS, HEAD_SIZE), jnp.float32),
-            pltpu.VMEM((slots, 2, ctx_rows, kv_width), bf16),
-            pltpu.SemaphoreType.DMA((slots,)),
+            pltpu.VMEM((slots + prefixes, 2, ctx_rows, kv_width), bf16),
+            pltpu.VMEM((slots, 2 * QUERY_HEADS, ctx_rows), jnp.float32),
+            pltpu.SemaphoreType.DMA((4 + 2 * (slots + prefixes),)),
         ],
-        compiler_params=params(12),
+        compiler_params=pltpu.CompilerParams(vmem_limit_bytes=ALL_VMEM),
         name="attention",
     )(first, cache_len, insert_slot, prefix_len, queries, cache_kv, inserted_key_value)
     pieces = exchanged(partials.reshape(slots * KEY_VALUE_HEADS, 2 * GROUP, HEAD_SIZE))
@@ -221,6 +286,7 @@
         in_specs=[IN_VMEM],
         out_specs=IN_VMEM,
         compiler_params=params(8),
+        cost_estimate=COVER,
         name="combine",
     )(pieces)
     attn = exchanged(own).reshape(slots * QUERY_HEADS, HEAD_SIZE)
@@ -235,8 +301,9 @@
         out_specs=(IN_VMEM, IN_VMEM),
         scratch_shapes=[pltpu.VMEM((slots * QUERY_HEADS, HEAD_SIZE), jnp.float32)],
         compiler_params=params(8),
+        cost_estimate=COVER,
         name="project",
-    )(attn, out_weight, hidden)
+    )(attn, out_weight.T, hidden)
     gathered = exchanged(packed).reshape(blocks, slots, LANES)
 
     expert = (dev_index * gate_up.shape[2] // FF).astype(jnp.int32).reshape(1)
@@ -250,10 +317,10 @@
     )(
         expert,
         gathered,
-        norm_gain.reshape(blocks, 1, LANES),
-        router_weight.T.reshape(EXPERTS, blocks, 1, LANES),
-        expert_ids,
-        gate_up,
+        norm_gain,
+        router_weight.T,
+        expert_ids.T,
+        jnp.swapaxes(gate_up, 1, 2),
         down_proj,
     )
     moe = exchanged(terms.reshape(devices, slots // share, LANES))

time: 127 us -> 112 us (0.88)
  blocking collectives: 63.8 us -> 81.1 us
  local copies, waits for them, and re-layouts: 14.9 us -> 2.07 us
  starting transfers between devices: 15.3 us -> 7.6 us
  Pallas kernels: 14.5 us -> 8.35 us
  waiting for transfers between devices: 17.7 us -> 12.4 us
    all_to_all x2 -> x3, blocking collectives: 63.8 us -> 81.1 us  [exchanged(): return lax.all_to_all(pieces, BLK, 0, 0, tiled=True)]
    unnamed x29 -> x14, local copies, waits for them, and re-layouts: 14.8 us -> 2.07 us
    all_to_all x2 -> x1, starting transfers between devices: 15.3 us -> 7.6 us  [exchanged(): return lax.all_to_all(pieces, BLK, 0, 0, tiled=True)]
    pallas_call x1, Pallas kernels: 10.2 us -> 4.35 us  [on_device(): pl.pallas_call(functools.partial(attention_kernel, devices * ctx_rows), o...]
    all_to_all x2 -> x1, waiting for transfers between devices: 17.7 us -> 12.4 us  [exchanged(): return lax.all_to_all(pieces, BLK, 0, 0, tiled=True)]
  transfers between devices with their start and end apart: 2 -> 1, of which waited for: 2 -> 1; matrix products, arithmetic and copies ran while one was open for 6% -> 0% of each run, Pallas kernels for 0% -> 0%
where the time goes in v3:
time: 112 us
  blocking collectives  81.1 us (72%)
  waiting for transfers between devices  12.4 us (11%)
  Pallas kernels  8.35 us (7%)
  starting transfers between devices  7.6 us (7%)
  local copies, waits for them, and re-layouts  2.07 us (2%)
    all_to_all x3, blocking collectives, exchanged(): return lax.all_to_all(pieces, BLK, 0, 0, tiled=True)  81.1 us
    all_to_all x1, waiting for transfers between devices, exchanged(): return lax.all_to_all(pieces, BLK, 0, 0, tiled=True)  12.4 us
    all_to_all x1, starting transfers between devices, exchanged(): return lax.all_to_all(pieces, BLK, 0, 0, tiled=True)  7.6 us
    pallas_call x1, Pallas kernels, on_device(): pl.pallas_call(functools.partial(attention_kernel, devices * ctx_rows), o...  4.35 us
  transfers between devices with their start and end apart: 1, of which 1 were waited for; matrix products, arithmetic and copies ran while one was open for 0% of the time, Pallas kernels for 0%

profile of v3, /device:TPU:513, one launch (start us, length us, event | category | flops | bytes accessed | tf_op | source)
XLA Modules:
  0.0 111.6 jit_solution(15188328008250939590)
XLA Ops:
  0.0 4.3 %attention.1 = bf16[16,64,128]{2,1,0:T(8,128)(2,1)} custom-call(s32[1]{0:T(128)} %bitcast.1.first, s32[16]{0:T(128)} %lengths_in.1, s32[8]{0:T(128)} %insert_slot_in.1, s32[8]{0:T(128)} %prefix_len_in.1, bf16[16,4096]{1,0:T(8,128)(2,1)} %queries_in.1, bf16[2,16,32,1024]{3,2,1,0:T(8,128)(2,1)} %cache.1, bf16[2,8,32,1024]{3,2,1,0:T(8,128)(2,1)} %inserted.1), custom_call_target="tpu_custom_call" | custom-call | tf_op jit(solution)/shard_map/attention/pallas_call | solution.py:263
  4.4 0.0 copy-start.5
  4.4 0.0 copy-start.6
  4.4 42.1 %all_to_all.20.pieces = bf16[128,8,128]{2,1,0:T(8,128)(2,1)S(1)} all-to-all(bf16[128,8,128]{2,1,0:T(8,128)(2,1)} %bitcast.17), channel_id=1, replica_groups=mesh['rep'=2,'blk_0'=8,'blk_1'=8,'blk_2'=2] {'blk_0','blk_1','blk_2'}, dimensions={0} | all-to-all | bytes 524288 | tf_op jit(solution)/shard_map/all_to_all | solution.py:30
  46.5 0.4 combine.1
  46.9 0.0 copy-start.1
  46.9 0.0 copy-start.2
  46.9 0.0 copy-start.3
  47.0 0.0 copy-start.4
  47.0 19.7 %all_to_all.21 = bf16[128,4,128]{2,1,0:T(4,128)(2,1)S(1)} all-to-all(bf16[128,4,128]{2,1,0:T(4,128)(2,1)S(1)} %combine.1), channel_id=1, replica_groups=mesh['rep'=2,'blk_0'=8,'blk_1'=8,'blk_2'=2] {'blk_0','blk_1','blk_2'}, dimensions={0} | all-to-all | bytes 262144 | tf_op jit(solution)/shard_map/all_to_all | solution.py:30
  66.6 0.0 copy-done.5
  66.6 0.0 copy-done.6
  66.6 1.0 project.1
  67.7 7.6 %all-to-all-start.2 = ((bf16[128,4,128]{2,1,0:T(4,128)(2,1)}), bf16[128,4,128]{2,1,0:T(4,128)(2,1)S(1)}, u32[]{:S(2)}, u32[]{:S(2)}) async-start(bf16[128,4,128]{2,1,0:T(4,128)(2,1)} %get-tuple-element.7), calls=%async_computation.2 | async-start | bytes 262144 | tf_op jit(solution)/shard_map/all_to_all | solution.py:30
  75.3 12.4 %all-to-all-done.2 = bf16[128,4,128]{2,1,0:T(4,128)(2,1)S(1)} async-done(((bf16[128,4,128]{2,1,0:T(4,128)(2,1)}), bf16[128,4,128]{2,1,0:T(4,128)(2,1)S(1)}, u32[]{:S(2)}, u32[]{:S(2)}) %all-to-all-start.2) | async-done | bytes 131104 | tf_op jit(solution)/shard_map/all_to_all | solution.py:30
  87.7 0.0 copy-done.1
  87.7 0.0 copy-done.2
  87.7 0.0 copy-done.3
  87.7 0.0 copy-done.4
  87.7 0.0 copy-start
  87.7 2.0 %copy-done = bf16[2,4096,224]{1,2,0:T(8,128)(2,1)S(1)} copy-done((bf16[2,4096,224]{1,2,0:T(8,128)(2,1)S(1)}, bf16[2,4096,224]{1,2,0:T(8,128)(2,1)}, u32[]{:S(2)}) %copy-start) | copy-done | bytes 3670040
  89.7 1.8 %experts.1 = bf16[32,16,128]{2,1,0:T(8,128)(2,1)S(1)} custom-call(s32[1]{0:T(128)} %bitcast.expert, bf16[32,16,128]{2,1,0:T(8,128)(2,1)S(1)} %bitcast.11, bf16[4096]{0:T(1024)(128)(2,1)S(1)} %copy-done.3, bf16[4,4096]{1,0:T(4,128)(2,1)S(1)} %bitcast.14, s32[2,16]{1,0:T(2,128)S(1)} %bitcast.15, bf16[2,224,4096]{2,1,0:T(8,128)(2,1)S(1)} %bitcast.10, ...), custom_call_target="tpu_custom_call" | custom-call | tf_op jit(solution)/shard_map/experts/pallas_call | solution.py:310
  91.5 19.3 %all_to_all.22.pieces = bf16[128,4,128]{2,1,0:T(4,128)(2,1)S(1)} all-to-all(bf16[128,4,128]{2,1,0:T(4,128)(2,1)S(1)} %bitcast.12), channel_id=1, replica_groups=mesh['rep'=2,'blk_0'=8,'blk_1'=8,'blk_2'=2] {'blk_0','blk_1','blk_2'}, dimensions={0} | all-to-all | bytes 262144 | tf_op jit(solution)/shard_map/all_to_all | solution.py:30
  110.8 0.8 final.1
Async XLA Ops:
  4.4 62.3 %copy-start.5 = (bf16[4096,32]{0,1:T(8,128)(2,1)S(1)}, bf16[4096,32]{0,1:T(8,128)(2,1)}, u32[]{:S(2)}) copy-start(bf16[4096,32]{0,1:T(8,128)(2,1)} %param.20) | copy-start | bytes 786436
  4.4 62.3 %copy-start.6 = (bf16[16,32]{1,0:T(8,128)(2,1)S(1)}, bf16[16,32]{1,0:T(8,128)(2,1)}, u32[]{:S(2)}) copy-start(bf16[16,32]{1,0:T(8,128)(2,1)} %hidden.1) | copy-start | bytes 3076
  46.9 40.8 %copy-start.1 = (bf16[224,4096]{1,0:T(8,128)(2,1)S(1)}, bf16[224,4096]{1,0:T(8,128)(2,1)}, u32[]{:S(2)}) copy-start(bf16[224,4096]{1,0:T(8,128)(2,1)} %down.1) | copy-start | bytes 5505028
  46.9 40.8 %copy-start.2 = (bf16[4096,4]{0,1:T(4,128)(2,1)S(1)}, bf16[4096,4]{0,1:T(4,128)(2,1)}, u32[]{:S(2)}) copy-start(bf16[4096,4]{0,1:T(4,128)(2,1)} %param.22) | copy-start | bytes 98308
  46.9 40.8 %copy-start.3 = (bf16[4096]{0:T(1024)(128)(2,1)S(1)}, bf16[4096]{0:T(1024)(128)(2,1)}, u32[]{:S(2)}) copy-start(bf16[4096]{0:T(1024)(128)(2,1)} %gain.1) | copy-start | bytes 24580
  47.0 40.7 %copy-start.4 = (s32[16,2]{0,1:T(2,128)S(1)}, s32[16,2]{0,1:T(2,128)}, u32[]{:S(2)}) copy-start(s32[16,2]{0,1:T(2,128)} %param.23) | copy-start | bytes 388
  67.7 20.0 %all-to-all-start.2 = ((bf16[128,4,128]{2,1,0:T(4,128)(2,1)}), bf16[128,4,128]{2,1,0:T(4,128)(2,1)S(1)}, u32[]{:S(2)}, u32[]{:S(2)}) async-start(bf16[128,4,128]{2,1,0:T(4,128)(2,1)} %get-tuple-element.7), calls=%async_computation.2 | async-start | bytes 262144 | tf_op jit(solution)/shard_map/all_to_all | solution.py:30
  87.7 2.0 %copy-start = (bf16[2,4096,224]{1,2,0:T(8,128)(2,1)S(1)}, bf16[2,4096,224]{1,2,0:T(8,128)(2,1)}, u32[]{:S(2)}) copy-start(bf16[2,4096,224]{1,2,0:T(8,128)(2,1)} %param.24) | copy-start | bytes 11010052

commit v4 on v3

--- a/solution.py
+++ b/solution.py
@@ -17,6 +17,7 @@
 BLK = ("blk_0", "blk_1", "blk_2")
 GROUP = QUERY_HEADS // KEY_VALUE_HEADS
 LANES = 128
+SPAN = LANES // GROUP
 IN_VMEM = pl.BlockSpec(memory_space=pltpu.VMEM)
 IN_SMEM = pl.BlockSpec(memory_space=pltpu.SMEM)
 IN_HBM = pl.BlockSpec(memory_space=pltpu.HBM)
@@ -26,8 +27,20 @@
 ALL_VMEM = 67043328
 
 
-def exchanged(pieces):
-    return lax.all_to_all(pieces, BLK, 0, 0, tiled=True)
+def exchanged(pieces, axis=BLK):
+    return lax.all_to_all(pieces, axis, 0, 0, tiled=True)
+
+
+def merging(kernel, shape, *pieces):
+    return pl.pallas_call(
+        kernel,
+        out_shape=jax.ShapeDtypeStruct(shape, jnp.bfloat16),
+        in_specs=[IN_VMEM] * len(pieces),
+        out_specs=IN_VMEM,
+        compiler_params=params(8),
+        cost_estimate=COVER,
+        name=kernel.__name__,
+    )(*pieces)
 
 
 def params(mib):
@@ -51,10 +64,12 @@
     spread,
     rows,
     score_of,
+    values,
+    stats,
     sems,
 ):
     slots, prefixes, count = lengths.shape[0], insert_slot.shape[0], rows.shape[2]
-    wide = 2 * QUERY_HEADS
+    wide = QUERY_HEADS
     copies = [
         pltpu.make_async_copy(lengths_in, lengths, sems.at[0]),
         pltpu.make_async_copy(insert_slot_in, insert_slot, sems.at[1]),
@@ -81,8 +96,7 @@
         for h in range(GROUP):
             at = (g * GROUP + h) * HEAD_SIZE
             one = queries[:, at : at + HEAD_SIZE].astype(jnp.float32)
-            for twin in range(2):
-                spread[pl.ds(g * 2 * GROUP + twin * GROUP + h, slots, stride=wide), :] = one
+            spread[pl.ds(g * GROUP + h, slots, stride=wide), :] = one
     here = first[0]
     half = positions // 2
     there = jnp.where(here < half, here + half, here - half)
@@ -100,11 +114,13 @@
         copy.wait()
     shape = (wide, KEY_VALUE_HEADS * HEAD_SIZE)
     own = (
-        lax.broadcasted_iota(jnp.int32, shape, 0) // (2 * GROUP)
+        lax.broadcasted_iota(jnp.int32, shape, 0) // GROUP
         == lax.broadcasted_iota(jnp.int32, shape, 1) // HEAD_SIZE
     )
-    is_value = lax.broadcasted_iota(jnp.int32, (wide, HEAD_SIZE), 0) % (2 * GROUP) < GROUP
-    is_peak = lax.broadcasted_iota(jnp.int32, (wide, HEAD_SIZE), 1) < HEAD_SIZE // 2
+    row = lax.broadcasted_iota(jnp.int32, (wide, HEAD_SIZE), 0)
+    lane = lax.broadcasted_iota(jnp.int32, (wide, HEAD_SIZE), 1)
+    counted = lane // SPAN == row % GROUP
+    early = lax.broadcasted_iota(jnp.int32, (2 * GROUP, HEAD_SIZE), 0) < GROUP
     place = lax.broadcasted_iota(jnp.int32, (wide, count), 1)
     for s in range(slots):
         one = spread[s * wide : (s + 1) * wide, :]
@@ -135,34 +151,97 @@
         for s, full, peak, total in zip(several, every, peaks, totals):
             value = jnp.concatenate(
                 [
-                    full[g * 2 * GROUP : (g + 1) * 2 * GROUP, g * HEAD_SIZE : (g + 1) * HEAD_SIZE]
-                    for g in range(KEY_VALUE_HEADS)
+                    jnp.where(
+                        early,
+                        full[g * GROUP : (g + 2) * GROUP, g * HEAD_SIZE : (g + 1) * HEAD_SIZE],
+                        full[
+                            g * GROUP : (g + 2) * GROUP, (g + 1) * HEAD_SIZE : (g + 2) * HEAD_SIZE
+                        ],
+                    )
+                    for g in range(0, KEY_VALUE_HEADS, 2)
                 ],
                 axis=0,
             )
-            value = value / jnp.where(total > 0.0, total, 1.0)
-            result = jnp.where(is_value, value, jnp.where(is_peak, peak, total))
-            out[s] = result.astype(jnp.bfloat16)
-
-
-def combine_kernel(pieces, out):
-    shape = pieces.shape[1:]
-    left = lax.broadcasted_iota(jnp.int32, shape, 1) < HEAD_SIZE // 2
-    half = HEAD_SIZE // 2
-    found = pieces[...].astype(jnp.float32)
-    highest = jnp.max(found, axis=0, keepdims=True)
-    scale = jnp.exp(found - highest) * pltpu.roll(found, half, axis=2)
-    scale = jnp.where(left[None], scale, pltpu.roll(scale, half, axis=2))
-    scale = pltpu.roll(scale, GROUP, axis=1)
-    value = jnp.sum(found * scale, axis=0) / jnp.sum(scale, axis=0)
-    out[...] = jnp.broadcast_to(value[None, :GROUP].astype(jnp.bfloat16), out.shape)
-
-
-def project_kernel(attn, weight, hidden, mixed, packed, spread):
+            values[pl.ds(s, wide, stride=slots), :] = value / jnp.where(total > 0.0, total, 1.0)
+            stats[pl.ds(s, wide, stride=slots), :] = jnp.where(
+                counted, packed_stats(lane, peak, total), 0.0
+            )
+    deep = GROUP * slots
+    for g in range(KEY_VALUE_HEADS):
+        out[g, :deep, :] = values[g * deep : (g + 1) * deep, :].astype(jnp.bfloat16)
+        one = [stats[g * deep + h * slots : g * deep + (h + 1) * slots, :] for h in range(GROUP)]
+        out[g, deep:, :] = sum(one).astype(jnp.bfloat16)
+
+
+def packed_stats(lane, peak, total):
+    rounded = total.astype(jnp.bfloat16).astype(jnp.float32)
+    at = lane % SPAN
+    return jnp.where(
+        at < SPAN // 2, peak, jnp.where(at < SPAN * 3 // 4, rounded, total - rounded)
+    )
+
+
+def merge(pieces):
+    slots = pieces[0].shape[0] // (GROUP + 1)
+    found = [x[GROUP * slots :].astype(jnp.float32) for x in pieces]
+    highest = functools.reduce(jnp.maximum, found)
+    scales = [
+        jnp.exp(x - highest)
+        * (
+            pltpu.roll(x, LANES - SPAN // 2, axis=1)
+            + pltpu.roll(x, LANES - SPAN * 3 // 4, axis=1)
+        )
+        for x in found
+    ]
+    total = sum(scales)
+    safe = jnp.where(total > 0.0, total, 1.0)
+    values = []
+    for h in range(GROUP):
+        column = slice(h * SPAN, h * SPAN + 1)
+        parts = [
+            x[h * slots : (h + 1) * slots].astype(jnp.float32) * y[:, column]
+            for x, y in zip(pieces, scales)
+        ]
+        values.append(sum(parts) / safe[:, column])
+    return values, highest, total
+
+
+def whole_part(pieces):
+    values, highest, total = merge(pieces)
+    lane = lax.broadcasted_iota(jnp.int32, highest.shape, 1)
+    total = pltpu.roll(total, SPAN // 2, axis=1)
+    rounded = total.astype(jnp.bfloat16).astype(jnp.float32)
+    rest = pltpu.roll(total - rounded, SPAN // 4, axis=1)
+    at = lane % SPAN
+    stats = jnp.where(at < SPAN // 2, highest, jnp.where(at < SPAN * 3 // 4, rounded, rest))
+    return jnp.concatenate(values + [stats], axis=0).astype(jnp.bfloat16)
+
+
+def spread_kernel(pieces, out):
+    part = whole_part([pieces[i] for i in range(pieces.shape[0])])
+    for i in range(out.shape[0]):
+        out[i] = part
+
+
+def part_kernel(pieces, out):
+    out[...] = whole_part([pieces[i] for i in range(pieces.shape[0])])
+
+
+def pair_kernel(mine, other, out):
+    values, _, _ = merge([mine[...], other[...]])
+    part = jnp.concatenate(values, axis=0).astype(jnp.bfloat16)
+    for i in range(out.shape[0]):
+        out[i] = part
+
+
+def project_kernel(attn, weight, hidden, mixed, packed):
     slots, columns = hidden.shape
-    spread[...] = attn[...].astype(jnp.float32)
-    blocks = [spread[pl.ds(k, slots, stride=QUERY_HEADS), :] for k in range(QUERY_HEADS)]
-    whole = jnp.concatenate(blocks, axis=1).astype(jnp.bfloat16)
+    blocks = [
+        attn[g, h * slots : (h + 1) * slots, :]
+        for g in range(KEY_VALUE_HEADS)
+        for h in range(GROUP)
+    ]
+    whole = jnp.concatenate(blocks, axis=1)
     total = hidden[...].astype(jnp.float32) + lax.dot_general(
         whole, weight[...], (((1,), (1,)), ((), ())), preferred_element_type=jnp.float32
     )
@@ -255,6 +334,7 @@
     ctx_rows, kv_width = cache_kv.shape[2:]
     prefixes = insert_slot.shape[0]
     share = LANES // columns
+    deep = slots * (GROUP + 1)
     width = devices * columns
     blocks = width // LANES
     bf16 = jnp.bfloat16
@@ -262,7 +342,7 @@
     first = (dev_index * ctx_rows).astype(jnp.int32).reshape(1)
     partials = pl.pallas_call(
         functools.partial(attention_kernel, devices * ctx_rows),
-        out_shape=jax.ShapeDtypeStruct((slots, 2 * QUERY_HEADS, HEAD_SIZE), bf16),
+        out_shape=jax.ShapeDtypeStruct((KEY_VALUE_HEADS, deep, HEAD_SIZE), bf16),
         in_specs=[IN_SMEM] + [IN_HBM] * 6,
         out_specs=IN_VMEM,
         scratch_shapes=[
@@ -270,26 +350,23 @@
             pltpu.SMEM((prefixes,), jnp.int32),
             pltpu.SMEM((prefixes,), jnp.int32),
             pltpu.VMEM(queries.shape, bf16),
-            pltpu.VMEM((slots * 2 * QUERY_HEADS, HEAD_SIZE), jnp.float32),
+            pltpu.VMEM((slots * QUERY_HEADS, HEAD_SIZE), jnp.float32),
             pltpu.VMEM((slots + prefixes, 2, ctx_rows, kv_width), bf16),
-            pltpu.VMEM((slots, 2 * QUERY_HEADS, ctx_rows), jnp.float32),
+            pltpu.VMEM((slots, QUERY_HEADS, ctx_rows), jnp.float32),
+            pltpu.VMEM((slots * QUERY_HEADS, HEAD_SIZE), jnp.float32),
+            pltpu.VMEM((slots * QUERY_HEADS, HEAD_SIZE), jnp.float32),
             pltpu.SemaphoreType.DMA((4 + 2 * (slots + prefixes),)),
         ],
         compiler_params=pltpu.CompilerParams(vmem_limit_bytes=ALL_VMEM),
         name="attention",
     )(first, cache_len, insert_slot, prefix_len, queries, cache_kv, inserted_key_value)
-    pieces = exchanged(partials.reshape(slots * KEY_VALUE_HEADS, 2 * GROUP, HEAD_SIZE))
-
-    own = pl.pallas_call(
-        combine_kernel,
-        out_shape=jax.ShapeDtypeStruct((devices, GROUP, HEAD_SIZE), bf16),
-        in_specs=[IN_VMEM],
-        out_specs=IN_VMEM,
-        compiler_params=params(8),
-        cost_estimate=COVER,
-        name="combine",
-    )(pieces)
-    attn = exchanged(own).reshape(slots * QUERY_HEADS, HEAD_SIZE)
+    along, across, pair = BLK
+    copies = lax.axis_size(across)
+    part = merging(spread_kernel, (copies, deep, HEAD_SIZE), exchanged(partials, along))
+    part = merging(part_kernel, (deep, HEAD_SIZE), exchanged(part, across))
+    other = lax.ppermute(part, pair, [(0, 1), (1, 0)])
+    own = merging(pair_kernel, (KEY_VALUE_HEADS, slots * GROUP, HEAD_SIZE), part, other)
+    attn = exchanged(own, along)
 
     local_mixed, packed = pl.pallas_call(
         project_kernel,
@@ -299,7 +376,6 @@
         ),
         in_specs=[IN_VMEM] * 3,
         out_specs=(IN_VMEM, IN_VMEM),
-        scratch_shapes=[pltpu.VMEM((slots * QUERY_HEADS, HEAD_SIZE), jnp.float32)],
         compiler_params=params(8),
         cost_estimate=COVER,
         name="project",

time: 112 us -> 108 us (0.964)
  blocking collectives: 81.1 us -> 67.5 us
  starting transfers between devices: 7.6 us -> 16.6 us
    all_to_all x3 -> x4, blocking collectives: 81.1 us -> 67.5 us  [exchanged(): return lax.all_to_all(pieces, axis, 0, 0, tiled=True)]
    ppermute x0 -> x1, starting transfers between devices: none -> 7.97 us  [on_device(): other = lax.ppermute(part, pair, [(0, 1), (1, 0)])]
  transfers between devices with their start and end apart: 1 -> 2, of which waited for: 1 -> 2; matrix products, arithmetic and copies ran while one was open for 0% -> 0% of each run, Pallas kernels for 0% -> 0%
where the time goes in v4:
time: 108 us
  blocking collectives  67.5 us (62%)
  starting transfers between devices  16.6 us (15%)
  waiting for transfers between devices  13.2 us (12%)
  Pallas kernels  8.1 us (8%)
  local copies, waits for them, and re-layouts  2.07 us (2%)
    all_to_all x4, blocking collectives, exchanged(): return lax.all_to_all(pieces, axis, 0, 0, tiled=True)  67.5 us
    all_to_all x1, waiting for transfers between devices, exchanged(): return lax.all_to_all(pieces, axis, 0, 0, tiled=True)  12.4 us
    all_to_all x1, starting transfers between devices, exchanged(): return lax.all_to_all(pieces, axis, 0, 0, tiled=True)  8.59 us
    ppermute x1, starting transfers between devices, on_device(): other = lax.ppermute(part, pair, [(0, 1), (1, 0)])  7.97 us
    pallas_call x1, Pallas kernels, on_device(): pl.pallas_call(functools.partial(attention_kernel, devices * ctx_rows), o...  3.88 us
  transfers between devices with their start and end apart: 2, of which 2 were waited for; matrix products, arithmetic and copies ran while one was open for 0% of the time, Pallas kernels for 0%

profile of v4, /device:TPU:513, one launch (start us, length us, event | category | flops | bytes accessed | tf_op | source)
XLA Modules:
  0.0 107.5 jit_solution(18166924984905083636)
XLA Ops:
  0.0 3.9 %attention.1 = bf16[8,80,128]{2,1,0:T(8,128)(2,1)} custom-call(s32[1]{0:T(128)} %bitcast.1.first, s32[16]{0:T(128)} %lengths_in.1, s32[8]{0:T(128)} %insert_slot_in.1, s32[8]{0:T(128)} %prefix_len_in.1, bf16[16,4096]{1,0:T(8,128)(2,1)} %queries_in.1, bf16[2,16,32,1024]{3,2,1,0:T(8,128)(2,1)} %cache.1, bf16[2,8,32,1024]{3,2,1,0:T(8,128)(2,1)} %inserted.1), custom_call_target="tpu_custom_call" | custom-call | tf_op jit(solution)/shard_map/attention/pallas_call | solution.py:343
  3.9 16.1 %all_to_all.25.pieces = bf16[8,80,128]{2,1,0:T(8,128)(2,1)S(1)} all-to-all(bf16[8,80,128]{2,1,0:T(8,128)(2,1)} %attention.1), channel_id=1, replica_groups=mesh['rep'=2,'blk_0'=8,'blk_1'=8,'blk_2'=2] {'blk_0'}, dimensions={0} | all-to-all | bytes 327680 | tf_op jit(solution)/shard_map/all_to_all | solution.py:31
  20.0 0.3 spread_kernel.1
  20.3 21.0 %all_to_all.26.pieces = bf16[8,80,128]{2,1,0:T(8,128)(2,1)S(1)} all-to-all(bf16[8,80,128]{2,1,0:T(8,128)(2,1)S(1)} %spread_kernel.1), channel_id=1, replica_groups=mesh['rep'=2,'blk_0'=8,'blk_1'=8,'blk_2'=2] {'blk_1'}, dimensions={0} | all-to-all | bytes 327680 | tf_op jit(solution)/shard_map/all_to_all | solution.py:31
  41.3 0.3 part_kernel.1.mine
  41.6 0.0 copy-start.5
  41.6 0.0 copy-start.6
  41.6 8.0 %collective-permute-start = (bf16[80,128]{1,0:T(8,128)(2,1)S(1)}, bf16[80,128]{1,0:T(8,128)(2,1)S(1)}, u32[]{:S(2)}, u32[]{:S(2)}) collective-permute-start(bf16[80,128]{1,0:T(8,128)(2,1)S(1)} %part_kernel.1.mine), channel_id=1, source_target_pairs={{0,1},{1,0},{2,3},{3,2},{4,5},{5,4},{6,7},{7,6},{8,9},{9,8},{10,11... | collective-permute-start | bytes 61448 | tf_op jit(solution)/shard_map/ppermute | solution.py:367
  49.6 0.8 collective-permute-done.other
  50.4 0.2 pair_kernel.1
  50.6 0.0 copy-start.1
  50.6 0.0 copy-start.2
  50.6 0.0 copy-start.3
  50.6 0.0 copy-start.4
  50.6 11.0 %all_to_all.27.attn = bf16[8,64,128]{2,1,0:T(8,128)(2,1)S(1)} all-to-all(bf16[8,64,128]{2,1,0:T(8,128)(2,1)S(1)} %pair_kernel.1), channel_id=1, replica_groups=mesh['rep'=2,'blk_0'=8,'blk_1'=8,'blk_2'=2] {'blk_0'}, dimensions={0} | all-to-all | bytes 262144 | tf_op jit(solution)/shard_map/all_to_all | solution.py:31
  61.6 0.0 copy-done.5
  61.6 0.0 copy-done.6
  61.6 0.9 project.1
  62.6 8.6 %all-to-all-start.3 = ((bf16[128,4,128]{2,1,0:T(4,128)(2,1)}), bf16[128,4,128]{2,1,0:T(4,128)(2,1)S(1)}, u32[]{:S(2)}, u32[]{:S(2)}) async-start(bf16[128,4,128]{2,1,0:T(4,128)(2,1)} %get-tuple-element.7), calls=%async_computation.3 | async-start | bytes 262144 | tf_op jit(solution)/shard_map/all_to_all | solution.py:31
  71.2 12.4 %all-to-all-done.3 = bf16[128,4,128]{2,1,0:T(4,128)(2,1)S(1)} async-done(((bf16[128,4,128]{2,1,0:T(4,128)(2,1)}), bf16[128,4,128]{2,1,0:T(4,128)(2,1)S(1)}, u32[]{:S(2)}, u32[]{:S(2)}) %all-to-all-start.3) | async-done | bytes 131104 | tf_op jit(solution)/shard_map/all_to_all | solution.py:31
  83.6 0.0 copy-done.1
  83.6 0.0 copy-done.2
  83.6 0.0 copy-done.3
  83.6 0.0 copy-done.4
  83.6 0.0 copy-start
  83.6 2.0 %copy-done = bf16[2,4096,224]{1,2,0:T(8,128)(2,1)S(1)} copy-done((bf16[2,4096,224]{1,2,0:T(8,128)(2,1)S(1)}, bf16[2,4096,224]{1,2,0:T(8,128)(2,1)}, u32[]{:S(2)}) %copy-start) | copy-done | bytes 3670040
  85.6 1.8 %experts.1 = bf16[32,16,128]{2,1,0:T(8,128)(2,1)S(1)} custom-call(s32[1]{0:T(128)} %bitcast.expert, bf16[32,16,128]{2,1,0:T(8,128)(2,1)S(1)} %bitcast.9, bf16[4096]{0:T(1024)(128)(2,1)S(1)} %copy-done.3, bf16[4,4096]{1,0:T(4,128)(2,1)S(1)} %bitcast.11, s32[2,16]{1,0:T(2,128)S(1)} %bitcast.12, bf16[2,224,4096]{2,1,0:T(8,128)(2,1)S(1)} %bitcast.8, ...), custom_call_target="tpu_custom_call" | custom-call | tf_op jit(solution)/shard_map/experts/pallas_call | solution.py:386
  87.4 19.3 %all_to_all.28.pieces = bf16[128,4,128]{2,1,0:T(4,128)(2,1)S(1)} all-to-all(bf16[128,4,128]{2,1,0:T(4,128)(2,1)S(1)} %bitcast.10), channel_id=1, replica_groups=mesh['rep'=2,'blk_0'=8,'blk_1'=8,'blk_2'=2] {'blk_0','blk_1','blk_2'}, dimensions={0} | all-to-all | bytes 262144 | tf_op jit(solution)/shard_map/all_to_all | solution.py:31
  106.7 0.8 final.1
Async XLA Ops:
  41.6 20.0 %copy-start.5 = (bf16[4096,32]{0,1:T(8,128)(2,1)S(1)}, bf16[4096,32]{0,1:T(8,128)(2,1)}, u32[]{:S(2)}) copy-start(bf16[4096,32]{0,1:T(8,128)(2,1)} %param.20) | copy-start | bytes 786436
  41.6 20.0 %copy-start.6 = (bf16[16,32]{1,0:T(8,128)(2,1)S(1)}, bf16[16,32]{1,0:T(8,128)(2,1)}, u32[]{:S(2)}) copy-start(bf16[16,32]{1,0:T(8,128)(2,1)} %hidden.1) | copy-start | bytes 3076
  41.6 8.8 %collective-permute-start = (bf16[80,128]{1,0:T(8,128)(2,1)S(1)}, bf16[80,128]{1,0:T(8,128)(2,1)S(1)}, u32[]{:S(2)}, u32[]{:S(2)}) collective-permute-start(bf16[80,128]{1,0:T(8,128)(2,1)S(1)} %part_kernel.1.mine), channel_id=1, source_target_pairs={{0,1},{1,0},{2,3},{3,2},{4,5},{5,4},{6,7},{7,6},{8,9},{9,8},{10,11... | collective-permute-start | bytes 61448 | tf_op jit(solution)/shard_map/ppermute | solution.py:367
  50.6 33.0 %copy-start.1 = (bf16[224,4096]{1,0:T(8,128)(2,1)S(1)}, bf16[224,4096]{1,0:T(8,128)(2,1)}, u32[]{:S(2)}) copy-start(bf16[224,4096]{1,0:T(8,128)(2,1)} %down.1) | copy-start | bytes 5505028
  50.6 33.0 %copy-start.2 = (bf16[4096,4]{0,1:T(4,128)(2,1)S(1)}, bf16[4096,4]{0,1:T(4,128)(2,1)}, u32[]{:S(2)}) copy-start(bf16[4096,4]{0,1:T(4,128)(2,1)} %param.22) | copy-start | bytes 98308
  50.6 33.0 %copy-start.3 = (bf16[4096]{0:T(1024)(128)(2,1)S(1)}, bf16[4096]{0:T(1024)(128)(2,1)}, u32[]{:S(2)}) copy-start(bf16[4096]{0:T(1024)(128)(2,1)} %gain.1) | copy-start | bytes 24580
  50.6 33.0 %copy-start.4 = (s32[16,2]{0,1:T(2,128)S(1)}, s32[16,2]{0,1:T(2,128)}, u32[]{:S(2)}) copy-start(s32[16,2]{0,1:T(2,128)} %param.23) | copy-start | bytes 388
  62.6 21.0 %all-to-all-start.3 = ((bf16[128,4,128]{2,1,0:T(4,128)(2,1)}), bf16[128,4,128]{2,1,0:T(4,128)(2,1)S(1)}, u32[]{:S(2)}, u32[]{:S(2)}) async-start(bf16[128,4,128]{2,1,0:T(4,128)(2,1)} %get-tuple-element.7), calls=%async_computation.3 | async-start | bytes 262144 | tf_op jit(solution)/shard_map/all_to_all | solution.py:31
  83.6 2.0 %copy-start = (bf16[2,4096,224]{1,2,0:T(8,128)(2,1)S(1)}, bf16[2,4096,224]{1,2,0:T(8,128)(2,1)}, u32[]{:S(2)}) copy-start(bf16[2,4096,224]{1,2,0:T(8,128)(2,1)} %param.24) | copy-start | bytes 11010052

commit v5 on v4

--- a/solution.py
+++ b/solution.py
@@ -22,6 +22,7 @@
 IN_SMEM = pl.BlockSpec(memory_space=pltpu.SMEM)
 IN_HBM = pl.BlockSpec(memory_space=pltpu.HBM)
 BATCH = 4
+CHUNKS = 4
 MIB = 1 << 20
 COVER = pl.CostEstimate(flops=8*10**8, bytes_accessed=8 << 20, transcendentals=0)
 ALL_VMEM = 67043328
@@ -54,6 +55,7 @@
     insert_slot_in,
     prefix_len_in,
     queries_in,
+    weight_in,
     cache,
     inserted,
     out,
@@ -61,6 +63,7 @@
     insert_slot,
     prefix_len,
     queries,
+    weight,
     spread,
     rows,
     score_of,
@@ -75,15 +78,16 @@
         pltpu.make_async_copy(insert_slot_in, insert_slot, sems.at[1]),
         pltpu.make_async_copy(prefix_len_in, prefix_len, sems.at[2]),
         pltpu.make_async_copy(queries_in, queries, sems.at[3]),
+        pltpu.make_async_copy(weight_in, weight, sems.at[4]),
     ]
     copies += [
-        pltpu.make_async_copy(cache.at[k, s], rows.at[s, k], sems.at[4 + 2 * s + k])
+        pltpu.make_async_copy(cache.at[k, s], rows.at[s, k], sems.at[5 + 2 * s + k])
         for s in range(slots)
         for k in range(2)
     ]
     copies += [
         pltpu.make_async_copy(
-            inserted.at[k, j], rows.at[slots + j, k], sems.at[4 + 2 * (slots + j) + k]
+            inserted.at[k, j], rows.at[slots + j, k], sems.at[5 + 2 * (slots + j) + k]
         )
         for j in range(prefixes)
         for k in range(2)
@@ -170,7 +174,11 @@
     for g in range(KEY_VALUE_HEADS):
         out[g, :deep, :] = values[g * deep : (g + 1) * deep, :].astype(jnp.bfloat16)
         one = [stats[g * deep + h * slots : g * deep + (h + 1) * slots, :] for h in range(GROUP)]
-        out[g, deep:, :] = sum(one).astype(jnp.bfloat16)
+        out[g, deep : deep + slots, :] = sum(one).astype(jnp.bfloat16)
+        for h in range(GROUP):
+            at = deep + slots + h * weight.shape[0]
+            head = (g * GROUP + h) * HEAD_SIZE
+            out[g, at : at + weight.shape[0], :] = weight[:, head : head + HEAD_SIZE]
 
 
 def packed_stats(lane, peak, total):
@@ -218,7 +226,7 @@
 
 
 def spread_kernel(pieces, out):
-    part = whole_part([pieces[i] for i in range(pieces.shape[0])])
+    part = whole_part([pieces[i, : out.shape[1], :] for i in range(pieces.shape[0])])
     for i in range(out.shape[0]):
         out[i] = part
 
@@ -227,29 +235,60 @@
     out[...] = whole_part([pieces[i] for i in range(pieces.shape[0])])
 
 
-def pair_kernel(mine, other, out):
+def project_kernel(place, mine, other, landed, hidden, out):
+    slots, columns = hidden.shape
+    count, deep = landed.shape[0], mine.shape[0]
     values, _, _ = merge([mine[...], other[...]])
-    part = jnp.concatenate(values, axis=0).astype(jnp.bfloat16)
+    attn = jnp.concatenate(values, axis=1).astype(jnp.bfloat16)
+    heads = []
+    for h in range(GROUP):
+        at = deep + h * columns
+        parts = [landed[i, at : at + columns, :] for i in range(count)]
+        heads.append(jnp.concatenate(parts, axis=0))
+    weight = jnp.concatenate(heads, axis=1)
+    total = lax.dot_general(
+        attn, weight, (((1,), (1,)), ((), ())), preferred_element_type=jnp.float32
+    )
+    tiled = jnp.concatenate([hidden[...].astype(jnp.float32)] * count, axis=1)
+    owner = lax.broadcasted_iota(jnp.int32, tiled.shape, 1) // columns
+    part = (total + jnp.where(owner == place[0], tiled, 0.0)).astype(jnp.bfloat16)
+    for i in range(count):
+        out[i] = part
+
+
+def mixed_kernel(place, pieces, own, out):
+    columns = own.shape[1]
+    total = pieces[0].astype(jnp.float32)
+    for i in range(1, pieces.shape[0]):
+        total = total + pieces[i].astype(jnp.float32)
+    mixed = total.astype(jnp.bfloat16)
     for i in range(out.shape[0]):
-        out[i] = part
-
-
-def project_kernel(attn, weight, hidden, mixed, packed):
-    slots, columns = hidden.shape
-    blocks = [
-        attn[g, h * slots : (h + 1) * slots, :]
-        for g in range(KEY_VALUE_HEADS)
-        for h in range(GROUP)
-    ]
-    whole = jnp.concatenate(blocks, axis=1)
-    total = hidden[...].astype(jnp.float32) + lax.dot_general(
-        whole, weight[...], (((1,), (1,)), ((), ())), preferred_element_type=jnp.float32
-    )
-    mixed[...] = total.astype(jnp.bfloat16)
-    share = LANES // columns
-    deep = slots // share
-    line = jnp.concatenate([total[b * deep : (b + 1) * deep] for b in range(share)], axis=1)
-    packed[...] = jnp.broadcast_to(line[None].astype(jnp.bfloat16), packed.shape)
+        out[i] = mixed
+    mine = [total[:, i * columns : (i + 1) * columns] for i in range(pieces.shape[0])]
+    own[...] = sum(jnp.where(place[0] == i, x, 0.0) for i, x in enumerate(mine)).astype(
+        jnp.bfloat16
+    )
+
+
+def in_feature_order(gathered, share):
+    count, slots, width = gathered.shape
+    columns, rows, halves = LANES // share, count // share, width // LANES
+    block = lax.broadcasted_iota(jnp.int32, (slots, LANES), 1) // columns
+    tiles = {}
+    for m in range(rows):
+        for half in range(halves):
+            found = [
+                gathered[share * m + j, :, half * LANES : (half + 1) * LANES].astype(jnp.float32)
+                for j in range(share)
+            ]
+            for b in range(share):
+                tile = found[b]
+                for j in range(share):
+                    if j != b:
+                        turned = pltpu.roll(found[j], (j - b) % share * columns, axis=1)
+                        tile = jnp.where(block == j, turned, tile)
+                tiles[(half * share + b) * rows + m] = tile
+    return jnp.concatenate([tiles[k] for k in range(len(tiles))], axis=1)
 
 
 def swapped(tiles, share):
@@ -265,10 +304,21 @@
     return result
 
 
-def experts_kernel(share, expert, gathered, gain, router, chosen, gate_up, down, out):
-    blocks, slots = gathered.shape[0], gathered.shape[1]
-    tiles = swapped(gathered[...].astype(jnp.float32), share)
-    mixed = jnp.concatenate([tiles[k] for k in range(blocks)], axis=1)
+def experts_kernel(
+    share, expert, gathered, gain, router, chosen, gate_up_in, down, out, gate_up, sems
+):
+    blocks, slots = out.shape[0], out.shape[1]
+    step = blocks * LANES // CHUNKS
+    copies = []
+    for i in range(CHUNKS):
+        lanes = pl.ds(i * step, step)
+        copies.append(
+            pltpu.make_async_copy(
+                gate_up_in.at[:, :, lanes], gate_up.at[:, :, lanes], sems.at[i]
+            )
+        )
+        copies[i].start()
+    mixed = in_feature_order(gathered, share)
     scale = lax.rsqrt(jnp.sum(mixed * mixed, axis=1, keepdims=True) / (blocks * LANES) + 1e-05)
     normed = (mixed * scale * gain[...].astype(jnp.float32).reshape(1, blocks * LANES)).astype(jnp.bfloat16)
     plain = normed.astype(jnp.float32)
@@ -291,12 +341,18 @@
     gates = [jax.nn.sigmoid(picked[i] - picked[1 - i]) for i in range(2)]
     mine = expert[0].astype(jnp.float32)
     part = sum(jnp.where(ids[i] == mine, gates[i], 0.0) for i in range(2))
-    gate, up = [
-        lax.dot_general(
-            normed, gate_up[i], (((1,), (1,)), ((), ())), preferred_element_type=jnp.float32
+    gate, up = 0.0, 0.0
+    for i in range(CHUNKS):
+        copies[i].wait()
+        lanes = slice(i * step, (i + 1) * step)
+        contract = functools.partial(
+            lax.dot_general,
+            normed[:, lanes],
+            dimension_numbers=(((1,), (1,)), ((), ())),
+            preferred_element_type=jnp.float32,
         )
-        for i in range(2)
-    ]
+        gate = gate + contract(gate_up[0, :, lanes])
+        up = up + contract(gate_up[1, :, lanes])
     act = (gate * jax.nn.sigmoid(gate) * up).astype(jnp.bfloat16)
     term = part * jnp.dot(act, down[...], preferred_element_type=jnp.float32)
     tiles = [term[None, :, k * LANES : (k + 1) * LANES] for k in range(blocks)]
@@ -342,53 +398,67 @@
     first = (dev_index * ctx_rows).astype(jnp.int32).reshape(1)
     partials = pl.pallas_call(
         functools.partial(attention_kernel, devices * ctx_rows),
-        out_shape=jax.ShapeDtypeStruct((KEY_VALUE_HEADS, deep, HEAD_SIZE), bf16),
-        in_specs=[IN_SMEM] + [IN_HBM] * 6,
+        out_shape=jax.ShapeDtypeStruct((KEY_VALUE_HEADS, deep + GROUP * columns, HEAD_SIZE), bf16),
+        in_specs=[IN_SMEM] + [IN_HBM] * 7,
         out_specs=IN_VMEM,
         scratch_shapes=[
             pltpu.SMEM((slots,), jnp.int32),
             pltpu.SMEM((prefixes,), jnp.int32),
             pltpu.SMEM((prefixes,), jnp.int32),
             pltpu.VMEM(queries.shape, bf16),
+            pltpu.VMEM(out_weight.shape[::-1], bf16),
             pltpu.VMEM((slots * QUERY_HEADS, HEAD_SIZE), jnp.float32),
             pltpu.VMEM((slots + prefixes, 2, ctx_rows, kv_width), bf16),
             pltpu.VMEM((slots, QUERY_HEADS, ctx_rows), jnp.float32),
             pltpu.VMEM((slots * QUERY_HEADS, HEAD_SIZE), jnp.float32),
             pltpu.VMEM((slots * QUERY_HEADS, HEAD_SIZE), jnp.float32),
-            pltpu.SemaphoreType.DMA((4 + 2 * (slots + prefixes),)),
+            pltpu.SemaphoreType.DMA((5 + 2 * (slots + prefixes),)),
         ],
         compiler_params=pltpu.CompilerParams(vmem_limit_bytes=ALL_VMEM),
         name="attention",
-    )(first, cache_len, insert_slot, prefix_len, queries, cache_kv, inserted_key_value)
+    )(first, cache_len, insert_slot, prefix_len, queries, out_weight.T, cache_kv, inserted_key_value)
     along, across, pair = BLK
     copies = lax.axis_size(across)
-    part = merging(spread_kernel, (copies, deep, HEAD_SIZE), exchanged(partials, along))
+    landed = exchanged(partials, along)
+    part = merging(spread_kernel, (copies, deep, HEAD_SIZE), landed)
     part = merging(part_kernel, (deep, HEAD_SIZE), exchanged(part, across))
     other = lax.ppermute(part, pair, [(0, 1), (1, 0)])
-    own = merging(pair_kernel, (KEY_VALUE_HEADS, slots * GROUP, HEAD_SIZE), part, other)
-    attn = exchanged(own, along)
-
+    count = lax.axis_size(along)
+    place = lax.axis_index(along).astype(jnp.int32).reshape(1)
+    parts = pl.pallas_call(
+        project_kernel,
+        out_shape=jax.ShapeDtypeStruct((count, slots, count * columns), bf16),
+        in_specs=[IN_SMEM] + [IN_VMEM] * 4,
+        out_specs=IN_VMEM,
+        compiler_params=params(8),
+        cost_estimate=COVER,
+        name="project",
+    )(place, part, other, landed, hidden)
     local_mixed, packed = pl.pallas_call(
-        project_kernel,
+        mixed_kernel,
         out_shape=(
             jax.ShapeDtypeStruct((slots, columns), bf16),
-            jax.ShapeDtypeStruct((devices, slots // share, LANES), bf16),
+            jax.ShapeDtypeStruct((devices // count, slots, count * columns), bf16),
         ),
-        in_specs=[IN_VMEM] * 3,
+        in_specs=[IN_SMEM, IN_VMEM],
         out_specs=(IN_VMEM, IN_VMEM),
         compiler_params=params(8),
         cost_estimate=COVER,
-        name="project",
-    )(attn, out_weight.T, hidden)
-    gathered = exchanged(packed).reshape(blocks, slots, LANES)
+        name="mixed",
+    )(place, exchanged(parts, along))
+    gathered = exchanged(packed, (across, pair))
 
     expert = (dev_index * gate_up.shape[2] // FF).astype(jnp.int32).reshape(1)
     terms = pl.pallas_call(
         functools.partial(experts_kernel, share),
         out_shape=jax.ShapeDtypeStruct((blocks, slots, LANES), bf16),
-        in_specs=[IN_SMEM] + [IN_VMEM] * 6,
+        in_specs=[IN_SMEM] + [IN_VMEM] * 4 + [IN_HBM, IN_VMEM],
         out_specs=IN_VMEM,
-        compiler_params=params(16),
+        scratch_shapes=[
+            pltpu.VMEM((2, gate_up.shape[2], width), bf16),
+            pltpu.SemaphoreType.DMA((CHUNKS,)),
+        ],
+        compiler_params=params(50),
         name="experts",
     )(
         expert,

time: 108 us -> 101 us (0.935)
  starting transfers between devices: 16.6 us -> 10 us
  blocking collectives: 67.5 us -> 71.2 us
  waiting for transfers between devices: 13.2 us -> 10.1 us
  local copies, waits for them, and re-layouts: 2.07 us -> 0.03 us
  Pallas kernels: 8.1 us -> 9.55 us
    all_to_all x4, blocking collectives: 67.5 us -> 71.2 us  [exchanged(): return lax.all_to_all(pieces, axis, 0, 0, tiled=True)]
    all_to_all x1, starting transfers between devices: 8.59 us -> 4.93 us  [exchanged(): return lax.all_to_all(pieces, axis, 0, 0, tiled=True)]
    all_to_all x1, waiting for transfers between devices: 12.4 us -> 9.25 us  [exchanged(): return lax.all_to_all(pieces, axis, 0, 0, tiled=True)]
    ppermute x1, starting transfers between devices: 7.97 us -> 5.07 us  [on_device(): other = lax.ppermute(part, pair, [(0, 1), (1, 0)])]
    unnamed x14 -> x10, local copies, waits for them, and re-layouts: 2.07 us -> 0.03 us
    pallas_call x1, Pallas kernels: 1.77 us -> 3.22 us  [on_device(): pl.pallas_call(functools.partial(experts_kernel, share), out_shape=jax.Sh...]
where the time goes in v5:
time: 101 us
  blocking collectives  71.2 us (70%)
  waiting for transfers between devices  10.1 us (10%)
  starting transfers between devices  10 us (10%)
  Pallas kernels  9.55 us (9%)
    all_to_all x4, blocking collectives, exchanged(): return lax.all_to_all(pieces, axis, 0, 0, tiled=True)  71.2 us
    all_to_all x1, waiting for transfers between devices, exchanged(): return lax.all_to_all(pieces, axis, 0, 0, tiled=True)  9.25 us
    ppermute x1, starting transfers between devices, on_device(): other = lax.ppermute(part, pair, [(0, 1), (1, 0)])  5.07 us
    all_to_all x1, starting transfers between devices, exchanged(): return lax.all_to_all(pieces, axis, 0, 0, tiled=True)  4.93 us
    pallas_call x1, Pallas kernels, on_device(): pl.pallas_call(functools.partial(attention_kernel, devices * ctx_rows), o...  4.03 us
    pallas_call x1, Pallas kernels, on_device(): pl.pallas_call(functools.partial(experts_kernel, share), out_shape=jax.Sh...  3.22 us
  transfers between devices with their start and end apart: 2, of which 2 were waited for; matrix products, arithmetic and copies ran while one was open for 0% of the time, Pallas kernels for 0%

profile of v5, /device:TPU:513, one launch (start us, length us, event | category | flops | bytes accessed | tf_op | source)
XLA Modules:
  0.0 101.0 jit_solution(3421060628097233686)
XLA Ops:
  0.0 4.0 %attention.1 = bf16[8,208,128]{2,1,0:T(8,128)(2,1)} custom-call(s32[1]{0:T(128)} %bitcast.2.first, s32[16]{0:T(128)} %lengths_in.1, s32[8]{0:T(128)} %insert_slot_in.1, s32[8]{0:T(128)} %prefix_len_in.1, bf16[16,4096]{1,0:T(8,128)(2,1)} %queries_in.1, bf16[32,4096]{1,0:T(8,128)(2,1)} %bitcast.12, bf16[2,16,32,1024]{3,2,1,0:T(8,128)(2,1)} %cache.1, ...), custom_call_target="tpu_custom_call" | custom-call | tf_op jit(solution)/shard_map/attention/pallas_call | solution.py:399
  4.0 19.0 %all_to_all.25.pieces.landed = bf16[8,208,128]{2,1,0:T(8,128)(2,1)S(1)} all-to-all(bf16[8,208,128]{2,1,0:T(8,128)(2,1)} %attention.1), channel_id=1, replica_groups=mesh['rep'=2,'blk_0'=8,'blk_1'=8,'blk_2'=2] {'blk_0'}, dimensions={0} | all-to-all | bytes 851968 | tf_op jit(solution)/shard_map/all_to_all | solution.py:32
  23.0 0.3 spread_kernel.1
  23.3 0.0 copy-start.4
  23.3 24.1 %all_to_all.26.pieces = bf16[8,80,128]{2,1,0:T(8,128)(2,1)S(1)} all-to-all(bf16[8,80,128]{2,1,0:T(8,128)(2,1)S(1)} %spread_kernel.1), channel_id=1, replica_groups=mesh['rep'=2,'blk_0'=8,'blk_1'=8,'blk_2'=2] {'blk_1'}, dimensions={0} | all-to-all | bytes 327680 | tf_op jit(solution)/shard_map/all_to_all | solution.py:32
  47.4 0.3 part_kernel.1.mine
  47.6 5.1 %collective-permute-start = (bf16[80,128]{1,0:T(8,128)(2,1)S(1)}, bf16[80,128]{1,0:T(8,128)(2,1)S(1)}, u32[]{:S(2)}, u32[]{:S(2)}) collective-permute-start(bf16[80,128]{1,0:T(8,128)(2,1)S(1)} %part_kernel.1.mine), channel_id=1, source_target_pairs={{0,1},{1,0},{2,3},{3,2},{4,5},{5,4},{6,7},{7,6},{8,9},{9,8},{10,11... | collective-permute-start | bytes 61448 | tf_op jit(solution)/shard_map/ppermute | solution.py:425
  52.7 0.8 collective-permute-done.other
  53.5 0.0 copy-done.4
  53.5 0.3 project.1
  53.8 0.0 copy-start
  53.8 0.0 copy-start.1
  53.8 0.0 copy-start.2
  53.9 0.0 copy-start.3
  53.9 9.7 %all_to_all.27.pieces = bf16[8,16,256]{2,1,0:T(8,128)(2,1)S(1)} all-to-all(bf16[8,16,256]{2,1,0:T(8,128)(2,1)S(1)} %project.1), channel_id=1, replica_groups=mesh['rep'=2,'blk_0'=8,'blk_1'=8,'blk_2'=2] {'blk_0'}, dimensions={0} | all-to-all | bytes 131072 | tf_op jit(solution)/shard_map/all_to_all | solution.py:32
  63.5 0.7 mixed.1
  64.2 4.9 %all-to-all-start.3 = ((bf16[16,16,256]{2,1,0:T(8,128)(2,1)}), bf16[16,16,256]{2,1,0:T(8,128)(2,1)S(1)}, u32[]{:S(2)}, u32[]{:S(2)}) async-start(bf16[16,16,256]{2,1,0:T(8,128)(2,1)} %get-tuple-element.7), calls=%async_computation.3 | async-start | bytes 262144 | tf_op jit(solution)/shard_map/all_to_all | solution.py:32
  69.1 9.3 %all-to-all-done.3.gathered = bf16[16,16,256]{2,1,0:T(8,128)(2,1)S(1)} async-done(((bf16[16,16,256]{2,1,0:T(8,128)(2,1)}), bf16[16,16,256]{2,1,0:T(8,128)(2,1)S(1)}, u32[]{:S(2)}, u32[]{:S(2)}) %all-to-all-start.3) | async-done | bytes 131104 | tf_op jit(solution)/shard_map/all_to_all | solution.py:32
  78.4 0.0 copy-done
  78.4 0.0 copy-done.1
  78.4 0.0 copy-done.2
  78.4 0.0 copy-done.3
  78.4 3.2 %experts.1 = bf16[32,16,128]{2,1,0:T(8,128)(2,1)S(1)} custom-call(s32[1]{0:T(128)} %bitcast.expert, bf16[16,16,256]{2,1,0:T(8,128)(2,1)S(1)} %all-to-all-done.3.gathered, bf16[4096]{0:T(1024)(128)(2,1)S(1)} %copy-done.2, bf16[4,4096]{1,0:T(4,128)(2,1)S(1)} %bitcast.9, s32[2,16]{1,0:T(2,128)S(1)} %bitcast.10, bf16[2,224,4096]{2,1,0:T(8,128)(2,1)} %bitcast.11, ...), custom_call_target="tpu_custom_call" | custom-call | tf_op jit(solution)/shard_map/experts/pallas_call | solution.py:452
  81.7 18.5 %all_to_all.28.pieces = bf16[128,4,128]{2,1,0:T(4,128)(2,1)S(1)} all-to-all(bf16[128,4,128]{2,1,0:T(4,128)(2,1)S(1)} %bitcast.8), channel_id=1, replica_groups=mesh['rep'=2,'blk_0'=8,'blk_1'=8,'blk_2'=2] {'blk_0','blk_1','blk_2'}, dimensions={0} | all-to-all | bytes 262144 | tf_op jit(solution)/shard_map/all_to_all | solution.py:32
  100.2 0.8 final.1
Async XLA Ops:
  23.3 30.3 %copy-start.4 = (bf16[16,32]{1,0:T(8,128)(2,1)S(1)}, bf16[16,32]{1,0:T(8,128)(2,1)}, u32[]{:S(2)}) copy-start(bf16[16,32]{1,0:T(8,128)(2,1)} %hidden.1) | copy-start | bytes 3076
  47.6 5.9 %collective-permute-start = (bf16[80,128]{1,0:T(8,128)(2,1)S(1)}, bf16[80,128]{1,0:T(8,128)(2,1)S(1)}, u32[]{:S(2)}, u32[]{:S(2)}) collective-permute-start(bf16[80,128]{1,0:T(8,128)(2,1)S(1)} %part_kernel.1.mine), channel_id=1, source_target_pairs={{0,1},{1,0},{2,3},{3,2},{4,5},{5,4},{6,7},{7,6},{8,9},{9,8},{10,11... | collective-permute-start | bytes 61448 | tf_op jit(solution)/shard_map/ppermute | solution.py:425
  53.8 24.6 %copy-start = (bf16[224,4096]{1,0:T(8,128)(2,1)S(1)}, bf16[224,4096]{1,0:T(8,128)(2,1)}, u32[]{:S(2)}) copy-start(bf16[224,4096]{1,0:T(8,128)(2,1)} %down.1) | copy-start | bytes 5505028
  53.8 24.6 %copy-start.1 = (bf16[4096,4]{0,1:T(4,128)(2,1)S(1)}, bf16[4096,4]{0,1:T(4,128)(2,1)}, u32[]{:S(2)}) copy-start(bf16[4096,4]{0,1:T(4,128)(2,1)} %param.22) | copy-start | bytes 98308
  53.8 24.6 %copy-start.2 = (bf16[4096]{0:T(1024)(128)(2,1)S(1)}, bf16[4096]{0:T(1024)(128)(2,1)}, u32[]{:S(2)}) copy-start(bf16[4096]{0:T(1024)(128)(2,1)} %gain.1) | copy-start | bytes 24580
  53.9 24.6 %copy-start.3 = (s32[16,2]{0,1:T(2,128)S(1)}, s32[16,2]{0,1:T(2,128)}, u32[]{:S(2)}) copy-start(s32[16,2]{0,1:T(2,128)} %param.23) | copy-start | bytes 388
  64.2 14.2 %all-to-all-start.3 = ((bf16[16,16,256]{2,1,0:T(8,128)(2,1)}), bf16[16,16,256]{2,1,0:T(8,128)(2,1)S(1)}, u32[]{:S(2)}, u32[]{:S(2)}) async-start(bf16[16,16,256]{2,1,0:T(8,128)(2,1)} %get-tuple-element.7), calls=%async_computation.3 | async-start | bytes 262144 | tf_op jit(solution)/shard_map/all_to_all | solution.py:32

commit v6 on v5

--- a/solution.py
+++ b/solution.py
@@ -80,18 +80,19 @@
         pltpu.make_async_copy(queries_in, queries, sems.at[3]),
         pltpu.make_async_copy(weight_in, weight, sems.at[4]),
     ]
-    copies += [
-        pltpu.make_async_copy(cache.at[k, s], rows.at[s, k], sems.at[5 + 2 * s + k])
-        for s in range(slots)
-        for k in range(2)
-    ]
-    copies += [
-        pltpu.make_async_copy(
-            inserted.at[k, j], rows.at[slots + j, k], sems.at[5 + 2 * (slots + j) + k]
-        )
-        for j in range(prefixes)
-        for k in range(2)
-    ]
+    key_copies, value_copies = [], []
+    for k, group in enumerate((key_copies, value_copies)):
+        for start in range(0, slots, BATCH):
+            here = pl.ds(start, BATCH)
+            group.append((cache.at[k, here], rows.at[k, here]))
+        for start in range(0, prefixes, BATCH):
+            group.append(
+                (inserted.at[k, pl.ds(start, BATCH)], rows.at[k, pl.ds(slots + start, BATCH)])
+            )
+    for at, group in ((5, key_copies), (5 + len(key_copies), value_copies)):
+        for i, (source_ref, target_ref) in enumerate(group):
+            group[i] = pltpu.make_async_copy(source_ref, target_ref, sems.at[at + i])
+    copies = copies[:4] + key_copies + value_copies + copies[4:]
     for copy in copies:
         copy.start()
     for copy in copies[:4]:
@@ -114,7 +115,7 @@
             start = jnp.where(mine, there, start)
         valid.append(length - start)
         source.append(at)
-    for copy in copies[4:]:
+    for copy in key_copies:
         copy.wait()
     shape = (wide, KEY_VALUE_HEADS * HEAD_SIZE)
     own = (
@@ -132,10 +133,12 @@
         blocks = jnp.where(own, tiled, 0.0).astype(jnp.bfloat16)
         score_of[s] = lax.dot_general(
             blocks,
-            rows[source[s], 0],
+            rows[0, source[s]],
             (((1,), (1,)), ((), ())),
             preferred_element_type=jnp.float32,
         ) * (1.0 / math.sqrt(HEAD_SIZE))
+    for copy in value_copies:
+        copy.wait()
     for batch in range(0, slots, BATCH):
         several = range(batch, batch + BATCH)
         inside = [place < valid[s] for s in several]
@@ -148,7 +151,7 @@
         totals = [jnp.sum(x, axis=1, keepdims=True) for x in weights]
         every = [
             jnp.dot(
-                x.astype(jnp.bfloat16), rows[source[s], 1], preferred_element_type=jnp.float32
+                x.astype(jnp.bfloat16), rows[1, source[s]], preferred_element_type=jnp.float32
             )
             for x, s in zip(weights, several)
         ]
@@ -171,6 +174,7 @@
                 counted, packed_stats(lane, peak, total), 0.0
             )
     deep = GROUP * slots
+    copies[-1].wait()
     for g in range(KEY_VALUE_HEADS):
         out[g, :deep, :] = values[g * deep : (g + 1) * deep, :].astype(jnp.bfloat16)
         one = [stats[g * deep + h * slots : g * deep + (h + 1) * slots, :] for h in range(GROUP)]
@@ -396,6 +400,9 @@
     bf16 = jnp.bfloat16
 
     first = (dev_index * ctx_rows).astype(jnp.int32).reshape(1)
+    place = lax.axis_index(BLK[0]).astype(jnp.int32).reshape(1)
+    expert = (dev_index * gate_up.shape[2] // FF).astype(jnp.int32).reshape(1)
+    first, place, expert = lax.optimization_barrier((first, place, expert))
     partials = pl.pallas_call(
         functools.partial(attention_kernel, devices * ctx_rows),
         out_shape=jax.ShapeDtypeStruct((KEY_VALUE_HEADS, deep + GROUP * columns, HEAD_SIZE), bf16),
@@ -408,11 +415,11 @@
             pltpu.VMEM(queries.shape, bf16),
             pltpu.VMEM(out_weight.shape[::-1], bf16),
             pltpu.VMEM((slots * QUERY_HEADS, HEAD_SIZE), jnp.float32),
-            pltpu.VMEM((slots + prefixes, 2, ctx_rows, kv_width), bf16),
+            pltpu.VMEM((2, slots + prefixes, ctx_rows, kv_width), bf16),
             pltpu.VMEM((slots, QUERY_HEADS, ctx_rows), jnp.float32),
             pltpu.VMEM((slots * QUERY_HEADS, HEAD_SIZE), jnp.float32),
             pltpu.VMEM((slots * QUERY_HEADS, HEAD_SIZE), jnp.float32),
-            pltpu.SemaphoreType.DMA((5 + 2 * (slots + prefixes),)),
+            pltpu.SemaphoreType.DMA((5 + 2 * (slots + prefixes) // BATCH,)),
         ],
         compiler_params=pltpu.CompilerParams(vmem_limit_bytes=ALL_VMEM),
         name="attention",
@@ -424,7 +431,6 @@
     part = merging(part_kernel, (deep, HEAD_SIZE), exchanged(part, across))
     other = lax.ppermute(part, pair, [(0, 1), (1, 0)])
     count = lax.axis_size(along)
-    place = lax.axis_index(along).astype(jnp.int32).reshape(1)
     parts = pl.pallas_call(
         project_kernel,
         out_shape=jax.ShapeDtypeStruct((count, slots, count * columns), bf16),
@@ -448,7 +454,6 @@
     )(place, exchanged(parts, along))
     gathered = exchanged(packed, (across, pair))
 
-    expert = (dev_index * gate_up.shape[2] // FF).astype(jnp.int32).reshape(1)
     terms = pl.pallas_call(
         functools.partial(experts_kernel, share),
         out_shape=jax.ShapeDtypeStruct((blocks, slots, LANES), bf16),

time: 101 us -> 99.3 us (0.983)
  blocking collectives: 71.2 us -> 84.5 us
  waiting for transfers between devices: 10.1 us -> 0.84 us
  starting transfers between devices: 10 us -> 5.07 us
  Pallas kernels: 9.55 us -> 8.42 us
    all_to_all x4 -> x5, blocking collectives: 71.2 us -> 84.5 us  [exchanged(): return lax.all_to_all(pieces, axis, 0, 0, tiled=True)]
    all_to_all x1 -> x0, waiting for transfers between devices: 9.25 us -> none  [exchanged(): return lax.all_to_all(pieces, axis, 0, 0, tiled=True)]
    all_to_all x1 -> x0, starting transfers between devices: 4.93 us -> none  [exchanged(): return lax.all_to_all(pieces, axis, 0, 0, tiled=True)]
  transfers between devices with their start and end apart: 2 -> 1, of which waited for: 2 -> 1; matrix products, arithmetic and copies ran while one was open for 0% -> 0% of each run, Pallas kernels for 0% -> 0%
where the time goes in v6:
time: 99.3 us; the launch traced here: 98.9 us
  blocking collectives  84.5 us (85%)
  Pallas kernels  8.42 us (8%)
  starting transfers between devices  5.07 us (5%)
    all_to_all x5, blocking collectives, exchanged(): return lax.all_to_all(pieces, axis, 0, 0, tiled=True)  84.5 us
    ppermute x1, starting transfers between devices, on_device(): other = lax.ppermute(part, pair, [(0, 1), (1, 0)])  5.07 us
    pallas_call x1, Pallas kernels, on_device(): pl.pallas_call(functools.partial(attention_kernel, devices * ctx_rows), o...  3.48 us
    pallas_call x1, Pallas kernels, on_device(): pl.pallas_call(functools.partial(experts_kernel, share), out_shape=jax.Sh...  3.22 us
  transfers between devices with their start and end apart: 1, of which 1 were waited for; matrix products, arithmetic and copies ran while one was open for 0% of the time, Pallas kernels for 0%

profile of v6, /device:TPU:513, one launch (start us, length us, event | category | flops | bytes accessed | tf_op | source)
XLA Modules:
  0.0 98.9 jit_solution(15630377999773689971)
XLA Ops:
  0.0 3.5 %attention.1 = bf16[8,208,128]{2,1,0:T(8,128)(2,1)} custom-call(s32[1]{0:T(128)} %bitcast.first, s32[16]{0:T(128)} %lengths_in.1, s32[8]{0:T(128)} %insert_slot_in.1, s32[8]{0:T(128)} %prefix_len_in.1, bf16[16,4096]{1,0:T(8,128)(2,1)} %queries_in.1, bf16[32,4096]{1,0:T(8,128)(2,1)} %bitcast.12, bf16[2,16,32,1024]{3,2,1,0:T(8,128)(2,1)} %cache.1, ...), custom_call_target="tpu_custom_call" | custom-call | tf_op jit(solution)/shard_map/attention/pallas_call | solution.py:406
  3.5 19.0 %all_to_all.25.pieces.landed = bf16[8,208,128]{2,1,0:T(8,128)(2,1)S(1)} all-to-all(bf16[8,208,128]{2,1,0:T(8,128)(2,1)} %attention.1), channel_id=1, replica_groups=mesh['rep'=2,'blk_0'=8,'blk_1'=8,'blk_2'=2] {'blk_0'}, dimensions={0} | all-to-all | bytes 851968 | tf_op jit(solution)/shard_map/all_to_all | solution.py:32
  22.4 0.3 spread_kernel.1
  22.7 0.0 copy-start.4
  22.7 24.1 %all_to_all.26.pieces = bf16[8,80,128]{2,1,0:T(8,128)(2,1)S(1)} all-to-all(bf16[8,80,128]{2,1,0:T(8,128)(2,1)S(1)} %spread_kernel.1), channel_id=1, replica_groups=mesh['rep'=2,'blk_0'=8,'blk_1'=8,'blk_2'=2] {'blk_1'}, dimensions={0} | all-to-all | bytes 327680 | tf_op jit(solution)/shard_map/all_to_all | solution.py:32
  46.8 0.3 part_kernel.1.mine
  47.1 5.1 %collective-permute-start = (bf16[80,128]{1,0:T(8,128)(2,1)S(1)}, bf16[80,128]{1,0:T(8,128)(2,1)S(1)}, u32[]{:S(2)}, u32[]{:S(2)}) collective-permute-start(bf16[80,128]{1,0:T(8,128)(2,1)S(1)} %part_kernel.1.mine), channel_id=1, source_target_pairs={{0,1},{1,0},{2,3},{3,2},{4,5},{5,4},{6,7},{7,6},{8,9},{9,8},{10,11... | collective-permute-start | bytes 61448 | tf_op jit(solution)/shard_map/ppermute | solution.py:432
  52.1 0.8 collective-permute-done.other
  53.0 0.0 copy-done.4
  53.0 0.3 project.1
  53.3 0.0 copy-start
  53.3 0.0 copy-start.1
  53.3 0.0 copy-start.2
  53.3 0.0 copy-start.3
  53.3 9.7 %all_to_all.27.pieces = bf16[8,16,256]{2,1,0:T(8,128)(2,1)S(1)} all-to-all(bf16[8,16,256]{2,1,0:T(8,128)(2,1)S(1)} %project.1), channel_id=1, replica_groups=mesh['rep'=2,'blk_0'=8,'blk_1'=8,'blk_2'=2] {'blk_0'}, dimensions={0} | all-to-all | bytes 131072 | tf_op jit(solution)/shard_map/all_to_all | solution.py:32
  63.0 0.1 mixed.1
  63.1 13.3 %all_to_all.28.gathered = bf16[16,16,256]{2,1,0:T(8,128)(2,1)S(1)} all-to-all(bf16[16,16,256]{2,1,0:T(8,128)(2,1)S(1)} %get-tuple-element.13), channel_id=1, replica_groups=mesh['rep'=2,'blk_0'=8,'blk_1'=8,'blk_2'=2] {'blk_1','blk_2'}, dimensions={0} | all-to-all | bytes 262144 | tf_op jit(solution)/shard_map/all_to_all | solution.py:32
  76.4 0.0 copy-done
  76.4 0.0 copy-done.1
  76.4 0.0 copy-done.2
  76.4 0.0 copy-done.3
  76.4 3.2 %experts.1 = bf16[32,16,128]{2,1,0:T(8,128)(2,1)S(1)} custom-call(s32[1]{0:T(128)} %bitcast.2.expert, bf16[16,16,256]{2,1,0:T(8,128)(2,1)S(1)} %all_to_all.28.gathered, bf16[4096]{0:T(1024)(128)(2,1)S(1)} %copy-done.2, bf16[4,4096]{1,0:T(4,128)(2,1)S(1)} %bitcast.9, s32[2,16]{1,0:T(2,128)S(1)} %bitcast.10, bf16[2,224,4096]{2,1,0:T(8,128)(2,1)} %bitcast.11, ...), custom_call_target="tpu_custom_call" | custom-call | tf_op jit(solution)/shard_map/experts/pallas_call | solution.py:457
  79.6 18.5 %all_to_all.29.pieces = bf16[128,4,128]{2,1,0:T(4,128)(2,1)S(1)} all-to-all(bf16[128,4,128]{2,1,0:T(4,128)(2,1)S(1)} %bitcast.8), channel_id=1, replica_groups=mesh['rep'=2,'blk_0'=8,'blk_1'=8,'blk_2'=2] {'blk_0','blk_1','blk_2'}, dimensions={0} | all-to-all | bytes 262144 | tf_op jit(solution)/shard_map/all_to_all | solution.py:32
  98.1 0.8 final.1
Async XLA Ops:
  22.7 30.3 %copy-start.4 = (bf16[16,32]{1,0:T(8,128)(2,1)S(1)}, bf16[16,32]{1,0:T(8,128)(2,1)}, u32[]{:S(2)}) copy-start(bf16[16,32]{1,0:T(8,128)(2,1)} %hidden.1) | copy-start | bytes 3076
  47.1 5.9 %collective-permute-start = (bf16[80,128]{1,0:T(8,128)(2,1)S(1)}, bf16[80,128]{1,0:T(8,128)(2,1)S(1)}, u32[]{:S(2)}, u32[]{:S(2)}) collective-permute-start(bf16[80,128]{1,0:T(8,128)(2,1)S(1)} %part_kernel.1.mine), channel_id=1, source_target_pairs={{0,1},{1,0},{2,3},{3,2},{4,5},{5,4},{6,7},{7,6},{8,9},{9,8},{10,11... | collective-permute-start | bytes 61448 | tf_op jit(solution)/shard_map/ppermute | solution.py:432
  53.3 23.1 %copy-start = (bf16[224,4096]{1,0:T(8,128)(2,1)S(1)}, bf16[224,4096]{1,0:T(8,128)(2,1)}, u32[]{:S(2)}) copy-start(bf16[224,4096]{1,0:T(8,128)(2,1)} %down.1) | copy-start | bytes 5505028
  53.3 23.1 %copy-start.1 = (bf16[4096,4]{0,1:T(4,128)(2,1)S(1)}, bf16[4096,4]{0,1:T(4,128)(2,1)}, u32[]{:S(2)}) copy-start(bf16[4096,4]{0,1:T(4,128)(2,1)} %param.22) | copy-start | bytes 98308
  53.3 23.1 %copy-start.2 = (bf16[4096]{0:T(1024)(128)(2,1)S(1)}, bf16[4096]{0:T(1024)(128)(2,1)}, u32[]{:S(2)}) copy-start(bf16[4096]{0:T(1024)(128)(2,1)} %gain.1) | copy-start | bytes 24580
  53.3 23.1 %copy-start.3 = (s32[16,2]{0,1:T(2,128)S(1)}, s32[16,2]{0,1:T(2,128)}, u32[]{:S(2)}) copy-start(s32[16,2]{0,1:T(2,128)} %param.23) | copy-start | bytes 388

commit v7 on v6

--- a/solution.py
+++ b/solution.py
@@ -22,7 +22,7 @@
 IN_SMEM = pl.BlockSpec(memory_space=pltpu.SMEM)
 IN_HBM = pl.BlockSpec(memory_space=pltpu.HBM)
 BATCH = 4
-CHUNKS = 4
+CHUNKS = 8
 MIB = 1 << 20
 COVER = pl.CostEstimate(flops=8*10**8, bytes_accessed=8 << 20, transcendentals=0)
 ALL_VMEM = 67043328
@@ -309,9 +309,9 @@
 
 
 def experts_kernel(
-    share, expert, gathered, gain, router, chosen, gate_up_in, down, out, gate_up, sems
+    share, expert, core, gathered, gain, router, chosen, gate_up_in, down, own, other, gate_up, sems
 ):
-    blocks, slots = out.shape[0], out.shape[1]
+    blocks, slots = own.shape[0], 2 * own.shape[1]
     step = blocks * LANES // CHUNKS
     copies = []
     for i in range(CHUNKS):
@@ -360,7 +360,21 @@
     act = (gate * jax.nn.sigmoid(gate) * up).astype(jnp.bfloat16)
     term = part * jnp.dot(act, down[...], preferred_element_type=jnp.float32)
     tiles = [term[None, :, k * LANES : (k + 1) * LANES] for k in range(blocks)]
-    out[...] = swapped(jnp.concatenate(tiles, axis=0), share).astype(jnp.bfloat16)
+    even, odd = by_core(swapped(jnp.concatenate(tiles, axis=0), share), slots // share)
+    own[...] = jnp.where(core[0] == 0, even, odd)
+    other[...] = jnp.where(core[0] == 0, odd, even).astype(jnp.bfloat16)
+
+
+def by_core(tiles, deep):
+    top, bottom = tiles[:, : 2 * deep], tiles[:, 2 * deep :]
+    first = lax.broadcasted_iota(jnp.int32, top.shape, 1) < deep
+    even = jnp.where(first, top, pltpu.roll(bottom, deep, axis=1))
+    odd = jnp.where(first, pltpu.roll(top, deep, axis=1), bottom)
+    return even, odd
+
+
+def add_kernel(own, other, out):
+    out[...] = (own[...] + other[...].astype(jnp.float32)).astype(jnp.bfloat16)
 
 
 def final_kernel(pieces, mixed, out):
@@ -402,7 +416,8 @@
     first = (dev_index * ctx_rows).astype(jnp.int32).reshape(1)
     place = lax.axis_index(BLK[0]).astype(jnp.int32).reshape(1)
     expert = (dev_index * gate_up.shape[2] // FF).astype(jnp.int32).reshape(1)
-    first, place, expert = lax.optimization_barrier((first, place, expert))
+    core = lax.axis_index(BLK[2]).astype(jnp.int32).reshape(1)
+    first, place, expert, core = lax.optimization_barrier((first, place, expert, core))
     partials = pl.pallas_call(
         functools.partial(attention_kernel, devices * ctx_rows),
         out_shape=jax.ShapeDtypeStruct((KEY_VALUE_HEADS, deep + GROUP * columns, HEAD_SIZE), bf16),
@@ -454,11 +469,14 @@
     )(place, exchanged(parts, along))
     gathered = exchanged(packed, (across, pair))
 
-    terms = pl.pallas_call(
+    own, other = pl.pallas_call(
         functools.partial(experts_kernel, share),
-        out_shape=jax.ShapeDtypeStruct((blocks, slots, LANES), bf16),
-        in_specs=[IN_SMEM] + [IN_VMEM] * 4 + [IN_HBM, IN_VMEM],
-        out_specs=IN_VMEM,
+        out_shape=(
+            jax.ShapeDtypeStruct((blocks, slots // 2, LANES), jnp.float32),
+            jax.ShapeDtypeStruct((blocks, slots // 2, LANES), bf16),
+        ),
+        in_specs=[IN_SMEM] * 2 + [IN_VMEM] * 4 + [IN_HBM, IN_VMEM],
+        out_specs=(IN_VMEM, IN_VMEM),
         scratch_shapes=[
             pltpu.VMEM((2, gate_up.shape[2], width), bf16),
             pltpu.SemaphoreType.DMA((CHUNKS,)),
@@ -467,6 +485,7 @@
         name="experts",
     )(
         expert,
+        core,
         gathered,
         norm_gain,
         router_weight.T,
@@ -474,7 +493,9 @@
         jnp.swapaxes(gate_up, 1, 2),
         down_proj,
     )
-    moe = exchanged(terms.reshape(devices, slots // share, LANES))
+    other = lax.ppermute(other, pair, [(0, 1), (1, 0)])
+    terms = merging(add_kernel, own.shape, own, other)
+    moe = exchanged(terms.reshape(devices // 2, slots // share, LANES), (along, across))
     return pl.pallas_call(
         final_kernel,
         out_shape=jax.ShapeDtypeStruct((slots, columns), bf16),

time: 99.3 us -> 97.5 us (0.982)
  blocking collectives: 84.5 us -> 81.6 us
  waiting for transfers between devices: 0.84 us -> 2.07 us
    all_to_all x5, blocking collectives: 84.5 us -> 81.6 us  [exchanged(): return lax.all_to_all(pieces, axis, 0, 0, tiled=True)]
    ppermute x0 -> x1, waiting for transfers between devices: none -> 1.23 us  [on_device(): other = lax.ppermute(other, pair, [(0, 1), (1, 0)])]
  transfers between devices with their start and end apart: 1 -> 2, of which waited for: 1 -> 2; matrix products, arithmetic and copies ran while one was open for 0% -> 0% of each run, Pallas kernels for 0% -> 0%
where the time goes in v7:
time: 97.5 us; the launch traced here: 97.1 us
  blocking collectives  81.6 us (84%)
  Pallas kernels  8.13 us (8%)
  starting transfers between devices  5.21 us (5%)
  waiting for transfers between devices  2.07 us (2%)
    all_to_all x5, blocking collectives, exchanged(): return lax.all_to_all(pieces, axis, 0, 0, tiled=True)  81.6 us
    ppermute x1, starting transfers between devices, on_device(): other = lax.ppermute(part, pair, [(0, 1), (1, 0)])  5.07 us
    pallas_call x1, Pallas kernels, on_device(): pl.pallas_call(functools.partial(attention_kernel, devices * ctx_rows), o...  3.48 us
    pallas_call x1, Pallas kernels, on_device(): pl.pallas_call(functools.partial(experts_kernel, share), out_shape=(jax.S...  2.99 us
  transfers between devices with their start and end apart: 2, of which 2 were waited for; matrix products, arithmetic and copies ran while one was open for 0% of the time, Pallas kernels for 0%

profile of v7, /device:TPU:513, one launch (start us, length us, event | category | flops | bytes accessed | tf_op | source)
XLA Modules:
  0.0 97.1 jit_solution(694059136196257786)
XLA Ops:
  0.0 3.5 %attention.1 = bf16[8,208,128]{2,1,0:T(8,128)(2,1)} custom-call(s32[1]{0:T(128)} %bitcast.first, s32[16]{0:T(128)} %lengths_in.1, s32[8]{0:T(128)} %insert_slot_in.1, s32[8]{0:T(128)} %prefix_len_in.1, bf16[16,4096]{1,0:T(8,128)(2,1)} %queries_in.1, bf16[32,4096]{1,0:T(8,128)(2,1)} %bitcast.13, bf16[2,16,32,1024]{3,2,1,0:T(8,128)(2,1)} %cache.1, ...), custom_call_target="tpu_custom_call" | custom-call | tf_op jit(solution)/shard_map/attention/pallas_call | solution.py:421
  3.5 19.0 %all_to_all.25.pieces.landed = bf16[8,208,128]{2,1,0:T(8,128)(2,1)S(1)} all-to-all(bf16[8,208,128]{2,1,0:T(8,128)(2,1)} %attention.1), channel_id=1, replica_groups=mesh['rep'=2,'blk_0'=8,'blk_1'=8,'blk_2'=2] {'blk_0'}, dimensions={0} | all-to-all | bytes 851968 | tf_op jit(solution)/shard_map/all_to_all | solution.py:32
  22.4 0.3 spread_kernel.1
  22.7 0.0 copy-start.4
  22.7 24.1 %all_to_all.26.pieces = bf16[8,80,128]{2,1,0:T(8,128)(2,1)S(1)} all-to-all(bf16[8,80,128]{2,1,0:T(8,128)(2,1)S(1)} %spread_kernel.1), channel_id=1, replica_groups=mesh['rep'=2,'blk_0'=8,'blk_1'=8,'blk_2'=2] {'blk_1'}, dimensions={0} | all-to-all | bytes 327680 | tf_op jit(solution)/shard_map/all_to_all | solution.py:32
  46.8 0.3 part_kernel.1.mine
  47.1 5.1 %collective-permute-start = (bf16[80,128]{1,0:T(8,128)(2,1)S(1)}, bf16[80,128]{1,0:T(8,128)(2,1)S(1)}, u32[]{:S(2)}, u32[]{:S(2)}) collective-permute-start(bf16[80,128]{1,0:T(8,128)(2,1)S(1)} %part_kernel.1.mine), channel_id=1, source_target_pairs={{0,1},{1,0},{2,3},{3,2},{4,5},{5,4},{6,7},{7,6},{8,9},{9,8},{10,11... | collective-permute-start | bytes 61448 | tf_op jit(solution)/shard_map/ppermute | solution.py:447
  52.1 0.8 collective-permute-done.other
  53.0 0.0 copy-done.4
  53.0 0.3 project.1
  53.3 0.0 copy-start
  53.3 0.0 copy-start.1
  53.3 0.0 copy-start.2
  53.3 0.0 copy-start.3
  53.3 9.7 %all_to_all.27.pieces = bf16[8,16,256]{2,1,0:T(8,128)(2,1)S(1)} all-to-all(bf16[8,16,256]{2,1,0:T(8,128)(2,1)S(1)} %project.1), channel_id=1, replica_groups=mesh['rep'=2,'blk_0'=8,'blk_1'=8,'blk_2'=2] {'blk_0'}, dimensions={0} | all-to-all | bytes 131072 | tf_op jit(solution)/shard_map/all_to_all | solution.py:32
  63.0 0.1 mixed.1
  63.1 13.3 %all_to_all.28.gathered = bf16[16,16,256]{2,1,0:T(8,128)(2,1)S(1)} all-to-all(bf16[16,16,256]{2,1,0:T(8,128)(2,1)S(1)} %get-tuple-element.17), channel_id=1, replica_groups=mesh['rep'=2,'blk_0'=8,'blk_1'=8,'blk_2'=2] {'blk_1','blk_2'}, dimensions={0} | all-to-all | bytes 262144 | tf_op jit(solution)/shard_map/all_to_all | solution.py:32
  76.4 0.0 copy-done
  76.4 0.0 copy-done.1
  76.4 0.0 copy-done.2
  76.4 0.0 copy-done.3
  76.4 3.0 %experts.1 = (f32[32,8,128]{2,1,0:T(8,128)S(1)}, bf16[32,8,128]{2,1,0:T(8,128)(2,1)S(1)}) custom-call(s32[1]{0:T(128)} %bitcast.2.expert, s32[1]{0:T(128)} %bitcast.3.core, bf16[16,16,256]{2,1,0:T(8,128)(2,1)S(1)} %all_to_all.28.gathered, bf16[4096]{0:T(1024)(128)(2,1)S(1)} %copy-done.2, bf16[4,4096]{1,0:T(4,128)(2,1)S(1)} %bitcast.10, ...), custom_call_target="tpu_custom_call" | custom-call | tf_op jit(solution)/shard_map/experts/pallas_call | solution.py:472
  79.4 0.1 collective-permute-start.1
  79.5 1.2 %collective-permute-done.1.other = bf16[32,8,128]{2,1,0:T(8,128)(2,1)S(1)} collective-permute-done((bf16[32,8,128]{2,1,0:T(8,128)(2,1)S(1)}, bf16[32,8,128]{2,1,0:T(8,128)(2,1)S(1)}, u32[]{:S(2)}, u32[]{:S(2)}) %collective-permute-start.1) | collective-permute-done | bytes 65568 | tf_op jit(solution)/shard_map/ppermute | solution.py:496
  80.8 15.6 %all_to_all.29.pieces = bf16[64,4,128]{2,1,0:T(4,128)(2,1)S(1)} all-to-all(bf16[64,4,128]{2,1,0:T(4,128)(2,1)S(1)} %bitcast.9), channel_id=1, replica_groups=mesh['rep'=2,'blk_0'=8,'blk_1'=8,'blk_2'=2] {'blk_0','blk_1'}, dimensions={0} | all-to-all | bytes 131072 | tf_op jit(solution)/shard_map/all_to_all | solution.py:32
  96.3 0.7 final.1
  (1 shorter events, 0.0 us)
Async XLA Ops:
  22.7 30.3 %copy-start.4 = (bf16[16,32]{1,0:T(8,128)(2,1)S(1)}, bf16[16,32]{1,0:T(8,128)(2,1)}, u32[]{:S(2)}) copy-start(bf16[16,32]{1,0:T(8,128)(2,1)} %hidden.1) | copy-start | bytes 3076
  47.1 5.9 %collective-permute-start = (bf16[80,128]{1,0:T(8,128)(2,1)S(1)}, bf16[80,128]{1,0:T(8,128)(2,1)S(1)}, u32[]{:S(2)}, u32[]{:S(2)}) collective-permute-start(bf16[80,128]{1,0:T(8,128)(2,1)S(1)} %part_kernel.1.mine), channel_id=1, source_target_pairs={{0,1},{1,0},{2,3},{3,2},{4,5},{5,4},{6,7},{7,6},{8,9},{9,8},{10,11... | collective-permute-start | bytes 61448 | tf_op jit(solution)/shard_map/ppermute | solution.py:447
  53.3 23.1 %copy-start = (bf16[224,4096]{1,0:T(8,128)(2,1)S(1)}, bf16[224,4096]{1,0:T(8,128)(2,1)}, u32[]{:S(2)}) copy-start(bf16[224,4096]{1,0:T(8,128)(2,1)} %down.1) | copy-start | bytes 5505028
  53.3 23.1 %copy-start.1 = (bf16[4096,4]{0,1:T(4,128)(2,1)S(1)}, bf16[4096,4]{0,1:T(4,128)(2,1)}, u32[]{:S(2)}) copy-start(bf16[4096,4]{0,1:T(4,128)(2,1)} %param.22) | copy-start | bytes 98308
  53.3 23.1 %copy-start.2 = (bf16[4096]{0:T(1024)(128)(2,1)S(1)}, bf16[4096]{0:T(1024)(128)(2,1)}, u32[]{:S(2)}) copy-start(bf16[4096]{0:T(1024)(128)(2,1)} %gain.1) | copy-start | bytes 24580
  53.3 23.1 %copy-start.3 = (s32[16,2]{0,1:T(2,128)S(1)}, s32[16,2]{0,1:T(2,128)}, u32[]{:S(2)}) copy-start(s32[16,2]{0,1:T(2,128)} %param.23) | copy-start | bytes 388
  79.4 1.4 %collective-permute-start.1 = (bf16[32,8,128]{2,1,0:T(8,128)(2,1)S(1)}, bf16[32,8,128]{2,1,0:T(8,128)(2,1)S(1)}, u32[]{:S(2)}, u32[]{:S(2)}) collective-permute-start(bf16[32,8,128]{2,1,0:T(8,128)(2,1)S(1)} %get-tuple-element.19), channel_id=1, source_target_pairs={{0,1},{1,0},{2,3},{3,2},{4,5},{5,4},{6,7},{7,6},{8,9},{9,8},{10,11... | collective-permute-start | bytes 196616 | tf_op jit(solution)/shard_map/ppermute | solution.py:496

commit v8 on v7

--- a/solution.py
+++ b/solution.py
@@ -25,7 +25,6 @@
 CHUNKS = 8
 MIB = 1 << 20
 COVER = pl.CostEstimate(flops=8*10**8, bytes_accessed=8 << 20, transcendentals=0)
-ALL_VMEM = 67043328
 
 
 def exchanged(pieces, axis=BLK):
@@ -42,6 +41,10 @@
         cost_estimate=COVER,
         name=kernel.__name__,
     )(*pieces)
+
+
+def in_hbm(array):
+    return pltpu.with_memory_space_constraint(array, pltpu.HBM)
 
 
 def params(mib):
@@ -436,9 +439,18 @@
             pltpu.VMEM((slots * QUERY_HEADS, HEAD_SIZE), jnp.float32),
             pltpu.SemaphoreType.DMA((5 + 2 * (slots + prefixes) // BATCH,)),
         ],
-        compiler_params=pltpu.CompilerParams(vmem_limit_bytes=ALL_VMEM),
+        compiler_params=params(24),
         name="attention",
-    )(first, cache_len, insert_slot, prefix_len, queries, out_weight.T, cache_kv, inserted_key_value)
+    )(
+        first,
+        in_hbm(cache_len),
+        in_hbm(insert_slot),
+        in_hbm(prefix_len),
+        in_hbm(queries),
+        in_hbm(out_weight.T),
+        in_hbm(cache_kv),
+        in_hbm(inserted_key_value),
+    )
     along, across, pair = BLK
     copies = lax.axis_size(across)
     landed = exchanged(partials, along)
@@ -481,7 +493,7 @@
             pltpu.VMEM((2, gate_up.shape[2], width), bf16),
             pltpu.SemaphoreType.DMA((CHUNKS,)),
         ],
-        compiler_params=params(50),
+        compiler_params=params(24),
         name="experts",
     )(
         expert,
@@ -490,7 +502,7 @@
         norm_gain,
         router_weight.T,
         expert_ids.T,
-        jnp.swapaxes(gate_up, 1, 2),
+        in_hbm(jnp.swapaxes(gate_up, 1, 2)),
         down_proj,
     )
     other = lax.ppermute(other, pair, [(0, 1), (1, 0)])

time: 97.5 us -> 95.7 us (0.982)
  no operation moved by 1% of the time
where the time goes in v8:
time: 95.7 us; the launch traced here: 95.3 us
  blocking collectives  81.4 us (85%)
  Pallas kernels  7.38 us (8%)
  starting transfers between devices  4.42 us (5%)
  waiting for transfers between devices  2.07 us (2%)
    all_to_all x5, blocking collectives, exchanged(): return lax.all_to_all(pieces, axis, 0, 0, tiled=True)  81.4 us
    ppermute x1, starting transfers between devices, on_device(): other = lax.ppermute(part, pair, [(0, 1), (1, 0)])  4.28 us
    pallas_call x1, Pallas kernels, on_device(): pl.pallas_call(functools.partial(experts_kernel, share), out_shape=(jax.S...  2.99 us
    pallas_call x1, Pallas kernels, on_device(): pl.pallas_call(functools.partial(attention_kernel, devices * ctx_rows), o...  2.73 us
  transfers between devices with their start and end apart: 2, of which 2 were waited for; matrix products, arithmetic and copies ran while one was open for 0% of the time, Pallas kernels for 0%

profile of v8, /device:TPU:513, one launch (start us, length us, event | category | flops | bytes accessed | tf_op | source)
XLA Modules:
  0.0 95.3 jit_solution(5637331418082577270)
XLA Ops:
  0.0 2.7 %attention.1 = bf16[8,208,128]{2,1,0:T(8,128)(2,1)S(1)} custom-call(s32[1]{0:T(128)} %bitcast.first, s32[16]{0:T(128)} %lengths_in.1, s32[8]{0:T(128)} %insert_slot_in.1, s32[8]{0:T(128)} %prefix_len_in.1, bf16[16,4096]{1,0:T(8,128)(2,1)} %queries_in.1, bf16[32,4096]{1,0:T(8,128)(2,1)} %bitcast.13, bf16[2,16,32,1024]{3,2,1,0:T(8,128)(2,1)} %cache.1, ...), custom_call_target="tpu_custom_call" | custom-call | tf_op jit(solution)/shard_map/attention/pallas_call | solution.py:424
  2.7 18.7 %all_to_all.25.pieces.landed = bf16[8,208,128]{2,1,0:T(8,128)(2,1)S(1)} all-to-all(bf16[8,208,128]{2,1,0:T(8,128)(2,1)S(1)} %attention.1), channel_id=1, replica_groups=mesh['rep'=2,'blk_0'=8,'blk_1'=8,'blk_2'=2] {'blk_0'}, dimensions={0} | all-to-all | bytes 851968 | tf_op jit(solution)/shard_map/all_to_all | solution.py:31
  21.5 0.3 spread_kernel.1
  21.7 0.0 copy-start.4
  21.7 24.1 %all_to_all.26.pieces = bf16[8,80,128]{2,1,0:T(8,128)(2,1)S(1)} all-to-all(bf16[8,80,128]{2,1,0:T(8,128)(2,1)S(1)} %spread_kernel.1), channel_id=1, replica_groups=mesh['rep'=2,'blk_0'=8,'blk_1'=8,'blk_2'=2] {'blk_1'}, dimensions={0} | all-to-all | bytes 327680 | tf_op jit(solution)/shard_map/all_to_all | solution.py:31
  45.9 0.3 part_kernel.1.mine
  46.1 4.3 %collective-permute-start = (bf16[80,128]{1,0:T(8,128)(2,1)S(1)}, bf16[80,128]{1,0:T(8,128)(2,1)S(1)}, u32[]{:S(2)}, u32[]{:S(2)}) collective-permute-start(bf16[80,128]{1,0:T(8,128)(2,1)S(1)} %part_kernel.1.mine), channel_id=1, source_target_pairs={{0,1},{1,0},{2,3},{3,2},{4,5},{5,4},{6,7},{7,6},{8,9},{9,8},{10,11... | collective-permute-start | bytes 61448 | tf_op jit(solution)/shard_map/ppermute | solution.py:459
  50.4 0.8 collective-permute-done.other
  51.2 0.0 copy-done.4
  51.2 0.3 project.1
  51.5 0.0 copy-start
  51.6 0.0 copy-start.1
  51.6 0.0 copy-start.2
  51.6 0.0 copy-start.3
  51.6 9.7 %all_to_all.27.pieces = bf16[8,16,256]{2,1,0:T(8,128)(2,1)S(1)} all-to-all(bf16[8,16,256]{2,1,0:T(8,128)(2,1)S(1)} %project.1), channel_id=1, replica_groups=mesh['rep'=2,'blk_0'=8,'blk_1'=8,'blk_2'=2] {'blk_0'}, dimensions={0} | all-to-all | bytes 131072 | tf_op jit(solution)/shard_map/all_to_all | solution.py:31
  61.3 0.1 mixed.1
  61.4 13.3 %all_to_all.28.gathered = bf16[16,16,256]{2,1,0:T(8,128)(2,1)S(1)} all-to-all(bf16[16,16,256]{2,1,0:T(8,128)(2,1)S(1)} %get-tuple-element.17), channel_id=1, replica_groups=mesh['rep'=2,'blk_0'=8,'blk_1'=8,'blk_2'=2] {'blk_1','blk_2'}, dimensions={0} | all-to-all | bytes 262144 | tf_op jit(solution)/shard_map/all_to_all | solution.py:31
  74.6 0.0 copy-done
  74.6 0.0 copy-done.1
  74.6 0.0 copy-done.2
  74.6 0.0 copy-done.3
  74.7 3.0 %experts.1 = (f32[32,8,128]{2,1,0:T(8,128)S(1)}, bf16[32,8,128]{2,1,0:T(8,128)(2,1)S(1)}) custom-call(s32[1]{0:T(128)} %bitcast.2.expert, s32[1]{0:T(128)} %bitcast.3.core, bf16[16,16,256]{2,1,0:T(8,128)(2,1)S(1)} %all_to_all.28.gathered, bf16[4096]{0:T(1024)(128)(2,1)S(1)} %copy-done.2, bf16[4,4096]{1,0:T(4,128)(2,1)S(1)} %bitcast.10, ...), custom_call_target="tpu_custom_call" | custom-call | tf_op jit(solution)/shard_map/experts/pallas_call | solution.py:484
  77.6 0.1 collective-permute-start.1
  77.8 1.2 %collective-permute-done.1.other = bf16[32,8,128]{2,1,0:T(8,128)(2,1)S(1)} collective-permute-done((bf16[32,8,128]{2,1,0:T(8,128)(2,1)S(1)}, bf16[32,8,128]{2,1,0:T(8,128)(2,1)S(1)}, u32[]{:S(2)}, u32[]{:S(2)}) %collective-permute-start.1) | collective-permute-done | bytes 65568 | tf_op jit(solution)/shard_map/ppermute | solution.py:508
  79.0 15.6 %all_to_all.29.pieces = bf16[64,4,128]{2,1,0:T(4,128)(2,1)S(1)} all-to-all(bf16[64,4,128]{2,1,0:T(4,128)(2,1)S(1)} %bitcast.9), channel_id=1, replica_groups=mesh['rep'=2,'blk_0'=8,'blk_1'=8,'blk_2'=2] {'blk_0','blk_1'}, dimensions={0} | all-to-all | bytes 131072 | tf_op jit(solution)/shard_map/all_to_all | solution.py:31
  94.6 0.7 final.1
  (1 shorter events, 0.0 us)
Async XLA Ops:
  21.7 29.5 %copy-start.4 = (bf16[16,32]{1,0:T(8,128)(2,1)S(1)}, bf16[16,32]{1,0:T(8,128)(2,1)}, u32[]{:S(2)}) copy-start(bf16[16,32]{1,0:T(8,128)(2,1)} %hidden.1) | copy-start | bytes 3076
  46.1 5.1 %collective-permute-start = (bf16[80,128]{1,0:T(8,128)(2,1)S(1)}, bf16[80,128]{1,0:T(8,128)(2,1)S(1)}, u32[]{:S(2)}, u32[]{:S(2)}) collective-permute-start(bf16[80,128]{1,0:T(8,128)(2,1)S(1)} %part_kernel.1.mine), channel_id=1, source_target_pairs={{0,1},{1,0},{2,3},{3,2},{4,5},{5,4},{6,7},{7,6},{8,9},{9,8},{10,11... | collective-permute-start | bytes 61448 | tf_op jit(solution)/shard_map/ppermute | solution.py:459
  51.5 23.1 %copy-start = (bf16[224,4096]{1,0:T(8,128)(2,1)S(1)}, bf16[224,4096]{1,0:T(8,128)(2,1)}, u32[]{:S(2)}) copy-start(bf16[224,4096]{1,0:T(8,128)(2,1)} %down.1) | copy-start | bytes 5505028
  51.6 23.1 %copy-start.1 = (bf16[4096,4]{0,1:T(4,128)(2,1)S(1)}, bf16[4096,4]{0,1:T(4,128)(2,1)}, u32[]{:S(2)}) copy-start(bf16[4096,4]{0,1:T(4,128)(2,1)} %param.22) | copy-start | bytes 98308
  51.6 23.1 %copy-start.2 = (bf16[4096]{0:T(1024)(128)(2,1)S(1)}, bf16[4096]{0:T(1024)(128)(2,1)}, u32[]{:S(2)}) copy-start(bf16[4096]{0:T(1024)(128)(2,1)} %gain.1) | copy-start | bytes 24580
  51.6 23.1 %copy-start.3 = (s32[16,2]{0,1:T(2,128)S(1)}, s32[16,2]{0,1:T(2,128)}, u32[]{:S(2)}) copy-start(s32[16,2]{0,1:T(2,128)} %param.23) | copy-start | bytes 388
  77.6 1.4 %collective-permute-start.1 = (bf16[32,8,128]{2,1,0:T(8,128)(2,1)S(1)}, bf16[32,8,128]{2,1,0:T(8,128)(2,1)S(1)}, u32[]{:S(2)}, u32[]{:S(2)}) collective-permute-start(bf16[32,8,128]{2,1,0:T(8,128)(2,1)S(1)} %get-tuple-element.19), channel_id=1, source_target_pairs={{0,1},{1,0},{2,3},{3,2},{4,5},{5,4},{6,7},{7,6},{8,9},{9,8},{10,11... | collective-permute-start | bytes 196616 | tf_op jit(solution)/shard_map/ppermute | solution.py:508

commit v9 on v8

--- a/solution.py
+++ b/solution.py
@@ -22,7 +22,6 @@
 IN_SMEM = pl.BlockSpec(memory_space=pltpu.SMEM)
 IN_HBM = pl.BlockSpec(memory_space=pltpu.HBM)
 BATCH = 4
-CHUNKS = 8
 MIB = 1 << 20
 COVER = pl.CostEstimate(flops=8*10**8, bytes_accessed=8 << 20, transcendentals=0)
 
@@ -312,19 +311,9 @@
 
 
 def experts_kernel(
-    share, expert, core, gathered, gain, router, chosen, gate_up_in, down, own, other, gate_up, sems
+    share, expert, core, gathered, gain, router, chosen, gate_up, down, own, other
 ):
     blocks, slots = own.shape[0], 2 * own.shape[1]
-    step = blocks * LANES // CHUNKS
-    copies = []
-    for i in range(CHUNKS):
-        lanes = pl.ds(i * step, step)
-        copies.append(
-            pltpu.make_async_copy(
-                gate_up_in.at[:, :, lanes], gate_up.at[:, :, lanes], sems.at[i]
-            )
-        )
-        copies[i].start()
     mixed = in_feature_order(gathered, share)
     scale = lax.rsqrt(jnp.sum(mixed * mixed, axis=1, keepdims=True) / (blocks * LANES) + 1e-05)
     normed = (mixed * scale * gain[...].astype(jnp.float32).reshape(1, blocks * LANES)).astype(jnp.bfloat16)
@@ -348,18 +337,12 @@
     gates = [jax.nn.sigmoid(picked[i] - picked[1 - i]) for i in range(2)]
     mine = expert[0].astype(jnp.float32)
     part = sum(jnp.where(ids[i] == mine, gates[i], 0.0) for i in range(2))
-    gate, up = 0.0, 0.0
-    for i in range(CHUNKS):
-        copies[i].wait()
-        lanes = slice(i * step, (i + 1) * step)
-        contract = functools.partial(
-            lax.dot_general,
-            normed[:, lanes],
-            dimension_numbers=(((1,), (1,)), ((), ())),
-            preferred_element_type=jnp.float32,
+    gate, up = [
+        lax.dot_general(
+            normed, gate_up[i], (((1,), (1,)), ((), ())), preferred_element_type=jnp.float32
         )
-        gate = gate + contract(gate_up[0, :, lanes])
-        up = up + contract(gate_up[1, :, lanes])
+        for i in range(2)
+    ]
     act = (gate * jax.nn.sigmoid(gate) * up).astype(jnp.bfloat16)
     term = part * jnp.dot(act, down[...], preferred_element_type=jnp.float32)
     tiles = [term[None, :, k * LANES : (k + 1) * LANES] for k in range(blocks)]
@@ -487,12 +470,8 @@
             jax.ShapeDtypeStruct((blocks, slots // 2, LANES), jnp.float32),
             jax.ShapeDtypeStruct((blocks, slots // 2, LANES), bf16),
         ),
-        in_specs=[IN_SMEM] * 2 + [IN_VMEM] * 4 + [IN_HBM, IN_VMEM],
+        in_specs=[IN_SMEM] * 2 + [IN_VMEM] * 6,
         out_specs=(IN_VMEM, IN_VMEM),
-        scratch_shapes=[
-            pltpu.VMEM((2, gate_up.shape[2], width), bf16),
-            pltpu.SemaphoreType.DMA((CHUNKS,)),
-        ],
         compiler_params=params(24),
         name="experts",
     )(
@@ -502,7 +481,7 @@
         norm_gain,
         router_weight.T,
         expert_ids.T,
-        in_hbm(jnp.swapaxes(gate_up, 1, 2)),
+        jnp.swapaxes(gate_up, 1, 2),
         down_proj,
     )
     other = lax.ppermute(other, pair, [(0, 1), (1, 0)])

time: 95.7 us -> 94.6 us (0.989)
  Pallas kernels: 7.38 us -> 6.17 us
    pallas_call x1, Pallas kernels: 2.99 us -> 1.77 us  [on_device(): pl.pallas_call(functools.partial(experts_kernel, share), out_shape=(jax.S...]
where the time goes in v9:
time: 94.6 us; the launch traced here: 94.3 us
  blocking collectives  81.5 us (86%)
  Pallas kernels  6.17 us (7%)
  starting transfers between devices  4.42 us (5%)
  waiting for transfers between devices  2.07 us (2%)
    all_to_all x5, blocking collectives, exchanged(): return lax.all_to_all(pieces, axis, 0, 0, tiled=True)  81.5 us
    ppermute x1, starting transfers between devices, on_device(): other = lax.ppermute(part, pair, [(0, 1), (1, 0)])  4.28 us
    pallas_call x1, Pallas kernels, on_device(): pl.pallas_call(functools.partial(attention_kernel, devices * ctx_rows), o...  2.73 us
  transfers between devices with their start and end apart: 2, of which 2 were waited for; matrix products, arithmetic and copies ran while one was open for 0% of the time, Pallas kernels for 0%

profile of v9, /device:TPU:513, one launch (start us, length us, event | category | flops | bytes accessed | tf_op | source)
XLA Modules:
  0.0 94.3 jit_solution(12586349173117119810)
XLA Ops:
  0.0 2.7 %attention.1 = bf16[8,208,128]{2,1,0:T(8,128)(2,1)S(1)} custom-call(s32[1]{0:T(128)} %bitcast.first, s32[16]{0:T(128)} %lengths_in.1, s32[8]{0:T(128)} %insert_slot_in.1, s32[8]{0:T(128)} %prefix_len_in.1, bf16[16,4096]{1,0:T(8,128)(2,1)} %queries_in.1, bf16[32,4096]{1,0:T(8,128)(2,1)} %bitcast.13, bf16[2,16,32,1024]{3,2,1,0:T(8,128)(2,1)} %cache.1, ...), custom_call_target="tpu_custom_call" | custom-call | tf_op jit(solution)/shard_map/attention/pallas_call | solution.py:407
  2.7 18.7 %all_to_all.25.pieces.landed = bf16[8,208,128]{2,1,0:T(8,128)(2,1)S(1)} all-to-all(bf16[8,208,128]{2,1,0:T(8,128)(2,1)S(1)} %attention.1), channel_id=1, replica_groups=mesh['rep'=2,'blk_0'=8,'blk_1'=8,'blk_2'=2] {'blk_0'}, dimensions={0} | all-to-all | bytes 851968 | tf_op jit(solution)/shard_map/all_to_all | solution.py:30
  21.5 0.3 spread_kernel.1
  21.7 0.0 copy-start.5
  21.7 24.1 %all_to_all.26.pieces = bf16[8,80,128]{2,1,0:T(8,128)(2,1)S(1)} all-to-all(bf16[8,80,128]{2,1,0:T(8,128)(2,1)S(1)} %spread_kernel.1), channel_id=1, replica_groups=mesh['rep'=2,'blk_0'=8,'blk_1'=8,'blk_2'=2] {'blk_1'}, dimensions={0} | all-to-all | bytes 327680 | tf_op jit(solution)/shard_map/all_to_all | solution.py:30
  45.9 0.3 part_kernel.1.mine
  46.1 4.3 %collective-permute-start = (bf16[80,128]{1,0:T(8,128)(2,1)S(1)}, bf16[80,128]{1,0:T(8,128)(2,1)S(1)}, u32[]{:S(2)}, u32[]{:S(2)}) collective-permute-start(bf16[80,128]{1,0:T(8,128)(2,1)S(1)} %part_kernel.1.mine), channel_id=1, source_target_pairs={{0,1},{1,0},{2,3},{3,2},{4,5},{5,4},{6,7},{7,6},{8,9},{9,8},{10,11... | collective-permute-start | bytes 61448 | tf_op jit(solution)/shard_map/ppermute | solution.py:442
  50.4 0.8 collective-permute-done.other
  51.2 0.0 copy-done.5
  51.2 0.0 copy-start
  51.3 0.3 project.1
  51.5 0.0 copy-start.1
  51.6 0.0 copy-start.2
  51.6 0.0 copy-start.3
  51.6 0.0 copy-start.4
  51.6 9.8 %all_to_all.27.pieces = bf16[8,16,256]{2,1,0:T(8,128)(2,1)S(1)} all-to-all(bf16[8,16,256]{2,1,0:T(8,128)(2,1)S(1)} %project.1), channel_id=1, replica_groups=mesh['rep'=2,'blk_0'=8,'blk_1'=8,'blk_2'=2] {'blk_0'}, dimensions={0} | all-to-all | bytes 131072 | tf_op jit(solution)/shard_map/all_to_all | solution.py:30
  61.4 0.1 mixed.1
  61.5 13.3 %all_to_all.28.gathered = bf16[16,16,256]{2,1,0:T(8,128)(2,1)S(1)} all-to-all(bf16[16,16,256]{2,1,0:T(8,128)(2,1)S(1)} %get-tuple-element.17), channel_id=1, replica_groups=mesh['rep'=2,'blk_0'=8,'blk_1'=8,'blk_2'=2] {'blk_1','blk_2'}, dimensions={0} | all-to-all | bytes 262144 | tf_op jit(solution)/shard_map/all_to_all | solution.py:30
  74.8 0.0 copy-done
  74.8 0.0 copy-done.1
  74.8 0.0 copy-done.2
  74.8 0.0 copy-done.3
  74.8 0.0 copy-done.4
  74.8 1.8 %experts.1 = (f32[32,8,128]{2,1,0:T(8,128)S(1)}, bf16[32,8,128]{2,1,0:T(8,128)(2,1)S(1)}) custom-call(s32[1]{0:T(128)} %bitcast.2.expert, s32[1]{0:T(128)} %bitcast.3.core, bf16[16,16,256]{2,1,0:T(8,128)(2,1)S(1)} %all_to_all.28.gathered, bf16[4096]{0:T(1024)(128)(2,1)S(1)} %copy-done.3, bf16[4,4096]{1,0:T(4,128)(2,1)S(1)} %bitcast.11, ...), custom_call_target="tpu_custom_call" | custom-call | tf_op jit(solution)/shard_map/experts/pallas_call | solution.py:467
  76.6 0.1 collective-permute-start.1
  76.7 1.2 %collective-permute-done.1.other = bf16[32,8,128]{2,1,0:T(8,128)(2,1)S(1)} collective-permute-done((bf16[32,8,128]{2,1,0:T(8,128)(2,1)S(1)}, bf16[32,8,128]{2,1,0:T(8,128)(2,1)S(1)}, u32[]{:S(2)}, u32[]{:S(2)}) %collective-permute-start.1) | collective-permute-done | bytes 65568 | tf_op jit(solution)/shard_map/ppermute | solution.py:487
  78.0 15.6 %all_to_all.29.pieces = bf16[64,4,128]{2,1,0:T(4,128)(2,1)S(1)} all-to-all(bf16[64,4,128]{2,1,0:T(4,128)(2,1)S(1)} %bitcast.10), channel_id=1, replica_groups=mesh['rep'=2,'blk_0'=8,'blk_1'=8,'blk_2'=2] {'blk_0','blk_1'}, dimensions={0} | all-to-all | bytes 131072 | tf_op jit(solution)/shard_map/all_to_all | solution.py:30
  93.5 0.7 final.1
  (1 shorter events, 0.0 us)
Async XLA Ops:
  21.7 29.5 %copy-start.5 = (bf16[16,32]{1,0:T(8,128)(2,1)S(1)}, bf16[16,32]{1,0:T(8,128)(2,1)}, u32[]{:S(2)}) copy-start(bf16[16,32]{1,0:T(8,128)(2,1)} %hidden.1) | copy-start | bytes 3076
  46.1 5.1 %collective-permute-start = (bf16[80,128]{1,0:T(8,128)(2,1)S(1)}, bf16[80,128]{1,0:T(8,128)(2,1)S(1)}, u32[]{:S(2)}, u32[]{:S(2)}) collective-permute-start(bf16[80,128]{1,0:T(8,128)(2,1)S(1)} %part_kernel.1.mine), channel_id=1, source_target_pairs={{0,1},{1,0},{2,3},{3,2},{4,5},{5,4},{6,7},{7,6},{8,9},{9,8},{10,11... | collective-permute-start | bytes 61448 | tf_op jit(solution)/shard_map/ppermute | solution.py:442
  51.2 23.5 %copy-start = (bf16[2,4096,224]{1,2,0:T(8,128)(2,1)S(1)}, bf16[2,4096,224]{1,2,0:T(8,128)(2,1)}, u32[]{:S(2)}) copy-start(bf16[2,4096,224]{1,2,0:T(8,128)(2,1)} %param.24) | copy-start | bytes 11010052
  51.5 23.2 %copy-start.1 = (bf16[224,4096]{1,0:T(8,128)(2,1)S(1)}, bf16[224,4096]{1,0:T(8,128)(2,1)}, u32[]{:S(2)}) copy-start(bf16[224,4096]{1,0:T(8,128)(2,1)} %down.1) | copy-start | bytes 5505028
  51.6 23.2 %copy-start.2 = (bf16[4096,4]{0,1:T(4,128)(2,1)S(1)}, bf16[4096,4]{0,1:T(4,128)(2,1)}, u32[]{:S(2)}) copy-start(bf16[4096,4]{0,1:T(4,128)(2,1)} %param.22) | copy-start | bytes 98308
  51.6 23.2 %copy-start.3 = (bf16[4096]{0:T(1024)(128)(2,1)S(1)}, bf16[4096]{0:T(1024)(128)(2,1)}, u32[]{:S(2)}) copy-start(bf16[4096]{0:T(1024)(128)(2,1)} %gain.1) | copy-start | bytes 24580
  51.6 23.2 %copy-start.4 = (s32[16,2]{0,1:T(2,128)S(1)}, s32[16,2]{0,1:T(2,128)}, u32[]{:S(2)}) copy-start(s32[16,2]{0,1:T(2,128)} %param.23) | copy-start | bytes 388
  76.6 1.4 %collective-permute-start.1 = (bf16[32,8,128]{2,1,0:T(8,128)(2,1)S(1)}, bf16[32,8,128]{2,1,0:T(8,128)(2,1)S(1)}, u32[]{:S(2)}, u32[]{:S(2)}) collective-permute-start(bf16[32,8,128]{2,1,0:T(8,128)(2,1)S(1)} %get-tuple-element.19), channel_id=1, source_target_pairs={{0,1},{1,0},{2,3},{3,2},{4,5},{5,4},{6,7},{7,6},{8,9},{9,8},{10,11... | collective-permute-start | bytes 196616 | tf_op jit(solution)/shard_map/ppermute | solution.py:487

commit v10 on v9

--- a/solution.py
+++ b/solution.py
@@ -17,7 +17,9 @@
 BLK = ("blk_0", "blk_1", "blk_2")
 GROUP = QUERY_HEADS // KEY_VALUE_HEADS
 LANES = 128
-SPAN = LANES // GROUP
+HEADS = 2
+PARTS = QUERY_HEADS // HEADS
+SPAN = LANES // HEADS
 IN_VMEM = pl.BlockSpec(memory_space=pltpu.VMEM)
 IN_SMEM = pl.BlockSpec(memory_space=pltpu.SMEM)
 IN_HBM = pl.BlockSpec(memory_space=pltpu.HBM)
@@ -126,7 +128,7 @@
     )
     row = lax.broadcasted_iota(jnp.int32, (wide, HEAD_SIZE), 0)
     lane = lax.broadcasted_iota(jnp.int32, (wide, HEAD_SIZE), 1)
-    counted = lane // SPAN == row % GROUP
+    counted = lane // SPAN == row % HEADS
     early = lax.broadcasted_iota(jnp.int32, (2 * GROUP, HEAD_SIZE), 0) < GROUP
     place = lax.broadcasted_iota(jnp.int32, (wide, count), 1)
     for s in range(slots):
@@ -175,16 +177,16 @@
             stats[pl.ds(s, wide, stride=slots), :] = jnp.where(
                 counted, packed_stats(lane, peak, total), 0.0
             )
-    deep = GROUP * slots
+    deep = HEADS * slots
     copies[-1].wait()
-    for g in range(KEY_VALUE_HEADS):
-        out[g, :deep, :] = values[g * deep : (g + 1) * deep, :].astype(jnp.bfloat16)
-        one = [stats[g * deep + h * slots : g * deep + (h + 1) * slots, :] for h in range(GROUP)]
-        out[g, deep : deep + slots, :] = sum(one).astype(jnp.bfloat16)
-        for h in range(GROUP):
+    for o in range(PARTS):
+        out[o, :deep, :] = values[o * deep : (o + 1) * deep, :].astype(jnp.bfloat16)
+        one = [stats[o * deep + h * slots : o * deep + (h + 1) * slots, :] for h in range(HEADS)]
+        out[o, deep : deep + slots, :] = sum(one).astype(jnp.bfloat16)
+        for h in range(HEADS):
             at = deep + slots + h * weight.shape[0]
-            head = (g * GROUP + h) * HEAD_SIZE
-            out[g, at : at + weight.shape[0], :] = weight[:, head : head + HEAD_SIZE]
+            head = (o * HEADS + h) * HEAD_SIZE
+            out[o, at : at + weight.shape[0], :] = weight[:, head : head + HEAD_SIZE]
 
 
 def packed_stats(lane, peak, total):
@@ -196,8 +198,8 @@
 
 
 def merge(pieces):
-    slots = pieces[0].shape[0] // (GROUP + 1)
-    found = [x[GROUP * slots :].astype(jnp.float32) for x in pieces]
+    slots = pieces[0].shape[0] // (HEADS + 1)
+    found = [x[HEADS * slots :].astype(jnp.float32) for x in pieces]
     highest = functools.reduce(jnp.maximum, found)
     scales = [
         jnp.exp(x - highest)
@@ -210,7 +212,7 @@
     total = sum(scales)
     safe = jnp.where(total > 0.0, total, 1.0)
     values = []
-    for h in range(GROUP):
+    for h in range(HEADS):
         column = slice(h * SPAN, h * SPAN + 1)
         parts = [
             x[h * slots : (h + 1) * slots].astype(jnp.float32) * y[:, column]
@@ -237,19 +239,16 @@
         out[i] = part
 
 
-def part_kernel(pieces, out):
-    out[...] = whole_part([pieces[i] for i in range(pieces.shape[0])])
-
-
-def project_kernel(place, mine, other, landed, hidden, out):
+def project_kernel(place, pieces, landed, hidden, out):
     slots, columns = hidden.shape
-    count, deep = landed.shape[0], mine.shape[0]
-    values, _, _ = merge([mine[...], other[...]])
+    count, deep = landed.shape[0], pieces.shape[1]
+    values, _, _ = merge([pieces[i] for i in range(pieces.shape[0])])
     attn = jnp.concatenate(values, axis=1).astype(jnp.bfloat16)
+    order = [i for core in range(2) for i in range(core, count, 2)]
     heads = []
-    for h in range(GROUP):
+    for h in range(HEADS):
         at = deep + h * columns
-        parts = [landed[i, at : at + columns, :] for i in range(count)]
+        parts = [landed[i, at : at + columns, :] for i in order]
         heads.append(jnp.concatenate(parts, axis=0))
     weight = jnp.concatenate(heads, axis=1)
     total = lax.dot_general(
@@ -258,8 +257,9 @@
     tiled = jnp.concatenate([hidden[...].astype(jnp.float32)] * count, axis=1)
     owner = lax.broadcasted_iota(jnp.int32, tiled.shape, 1) // columns
     part = (total + jnp.where(owner == place[0], tiled, 0.0)).astype(jnp.bfloat16)
+    half = count * columns // 2
     for i in range(count):
-        out[i] = part
+        out[i] = part[:, i % 2 * half : (i % 2 + 1) * half]
 
 
 def mixed_kernel(place, pieces, own, out):
@@ -270,7 +270,9 @@
     mixed = total.astype(jnp.bfloat16)
     for i in range(out.shape[0]):
         out[i] = mixed
-    mine = [total[:, i * columns : (i + 1) * columns] for i in range(pieces.shape[0])]
+    mine = [
+        total[:, i * columns : (i + 1) * columns] for i in range(total.shape[1] // columns)
+    ]
     own[...] = sum(jnp.where(place[0] == i, x, 0.0) for i, x in enumerate(mine)).astype(
         jnp.bfloat16
     )
@@ -394,7 +396,7 @@
     ctx_rows, kv_width = cache_kv.shape[2:]
     prefixes = insert_slot.shape[0]
     share = LANES // columns
-    deep = slots * (GROUP + 1)
+    deep = slots * (HEADS + 1)
     width = devices * columns
     blocks = width // LANES
     bf16 = jnp.bfloat16
@@ -403,10 +405,13 @@
     place = lax.axis_index(BLK[0]).astype(jnp.int32).reshape(1)
     expert = (dev_index * gate_up.shape[2] // FF).astype(jnp.int32).reshape(1)
     core = lax.axis_index(BLK[2]).astype(jnp.int32).reshape(1)
-    first, place, expert, core = lax.optimization_barrier((first, place, expert, core))
+    block = core * lax.axis_size(BLK[0]) + place
+    first, place, expert, core, block = lax.optimization_barrier(
+        (first, place, expert, core, block)
+    )
     partials = pl.pallas_call(
         functools.partial(attention_kernel, devices * ctx_rows),
-        out_shape=jax.ShapeDtypeStruct((KEY_VALUE_HEADS, deep + GROUP * columns, HEAD_SIZE), bf16),
+        out_shape=jax.ShapeDtypeStruct((PARTS, deep + HEADS * columns, HEAD_SIZE), bf16),
         in_specs=[IN_SMEM] + [IN_HBM] * 7,
         out_specs=IN_VMEM,
         scratch_shapes=[
@@ -436,20 +441,18 @@
     )
     along, across, pair = BLK
     copies = lax.axis_size(across)
-    landed = exchanged(partials, along)
+    landed = exchanged(partials, (along, pair))
     part = merging(spread_kernel, (copies, deep, HEAD_SIZE), landed)
-    part = merging(part_kernel, (deep, HEAD_SIZE), exchanged(part, across))
-    other = lax.ppermute(part, pair, [(0, 1), (1, 0)])
     count = lax.axis_size(along)
     parts = pl.pallas_call(
         project_kernel,
-        out_shape=jax.ShapeDtypeStruct((count, slots, count * columns), bf16),
-        in_specs=[IN_SMEM] + [IN_VMEM] * 4,
+        out_shape=jax.ShapeDtypeStruct((2 * count, slots, count * columns), bf16),
+        in_specs=[IN_SMEM] + [IN_VMEM] * 3,
         out_specs=IN_VMEM,
         compiler_params=params(8),
         cost_estimate=COVER,
         name="project",
-    )(place, part, other, landed, hidden)
+    )(block, exchanged(part, across), landed, hidden)
     local_mixed, packed = pl.pallas_call(
         mixed_kernel,
         out_shape=(
@@ -461,7 +464,7 @@
         compiler_params=params(8),
         cost_estimate=COVER,
         name="mixed",
-    )(place, exchanged(parts, along))
+    )(place, exchanged(parts, (along, pair)))
     gathered = exchanged(packed, (across, pair))
 
     own, other = pl.pallas_call(

time: 94.6 us -> 96.8 us (1.023)
  blocking collectives: 81.5 us -> 89.1 us
  starting transfers between devices: 4.42 us -> 0.14 us
    all_to_all x5, blocking collectives: 81.5 us -> 89.1 us  [exchanged(): return lax.all_to_all(pieces, axis, 0, 0, tiled=True)]
    ppermute x1 -> x0, starting transfers between devices: 4.28 us -> none  [on_device(): other = lax.ppermute(part, pair, [(0, 1), (1, 0)])]
  transfers between devices with their start and end apart: 2 -> 1, of which waited for: 2 -> 1; matrix products, arithmetic and copies ran while one was open for 0% -> 0% of each run, Pallas kernels for 0% -> 0%
where the time goes in v10:
time: 96.8 us; the launch traced here: 96.5 us
  blocking collectives  89.1 us (92%)
  Pallas kernels  5.92 us (6%)
  waiting for transfers between devices  1.23 us (1%)
    all_to_all x5, blocking collectives, exchanged(): return lax.all_to_all(pieces, axis, 0, 0, tiled=True)  89.1 us
    pallas_call x1, Pallas kernels, on_device(): pl.pallas_call(functools.partial(attention_kernel, devices * ctx_rows), o...  2.72 us
  transfers between devices with their start and end apart: 1, of which 1 were waited for; matrix products, arithmetic and copies ran while one was open for 0% of the time, Pallas kernels for 0%

profile of v10, /device:TPU:513, one launch (start us, length us, event | category | flops | bytes accessed | tf_op | source)
XLA Modules:
  0.0 96.5 jit_solution(3176121961953948353)
XLA Ops:
  0.0 2.7 %attention.1 = bf16[16,112,128]{2,1,0:T(8,128)(2,1)S(1)} custom-call(s32[1]{0:T(128)} %bitcast.first, s32[16]{0:T(128)} %lengths_in.1, s32[8]{0:T(128)} %insert_slot_in.1, s32[8]{0:T(128)} %prefix_len_in.1, bf16[16,4096]{1,0:T(8,128)(2,1)} %queries_in.1, bf16[32,4096]{1,0:T(8,128)(2,1)} %bitcast.13, bf16[2,16,32,1024]{3,2,1,0:T(8,128)(2,1)} %cache.1, ...), custom_call_target="tpu_custom_call" | custom-call | tf_op jit(solution)/shard_map/attention/pallas_call | solution.py:412
  2.7 0.0 copy-start.5
  2.7 38.7 %all_to_all.25.pieces.landed = bf16[16,112,128]{2,1,0:T(8,128)(2,1)S(1)} all-to-all(bf16[16,112,128]{2,1,0:T(8,128)(2,1)S(1)} %attention.1), channel_id=1, replica_groups=mesh['rep'=2,'blk_0'=8,'blk_1'=8,'blk_2'=2] {'blk_0','blk_2'}, dimensions={0} | all-to-all | bytes 917504 | tf_op jit(solution)/shard_map/all_to_all | solution.py:32
  41.4 0.3 spread_kernel.1
  41.7 10.7 %all_to_all.26.pieces = bf16[8,48,128]{2,1,0:T(8,128)(2,1)S(1)} all-to-all(bf16[8,48,128]{2,1,0:T(8,128)(2,1)S(1)} %spread_kernel.1), channel_id=1, replica_groups=mesh['rep'=2,'blk_0'=8,'blk_1'=8,'blk_2'=2] {'blk_1'}, dimensions={0} | all-to-all | bytes 196608 | tf_op jit(solution)/shard_map/all_to_all | solution.py:32
  52.3 0.0 copy-done.5
  52.3 0.0 copy-start
  52.3 0.3 project.1
  52.7 0.0 copy-start.1
  52.7 0.0 copy-start.2
  52.7 0.0 copy-start.3
  52.7 0.0 copy-start.4
  52.7 12.7 %all_to_all.27.pieces = bf16[16,16,256]{2,1,0:T(8,128)(2,1)S(1)} all-to-all(bf16[16,16,256]{2,1,0:T(8,128)(2,1)S(1)} %project.1), channel_id=1, replica_groups=mesh['rep'=2,'blk_0'=8,'blk_1'=8,'blk_2'=2] {'blk_0','blk_2'}, dimensions={0} | all-to-all | bytes 262144 | tf_op jit(solution)/shard_map/all_to_all | solution.py:32
  65.4 0.1 mixed.1
  65.5 11.5 %all_to_all.28.gathered = bf16[16,16,256]{2,1,0:T(8,128)(2,1)S(1)} all-to-all(bf16[16,16,256]{2,1,0:T(8,128)(2,1)S(1)} %get-tuple-element.19), channel_id=1, replica_groups=mesh['rep'=2,'blk_0'=8,'blk_1'=8,'blk_2'=2] {'blk_1','blk_2'}, dimensions={0} | all-to-all | bytes 262144 | tf_op jit(solution)/shard_map/all_to_all | solution.py:32
  77.0 0.0 copy-done
  77.0 0.0 copy-done.1
  77.0 0.0 copy-done.2
  77.0 0.0 copy-done.3
  77.0 0.0 copy-done.4
  77.0 1.8 %experts.1 = (f32[32,8,128]{2,1,0:T(8,128)S(1)}, bf16[32,8,128]{2,1,0:T(8,128)(2,1)S(1)}) custom-call(s32[1]{0:T(128)} %bitcast.2.expert, s32[1]{0:T(128)} %bitcast.3.core, bf16[16,16,256]{2,1,0:T(8,128)(2,1)S(1)} %all_to_all.28.gathered, bf16[4096]{0:T(1024)(128)(2,1)S(1)} %copy-done.3, bf16[4,4096]{1,0:T(4,128)(2,1)S(1)} %bitcast.11, ...), custom_call_target="tpu_custom_call" | custom-call | tf_op jit(solution)/shard_map/experts/pallas_call | solution.py:470
  78.8 0.1 collective-permute-start
  79.0 1.2 %collective-permute-done.other = bf16[32,8,128]{2,1,0:T(8,128)(2,1)S(1)} collective-permute-done((bf16[32,8,128]{2,1,0:T(8,128)(2,1)S(1)}, bf16[32,8,128]{2,1,0:T(8,128)(2,1)S(1)}, u32[]{:S(2)}, u32[]{:S(2)}) %collective-permute-start) | collective-permute-done | bytes 65568 | tf_op jit(solution)/shard_map/ppermute | solution.py:490
  80.2 15.5 %all_to_all.29.pieces = bf16[64,4,128]{2,1,0:T(4,128)(2,1)S(1)} all-to-all(bf16[64,4,128]{2,1,0:T(4,128)(2,1)S(1)} %bitcast.10), channel_id=1, replica_groups=mesh['rep'=2,'blk_0'=8,'blk_1'=8,'blk_2'=2] {'blk_0','blk_1'}, dimensions={0} | all-to-all | bytes 131072 | tf_op jit(solution)/shard_map/all_to_all | solution.py:32
  95.8 0.7 final.1
  (1 shorter events, 0.0 us)
Async XLA Ops:
  2.7 49.6 %copy-start.5 = (bf16[16,32]{1,0:T(8,128)(2,1)S(1)}, bf16[16,32]{1,0:T(8,128)(2,1)}, u32[]{:S(2)}) copy-start(bf16[16,32]{1,0:T(8,128)(2,1)} %hidden.1) | copy-start | bytes 3076
  52.3 24.7 %copy-start = (bf16[2,4096,224]{1,2,0:T(8,128)(2,1)S(1)}, bf16[2,4096,224]{1,2,0:T(8,128)(2,1)}, u32[]{:S(2)}) copy-start(bf16[2,4096,224]{1,2,0:T(8,128)(2,1)} %param.24) | copy-start | bytes 11010052
  52.7 24.3 %copy-start.1 = (bf16[224,4096]{1,0:T(8,128)(2,1)S(1)}, bf16[224,4096]{1,0:T(8,128)(2,1)}, u32[]{:S(2)}) copy-start(bf16[224,4096]{1,0:T(8,128)(2,1)} %down.1) | copy-start | bytes 5505028
  52.7 24.3 %copy-start.2 = (bf16[4096,4]{0,1:T(4,128)(2,1)S(1)}, bf16[4096,4]{0,1:T(4,128)(2,1)}, u32[]{:S(2)}) copy-start(bf16[4096,4]{0,1:T(4,128)(2,1)} %param.22) | copy-start | bytes 98308
  52.7 24.3 %copy-start.3 = (bf16[4096]{0:T(1024)(128)(2,1)S(1)}, bf16[4096]{0:T(1024)(128)(2,1)}, u32[]{:S(2)}) copy-start(bf16[4096]{0:T(1024)(128)(2,1)} %gain.1) | copy-start | bytes 24580
  52.7 24.3 %copy-start.4 = (s32[16,2]{0,1:T(2,128)S(1)}, s32[16,2]{0,1:T(2,128)}, u32[]{:S(2)}) copy-start(s32[16,2]{0,1:T(2,128)} %param.23) | copy-start | bytes 388
  78.8 1.4 %collective-permute-start = (bf16[32,8,128]{2,1,0:T(8,128)(2,1)S(1)}, bf16[32,8,128]{2,1,0:T(8,128)(2,1)S(1)}, u32[]{:S(2)}, u32[]{:S(2)}) collective-permute-start(bf16[32,8,128]{2,1,0:T(8,128)(2,1)S(1)} %get-tuple-element.21), channel_id=1, source_target_pairs={{0,1},{1,0},{2,3},{3,2},{4,5},{5,4},{6,7},{7,6},{8,9},{9,8},{10,11... | collective-permute-start | bytes 196616 | tf_op jit(solution)/shard_map/ppermute | solution.py:490

commit v11 on v9

--- a/solution.py
+++ b/solution.py
@@ -22,6 +22,7 @@
 IN_SMEM = pl.BlockSpec(memory_space=pltpu.SMEM)
 IN_HBM = pl.BlockSpec(memory_space=pltpu.HBM)
 BATCH = 4
+SOFTMAX_BATCH = 8
 MIB = 1 << 20
 COVER = pl.CostEstimate(flops=8*10**8, bytes_accessed=8 << 20, transcendentals=0)
 
@@ -141,8 +142,8 @@
         ) * (1.0 / math.sqrt(HEAD_SIZE))
     for copy in value_copies:
         copy.wait()
-    for batch in range(0, slots, BATCH):
-        several = range(batch, batch + BATCH)
+    for batch in range(0, slots, SOFTMAX_BATCH):
+        several = range(batch, batch + SOFTMAX_BATCH)
         inside = [place < valid[s] for s in several]
         scores = [jnp.where(i, score_of[s], -1e30) for i, s in zip(inside, several)]
         peaks = [jnp.max(x, axis=1, keepdims=True) for x in scores]

time: 94.6 us -> 94.6 us (level)
  no operation moved by 1% of the time
where the time goes in v11:
time: 94.6 us; the launch traced here: 94.3 us
  blocking collectives  81.5 us (86%)
  Pallas kernels  6.17 us (7%)
  starting transfers between devices  4.42 us (5%)
  waiting for transfers between devices  2.07 us (2%)
    all_to_all x5, blocking collectives, exchanged(): return lax.all_to_all(pieces, axis, 0, 0, tiled=True)  81.5 us
    ppermute x1, starting transfers between devices, on_device(): other = lax.ppermute(part, pair, [(0, 1), (1, 0)])  4.28 us
    pallas_call x1, Pallas kernels, on_device(): pl.pallas_call(functools.partial(attention_kernel, devices * ctx_rows), o...  2.73 us
  transfers between devices with their start and end apart: 2, of which 2 were waited for; matrix products, arithmetic and copies ran while one was open for 0% of the time, Pallas kernels for 0%

profile of v11, /device:TPU:513, one launch (start us, length us, event | category | flops | bytes accessed | tf_op | source)
XLA Modules:
  0.0 94.3 jit_solution(12586349173117119810)
XLA Ops:
  0.0 2.7 %attention.1 = bf16[8,208,128]{2,1,0:T(8,128)(2,1)S(1)} custom-call(s32[1]{0:T(128)} %bitcast.first, s32[16]{0:T(128)} %lengths_in.1, s32[8]{0:T(128)} %insert_slot_in.1, s32[8]{0:T(128)} %prefix_len_in.1, bf16[16,4096]{1,0:T(8,128)(2,1)} %queries_in.1, bf16[32,4096]{1,0:T(8,128)(2,1)} %bitcast.13, bf16[2,16,32,1024]{3,2,1,0:T(8,128)(2,1)} %cache.1, ...), custom_call_target="tpu_custom_call" | custom-call | tf_op jit(solution)/shard_map/attention/pallas_call | solution.py:408
  2.7 18.7 %all_to_all.25.pieces.landed = bf16[8,208,128]{2,1,0:T(8,128)(2,1)S(1)} all-to-all(bf16[8,208,128]{2,1,0:T(8,128)(2,1)S(1)} %attention.1), channel_id=1, replica_groups=mesh['rep'=2,'blk_0'=8,'blk_1'=8,'blk_2'=2] {'blk_0'}, dimensions={0} | all-to-all | bytes 851968 | tf_op jit(solution)/shard_map/all_to_all | solution.py:31
  21.5 0.3 spread_kernel.1
  21.7 0.0 copy-start.5
  21.7 24.1 %all_to_all.26.pieces = bf16[8,80,128]{2,1,0:T(8,128)(2,1)S(1)} all-to-all(bf16[8,80,128]{2,1,0:T(8,128)(2,1)S(1)} %spread_kernel.1), channel_id=1, replica_groups=mesh['rep'=2,'blk_0'=8,'blk_1'=8,'blk_2'=2] {'blk_1'}, dimensions={0} | all-to-all | bytes 327680 | tf_op jit(solution)/shard_map/all_to_all | solution.py:31
  45.9 0.3 part_kernel.1.mine
  46.1 4.3 %collective-permute-start = (bf16[80,128]{1,0:T(8,128)(2,1)S(1)}, bf16[80,128]{1,0:T(8,128)(2,1)S(1)}, u32[]{:S(2)}, u32[]{:S(2)}) collective-permute-start(bf16[80,128]{1,0:T(8,128)(2,1)S(1)} %part_kernel.1.mine), channel_id=1, source_target_pairs={{0,1},{1,0},{2,3},{3,2},{4,5},{5,4},{6,7},{7,6},{8,9},{9,8},{10,11... | collective-permute-start | bytes 61448 | tf_op jit(solution)/shard_map/ppermute | solution.py:443
  50.4 0.8 collective-permute-done.other
  51.2 0.0 copy-done.5
  51.2 0.0 copy-start
  51.3 0.3 project.1
  51.5 0.0 copy-start.1
  51.6 0.0 copy-start.2
  51.6 0.0 copy-start.3
  51.6 0.0 copy-start.4
  51.6 9.8 %all_to_all.27.pieces = bf16[8,16,256]{2,1,0:T(8,128)(2,1)S(1)} all-to-all(bf16[8,16,256]{2,1,0:T(8,128)(2,1)S(1)} %project.1), channel_id=1, replica_groups=mesh['rep'=2,'blk_0'=8,'blk_1'=8,'blk_2'=2] {'blk_0'}, dimensions={0} | all-to-all | bytes 131072 | tf_op jit(solution)/shard_map/all_to_all | solution.py:31
  61.4 0.1 mixed.1
  61.5 13.3 %all_to_all.28.gathered = bf16[16,16,256]{2,1,0:T(8,128)(2,1)S(1)} all-to-all(bf16[16,16,256]{2,1,0:T(8,128)(2,1)S(1)} %get-tuple-element.17), channel_id=1, replica_groups=mesh['rep'=2,'blk_0'=8,'blk_1'=8,'blk_2'=2] {'blk_1','blk_2'}, dimensions={0} | all-to-all | bytes 262144 | tf_op jit(solution)/shard_map/all_to_all | solution.py:31
  74.8 0.0 copy-done
  74.8 0.0 copy-done.1
  74.8 0.0 copy-done.2
  74.8 0.0 copy-done.3
  74.8 0.0 copy-done.4
  74.8 1.8 %experts.1 = (f32[32,8,128]{2,1,0:T(8,128)S(1)}, bf16[32,8,128]{2,1,0:T(8,128)(2,1)S(1)}) custom-call(s32[1]{0:T(128)} %bitcast.2.expert, s32[1]{0:T(128)} %bitcast.3.core, bf16[16,16,256]{2,1,0:T(8,128)(2,1)S(1)} %all_to_all.28.gathered, bf16[4096]{0:T(1024)(128)(2,1)S(1)} %copy-done.3, bf16[4,4096]{1,0:T(4,128)(2,1)S(1)} %bitcast.11, ...), custom_call_target="tpu_custom_call" | custom-call | tf_op jit(solution)/shard_map/experts/pallas_call | solution.py:468
  76.6 0.1 collective-permute-start.1
  76.7 1.2 %collective-permute-done.1.other = bf16[32,8,128]{2,1,0:T(8,128)(2,1)S(1)} collective-permute-done((bf16[32,8,128]{2,1,0:T(8,128)(2,1)S(1)}, bf16[32,8,128]{2,1,0:T(8,128)(2,1)S(1)}, u32[]{:S(2)}, u32[]{:S(2)}) %collective-permute-start.1) | collective-permute-done | bytes 65568 | tf_op jit(solution)/shard_map/ppermute | solution.py:488
  78.0 15.6 %all_to_all.29.pieces = bf16[64,4,128]{2,1,0:T(4,128)(2,1)S(1)} all-to-all(bf16[64,4,128]{2,1,0:T(4,128)(2,1)S(1)} %bitcast.10), channel_id=1, replica_groups=mesh['rep'=2,'blk_0'=8,'blk_1'=8,'blk_2'=2] {'blk_0','blk_1'}, dimensions={0} | all-to-all | bytes 131072 | tf_op jit(solution)/shard_map/all_to_all | solution.py:31
  93.5 0.7 final.1
  (1 shorter events, 0.0 us)
Async XLA Ops:
  21.7 29.5 %copy-start.5 = (bf16[16,32]{1,0:T(8,128)(2,1)S(1)}, bf16[16,32]{1,0:T(8,128)(2,1)}, u32[]{:S(2)}) copy-start(bf16[16,32]{1,0:T(8,128)(2,1)} %hidden.1) | copy-start | bytes 3076
  46.1 5.1 %collective-permute-start = (bf16[80,128]{1,0:T(8,128)(2,1)S(1)}, bf16[80,128]{1,0:T(8,128)(2,1)S(1)}, u32[]{:S(2)}, u32[]{:S(2)}) collective-permute-start(bf16[80,128]{1,0:T(8,128)(2,1)S(1)} %part_kernel.1.mine), channel_id=1, source_target_pairs={{0,1},{1,0},{2,3},{3,2},{4,5},{5,4},{6,7},{7,6},{8,9},{9,8},{10,11... | collective-permute-start | bytes 61448 | tf_op jit(solution)/shard_map/ppermute | solution.py:443
  51.2 23.5 %copy-start = (bf16[2,4096,224]{1,2,0:T(8,128)(2,1)S(1)}, bf16[2,4096,224]{1,2,0:T(8,128)(2,1)}, u32[]{:S(2)}) copy-start(bf16[2,4096,224]{1,2,0:T(8,128)(2,1)} %param.24) | copy-start | bytes 11010052
  51.5 23.2 %copy-start.1 = (bf16[224,4096]{1,0:T(8,128)(2,1)S(1)}, bf16[224,4096]{1,0:T(8,128)(2,1)}, u32[]{:S(2)}) copy-start(bf16[224,4096]{1,0:T(8,128)(2,1)} %down.1) | copy-start | bytes 5505028
  51.6 23.2 %copy-start.2 = (bf16[4096,4]{0,1:T(4,128)(2,1)S(1)}, bf16[4096,4]{0,1:T(4,128)(2,1)}, u32[]{:S(2)}) copy-start(bf16[4096,4]{0,1:T(4,128)(2,1)} %param.22) | copy-start | bytes 98308
  51.6 23.2 %copy-start.3 = (bf16[4096]{0:T(1024)(128)(2,1)S(1)}, bf16[4096]{0:T(1024)(128)(2,1)}, u32[]{:S(2)}) copy-start(bf16[4096]{0:T(1024)(128)(2,1)} %gain.1) | copy-start | bytes 24580
  51.6 23.2 %copy-start.4 = (s32[16,2]{0,1:T(2,128)S(1)}, s32[16,2]{0,1:T(2,128)}, u32[]{:S(2)}) copy-start(s32[16,2]{0,1:T(2,128)} %param.23) | copy-start | bytes 388
  76.6 1.4 %collective-permute-start.1 = (bf16[32,8,128]{2,1,0:T(8,128)(2,1)S(1)}, bf16[32,8,128]{2,1,0:T(8,128)(2,1)S(1)}, u32[]{:S(2)}, u32[]{:S(2)}) collective-permute-start(bf16[32,8,128]{2,1,0:T(8,128)(2,1)S(1)} %get-tuple-element.19), channel_id=1, source_target_pairs={{0,1},{1,0},{2,3},{3,2},{4,5},{5,4},{6,7},{7,6},{8,9},{9,8},{10,11... | collective-permute-start | bytes 196616 | tf_op jit(solution)/shard_map/ppermute | solution.py:488

commit v12 on v9

--- a/solution.py
+++ b/solution.py
@@ -21,7 +21,7 @@
 IN_VMEM = pl.BlockSpec(memory_space=pltpu.VMEM)
 IN_SMEM = pl.BlockSpec(memory_space=pltpu.SMEM)
 IN_HBM = pl.BlockSpec(memory_space=pltpu.HBM)
-BATCH = 4
+BATCH = 8
 MIB = 1 << 20
 COVER = pl.CostEstimate(flops=8*10**8, bytes_accessed=8 << 20, transcendentals=0)
 

time: 94.6 us -> 94.5 us (level)
  no operation moved by 1% of the time
where the time goes in v12:
time: 94.5 us; the launch traced here: 94.2 us
  blocking collectives  81.5 us (86%)
  Pallas kernels  6.13 us (6%)
  starting transfers between devices  4.42 us (5%)
  waiting for transfers between devices  2.07 us (2%)
    all_to_all x5, blocking collectives, exchanged(): return lax.all_to_all(pieces, axis, 0, 0, tiled=True)  81.5 us
    ppermute x1, starting transfers between devices, on_device(): other = lax.ppermute(part, pair, [(0, 1), (1, 0)])  4.28 us
    pallas_call x1, Pallas kernels, on_device(): pl.pallas_call(functools.partial(attention_kernel, devices * ctx_rows), o...  2.69 us
  transfers between devices with their start and end apart: 2, of which 2 were waited for; matrix products, arithmetic and copies ran while one was open for 0% of the time, Pallas kernels for 0%

profile of v12, /device:TPU:513, one launch (start us, length us, event | category | flops | bytes accessed | tf_op | source)
XLA Modules:
  0.0 94.2 jit_solution(14014420078353003365)
XLA Ops:
  0.0 2.7 %attention.1 = bf16[8,208,128]{2,1,0:T(8,128)(2,1)S(1)} custom-call(s32[1]{0:T(128)} %bitcast.first, s32[16]{0:T(128)} %lengths_in.1, s32[8]{0:T(128)} %insert_slot_in.1, s32[8]{0:T(128)} %prefix_len_in.1, bf16[16,4096]{1,0:T(8,128)(2,1)} %queries_in.1, bf16[32,4096]{1,0:T(8,128)(2,1)} %bitcast.13, bf16[2,16,32,1024]{3,2,1,0:T(8,128)(2,1)} %cache.1, ...), custom_call_target="tpu_custom_call" | custom-call | tf_op jit(solution)/shard_map/attention/pallas_call | solution.py:407
  2.7 18.7 %all_to_all.25.pieces.landed = bf16[8,208,128]{2,1,0:T(8,128)(2,1)S(1)} all-to-all(bf16[8,208,128]{2,1,0:T(8,128)(2,1)S(1)} %attention.1), channel_id=1, replica_groups=mesh['rep'=2,'blk_0'=8,'blk_1'=8,'blk_2'=2] {'blk_0'}, dimensions={0} | all-to-all | bytes 851968 | tf_op jit(solution)/shard_map/all_to_all | solution.py:30
  21.4 0.3 spread_kernel.1
  21.7 0.0 copy-start.5
  21.7 24.1 %all_to_all.26.pieces = bf16[8,80,128]{2,1,0:T(8,128)(2,1)S(1)} all-to-all(bf16[8,80,128]{2,1,0:T(8,128)(2,1)S(1)} %spread_kernel.1), channel_id=1, replica_groups=mesh['rep'=2,'blk_0'=8,'blk_1'=8,'blk_2'=2] {'blk_1'}, dimensions={0} | all-to-all | bytes 327680 | tf_op jit(solution)/shard_map/all_to_all | solution.py:30
  45.8 0.3 part_kernel.1.mine
  46.1 4.3 %collective-permute-start = (bf16[80,128]{1,0:T(8,128)(2,1)S(1)}, bf16[80,128]{1,0:T(8,128)(2,1)S(1)}, u32[]{:S(2)}, u32[]{:S(2)}) collective-permute-start(bf16[80,128]{1,0:T(8,128)(2,1)S(1)} %part_kernel.1.mine), channel_id=1, source_target_pairs={{0,1},{1,0},{2,3},{3,2},{4,5},{5,4},{6,7},{7,6},{8,9},{9,8},{10,11... | collective-permute-start | bytes 61448 | tf_op jit(solution)/shard_map/ppermute | solution.py:442
  50.4 0.8 collective-permute-done.other
  51.2 0.0 copy-done.5
  51.2 0.0 copy-start
  51.2 0.3 project.1
  51.5 0.0 copy-start.1
  51.5 0.0 copy-start.2
  51.5 0.0 copy-start.3
  51.5 0.0 copy-start.4
  51.6 9.8 %all_to_all.27.pieces = bf16[8,16,256]{2,1,0:T(8,128)(2,1)S(1)} all-to-all(bf16[8,16,256]{2,1,0:T(8,128)(2,1)S(1)} %project.1), channel_id=1, replica_groups=mesh['rep'=2,'blk_0'=8,'blk_1'=8,'blk_2'=2] {'blk_0'}, dimensions={0} | all-to-all | bytes 131072 | tf_op jit(solution)/shard_map/all_to_all | solution.py:30
  61.4 0.1 mixed.1
  61.5 13.3 %all_to_all.28.gathered = bf16[16,16,256]{2,1,0:T(8,128)(2,1)S(1)} all-to-all(bf16[16,16,256]{2,1,0:T(8,128)(2,1)S(1)} %get-tuple-element.17), channel_id=1, replica_groups=mesh['rep'=2,'blk_0'=8,'blk_1'=8,'blk_2'=2] {'blk_1','blk_2'}, dimensions={0} | all-to-all | bytes 262144 | tf_op jit(solution)/shard_map/all_to_all | solution.py:30
  74.7 0.0 copy-done
  74.7 0.0 copy-done.1
  74.7 0.0 copy-done.2
  74.7 0.0 copy-done.3
  74.8 0.0 copy-done.4
  74.8 1.8 %experts.1 = (f32[32,8,128]{2,1,0:T(8,128)S(1)}, bf16[32,8,128]{2,1,0:T(8,128)(2,1)S(1)}) custom-call(s32[1]{0:T(128)} %bitcast.2.expert, s32[1]{0:T(128)} %bitcast.3.core, bf16[16,16,256]{2,1,0:T(8,128)(2,1)S(1)} %all_to_all.28.gathered, bf16[4096]{0:T(1024)(128)(2,1)S(1)} %copy-done.3, bf16[4,4096]{1,0:T(4,128)(2,1)S(1)} %bitcast.11, ...), custom_call_target="tpu_custom_call" | custom-call | tf_op jit(solution)/shard_map/experts/pallas_call | solution.py:467
  76.5 0.1 collective-permute-start.1
  76.7 1.2 %collective-permute-done.1.other = bf16[32,8,128]{2,1,0:T(8,128)(2,1)S(1)} collective-permute-done((bf16[32,8,128]{2,1,0:T(8,128)(2,1)S(1)}, bf16[32,8,128]{2,1,0:T(8,128)(2,1)S(1)}, u32[]{:S(2)}, u32[]{:S(2)}) %collective-permute-start.1) | collective-permute-done | bytes 65568 | tf_op jit(solution)/shard_map/ppermute | solution.py:487
  77.9 15.6 %all_to_all.29.pieces = bf16[64,4,128]{2,1,0:T(4,128)(2,1)S(1)} all-to-all(bf16[64,4,128]{2,1,0:T(4,128)(2,1)S(1)} %bitcast.10), channel_id=1, replica_groups=mesh['rep'=2,'blk_0'=8,'blk_1'=8,'blk_2'=2] {'blk_0','blk_1'}, dimensions={0} | all-to-all | bytes 131072 | tf_op jit(solution)/shard_map/all_to_all | solution.py:30
  93.5 0.7 final.1
  (1 shorter events, 0.0 us)
Async XLA Ops:
  21.7 29.5 %copy-start.5 = (bf16[16,32]{1,0:T(8,128)(2,1)S(1)}, bf16[16,32]{1,0:T(8,128)(2,1)}, u32[]{:S(2)}) copy-start(bf16[16,32]{1,0:T(8,128)(2,1)} %hidden.1) | copy-start | bytes 3076
  46.1 5.1 %collective-permute-start = (bf16[80,128]{1,0:T(8,128)(2,1)S(1)}, bf16[80,128]{1,0:T(8,128)(2,1)S(1)}, u32[]{:S(2)}, u32[]{:S(2)}) collective-permute-start(bf16[80,128]{1,0:T(8,128)(2,1)S(1)} %part_kernel.1.mine), channel_id=1, source_target_pairs={{0,1},{1,0},{2,3},{3,2},{4,5},{5,4},{6,7},{7,6},{8,9},{9,8},{10,11... | collective-permute-start | bytes 61448 | tf_op jit(solution)/shard_map/ppermute | solution.py:442
  51.2 23.5 %copy-start = (bf16[2,4096,224]{1,2,0:T(8,128)(2,1)S(1)}, bf16[2,4096,224]{1,2,0:T(8,128)(2,1)}, u32[]{:S(2)}) copy-start(bf16[2,4096,224]{1,2,0:T(8,128)(2,1)} %param.24) | copy-start | bytes 11010052
  51.5 23.2 %copy-start.1 = (bf16[224,4096]{1,0:T(8,128)(2,1)S(1)}, bf16[224,4096]{1,0:T(8,128)(2,1)}, u32[]{:S(2)}) copy-start(bf16[224,4096]{1,0:T(8,128)(2,1)} %down.1) | copy-start | bytes 5505028
  51.5 23.2 %copy-start.2 = (bf16[4096,4]{0,1:T(4,128)(2,1)S(1)}, bf16[4096,4]{0,1:T(4,128)(2,1)}, u32[]{:S(2)}) copy-start(bf16[4096,4]{0,1:T(4,128)(2,1)} %param.22) | copy-start | bytes 98308
  51.5 23.2 %copy-start.3 = (bf16[4096]{0:T(1024)(128)(2,1)S(1)}, bf16[4096]{0:T(1024)(128)(2,1)}, u32[]{:S(2)}) copy-start(bf16[4096]{0:T(1024)(128)(2,1)} %gain.1) | copy-start | bytes 24580
  51.5 23.2 %copy-start.4 = (s32[16,2]{0,1:T(2,128)S(1)}, s32[16,2]{0,1:T(2,128)}, u32[]{:S(2)}) copy-start(s32[16,2]{0,1:T(2,128)} %param.23) | copy-start | bytes 388
  76.5 1.4 %collective-permute-start.1 = (bf16[32,8,128]{2,1,0:T(8,128)(2,1)S(1)}, bf16[32,8,128]{2,1,0:T(8,128)(2,1)S(1)}, u32[]{:S(2)}, u32[]{:S(2)}) collective-permute-start(bf16[32,8,128]{2,1,0:T(8,128)(2,1)S(1)} %get-tuple-element.19), channel_id=1, source_target_pairs={{0,1},{1,0},{2,3},{3,2},{4,5},{5,4},{6,7},{7,6},{8,9},{9,8},{10,11... | collective-permute-start | bytes 196616 | tf_op jit(solution)/shard_map/ppermute | solution.py:487
